TPU v7x, 32 devices: a whole 2x2x4 slice. The times are simulated.
32 devices in a mesh: dp: 8 (over z, y), tensor: 4 (over x, core).
Axes of the slice: x: 2, y: 2, z: 4, core: 2. Of those that a mesh axis runs over, the one named last changes fastest.
Arguments:
- block_input: bfloat16 [2, 1024, 8, 1024], P(None, 'tensor', 'dp'), may hold values from -6 to 6
- qkv_weight: bfloat16 [1024, 3, 1024], P('dp', None, 'tensor'), may hold values from -0.1875 to 0.1875
- qv_bias: float32 [2, 1024], P(None, 'tensor'), may hold values from -2 to 2
- out_weight: bfloat16 [1024, 1024], P('dp', 'tensor'), may hold values from -0.75 to 0.75
- out_bias: float32 [1024], replicated, may hold values from -2 to 2
- fc_weight: bfloat16 [1024, 4096], P('dp', 'tensor'), may hold values from -0.1875 to 0.1875
- fc_bias: float32 [4096], P('tensor'), may hold values from -2 to 2
- proj_weight: bfloat16 [1024, 4096], P('dp', 'tensor'), may hold values from -0.09375 to 0.09375
- proj_bias: float32 [1024], replicated, may hold values from -2 to 2
- norm1_gain: float32 [1024], replicated, may hold values from 0.1 to 1.9
- norm1_shift: float32 [1024], replicated, may hold values from -2 to 2
- norm2_gain: float32 [1024], replicated, may hold values from 0.1 to 1.9
- norm2_shift: float32 [1024], replicated, may hold values from -2 to 2
- out_grad: bfloat16 [2, 1024, 8, 1024], P(None, 'tensor', 'dp'), may hold values from -6 to 6
Outputs:
- block_output: bfloat16 [2, 1024, 8, 1024], P(None, 'tensor', 'dp')
- input_grad: bfloat16 [2, 1024, 8, 1024], P(None, 'tensor', 'dp')
- qkv_weight_grad: float32 [1024, 3, 1024], P('dp', None, 'tensor')
- qv_bias_grad: float32 [2, 1024], P(None, 'tensor')
- out_weight_grad: float32 [1024, 1024], P('dp', 'tensor')
- out_bias_grad: float32 [1024], replicated
- fc_weight_grad: float32 [1024, 4096], P('dp', 'tensor')
- fc_bias_grad: float32 [4096], P('tensor')
- proj_weight_grad: float32 [1024, 4096], P('dp', 'tensor')
- proj_bias_grad: float32 [1024], replicated
- norm1_gain_grad: float32 [1024], replicated
- norm1_shift_grad: float32 [1024], replicated
- norm2_gain_grad: float32 [1024], replicated
- norm2_shift_grad: float32 [1024], replicated
All inputs are finite; a program needn't handle non-finite values.
Results may differ from a plain program's by a relative error of at most 0.012.
Values may be sent and summed in bfloat16 or wider, within the bound.
A program may use at most 128 MiB of HBM per device.

v0:
```python
import jax
import jax.numpy as jnp
from jax import lax
from jax.sharding import PartitionSpec as P

HEAD_DIM = 64


norm_eps = 1e-05
tanh_coef = 0.7978845608028654
cube_coef = 0.044715
block_rows = 512


def gelu_tanh(values):
    return (
        0.5 * values * (1.0 + jnp.tanh(tanh_coef * (values + cube_coef * values * values * values)))
    )


def norm_parts(rows):
    center = rows - jnp.mean(rows, axis=-1, keepdims=True)
    spread = jnp.mean(center * center, axis=-1, keepdims=True)
    inverse = lax.rsqrt(spread + norm_eps)
    return (center * inverse, inverse)


def norm_back(grad_out, normed, inverse, gain):
    grad_normed = grad_out * gain
    first = jnp.mean(grad_normed, axis=-1, keepdims=True)
    second = jnp.mean(grad_normed * normed, axis=-1, keepdims=True)
    return inverse * (grad_normed - first - normed * second)


def causal_scores(query_block, keys, offset):
    scores = jnp.einsum(
        "qbhe,kbhe->bhqk", query_block, keys, preferred_element_type=jnp.float32
    ) * HEAD_DIM ** (-0.5)
    height = query_block.shape[0]
    length = keys.shape[0]
    row_pos = lax.broadcasted_iota(jnp.int32, (height, length), 0) + offset
    col_pos = lax.broadcasted_iota(jnp.int32, (height, length), 1)
    return jnp.where(col_pos <= row_pos, scores, -1e30)


def attend_forward(queries, keys, values):
    length = keys.shape[0]
    span = min(block_rows, length)
    outputs = []
    totals = []
    for offset in range(0, length, span):
        scores = causal_scores(queries[offset : offset + span], keys, offset)
        peak = jnp.max(scores, axis=-1, keepdims=True)
        raised = jnp.exp(scores - peak)
        total = jnp.sum(raised, axis=-1, keepdims=True)
        weights = (raised / total).astype(jnp.bfloat16)
        outputs.append(
            jnp.einsum("bhqk,kbhe->qbhe", weights, values, preferred_element_type=jnp.float32)
        )
        totals.append(peak + jnp.log(total))
    return (jnp.concatenate(outputs, 0), jnp.concatenate(totals, 2))


def attend_backward(queries, keys, values, log_totals, grad_out):
    length = keys.shape[0]
    span = min(block_rows, length)
    scale = HEAD_DIM ** (-0.5)
    grad_queries = []
    grad_keys = jnp.zeros(keys.shape, jnp.float32)
    grad_values = jnp.zeros(values.shape, jnp.float32)
    for offset in range(0, length, span):
        query_block = queries[offset : offset + span]
        grad_block = grad_out[offset : offset + span]
        scores = causal_scores(query_block, keys, offset)
        probs = jnp.exp(scores - log_totals[:, :, offset : offset + span])
        grad_probs = jnp.einsum(
            "qbhe,kbhe->bhqk", grad_block, values, preferred_element_type=jnp.float32
        )
        inner = jnp.sum(probs * grad_probs, axis=-1, keepdims=True)
        grad_scores = (probs * (grad_probs - inner)).astype(jnp.bfloat16)
        grad_queries.append(
            jnp.einsum("bhqk,kbhe->qbhe", grad_scores, keys, preferred_element_type=jnp.float32)
            * scale
        )
        grad_keys = (
            grad_keys
            + jnp.einsum(
                "bhqk,qbhe->kbhe", grad_scores, query_block, preferred_element_type=jnp.float32
            )
            * scale
        )
        grad_values = grad_values + jnp.einsum(
            "bhqk,qbhe->kbhe",
            probs.astype(jnp.bfloat16),
            grad_block,
            preferred_element_type=jnp.float32,
        )
    return (jnp.concatenate(grad_queries, 0), grad_keys, grad_values)


def per_device(
    block_input,
    qkv_weight,
    qv_bias,
    out_weight,
    out_bias,
    fc_weight,
    fc_bias,
    proj_weight,
    proj_bias,
    norm1_gain,
    norm1_shift,
    norm2_gain,
    norm2_shift,
    out_grad,
):
    micro = block_input.shape[0]
    heads_local = qkv_weight.shape[2] // HEAD_DIM
    weight_init = (
        jnp.zeros(qkv_weight.shape, jnp.float32),
        jnp.zeros(out_weight.shape, jnp.float32),
        jnp.zeros(fc_weight.shape, jnp.float32),
        jnp.zeros(proj_weight.shape, jnp.float32),
    )
    small_init = (
        jnp.zeros(qv_bias.shape, jnp.float32),
        jnp.zeros(fc_bias.shape, jnp.float32),
        jnp.zeros(out_bias.shape, jnp.float32),
        jnp.zeros(proj_bias.shape, jnp.float32),
        jnp.zeros(norm1_gain.shape, jnp.float32),
        jnp.zeros(norm1_shift.shape, jnp.float32),
        jnp.zeros(norm2_gain.shape, jnp.float32),
        jnp.zeros(norm2_shift.shape, jnp.float32),
    )
    outputs_init = jnp.zeros(block_input.shape, jnp.bfloat16)
    in_grads_init = jnp.zeros(block_input.shape, jnp.bfloat16)

    def one_micro(index, carry):
        outputs_all, in_grads_all, weight_acc, small_acc = carry
        resid_in = lax.dynamic_index_in_dim(block_input, index, 0, keepdims=False).astype(
            jnp.float32
        )
        grad_top = lax.dynamic_index_in_dim(out_grad, index, 0, keepdims=False)
        qkv_full, out_full, fc_full, proj_full = (
            lax.all_gather(qkv_weight, "dp", axis=0, tiled=True),
            lax.all_gather(out_weight, "dp", axis=0, tiled=True),
            lax.all_gather(fc_weight, "dp", axis=0, tiled=True),
            lax.all_gather(proj_weight, "dp", axis=0, tiled=True),
        )
        normed1, inverse1 = norm_parts(resid_in)
        hidden1 = (normed1 * norm1_gain + norm1_shift).astype(jnp.bfloat16)
        hidden1_full = lax.all_gather(hidden1, "tensor", axis=0, tiled=True)
        length = hidden1_full.shape[0]
        batch = hidden1_full.shape[1]
        projected = jnp.einsum(
            "lbd,dce->lbce", hidden1_full, qkv_full, preferred_element_type=jnp.float32
        )
        qkv_bias = jnp.stack([qv_bias[0], jnp.zeros_like(qv_bias[0]), qv_bias[1]])
        qkv_values = (projected + qkv_bias).astype(jnp.bfloat16)
        split = qkv_values.reshape(length, batch, 3, heads_local, HEAD_DIM)
        queries = split[:, :, 0]
        keys = split[:, :, 1]
        values = split[:, :, 2]
        attended, log_totals = attend_forward(queries, keys, values)
        mixed = attended.astype(jnp.bfloat16).reshape(length, batch, heads_local * HEAD_DIM)
        attn_branch = lax.psum_scatter(
            jnp.einsum("lbi,oi->lbo", mixed, out_full, preferred_element_type=jnp.float32),
            "tensor",
            scatter_dimension=0,
            tiled=True,
        )
        middle = resid_in + attn_branch + out_bias
        normed2, inverse2 = norm_parts(middle)
        hidden2 = (normed2 * norm2_gain + norm2_shift).astype(jnp.bfloat16)
        hidden2_full = lax.all_gather(hidden2, "tensor", axis=0, tiled=True)
        pre_act = (
            jnp.einsum("lbd,df->lbf", hidden2_full, fc_full, preferred_element_type=jnp.float32)
            + fc_bias
        )
        activated = gelu_tanh(pre_act).astype(jnp.bfloat16)
        mlp_branch = lax.psum_scatter(
            jnp.einsum(
                "lbf,of->lbo", activated, proj_full, preferred_element_type=jnp.float32
            ).astype(jnp.bfloat16),
            "tensor",
            scatter_dimension=0,
            tiled=True,
        ).astype(jnp.float32)
        block_out = (middle + mlp_branch + proj_bias).astype(jnp.bfloat16)
        grad_top_full = lax.all_gather(grad_top, "tensor", axis=0, tiled=True)
        grad_proj = jnp.einsum(
            "lbo,lbf->of", grad_top_full, activated, preferred_element_type=jnp.float32
        )
        grad_act = jnp.einsum(
            "lbo,of->lbf", grad_top_full, proj_full, preferred_element_type=jnp.float32
        )
        _, gelu_pull = jax.vjp(gelu_tanh, pre_act)
        grad_pre = gelu_pull(grad_act)[0].astype(jnp.bfloat16)
        grad_fc_bias = jnp.sum(grad_pre.astype(jnp.float32), axis=(0, 1))
        grad_fc = jnp.einsum(
            "lbd,lbf->df", hidden2_full, grad_pre, preferred_element_type=jnp.float32
        )
        grad_h2 = lax.psum_scatter(
            jnp.einsum("lbf,df->lbd", grad_pre, fc_full, preferred_element_type=jnp.float32),
            "tensor",
            scatter_dimension=0,
            tiled=True,
        )
        grad_gain2 = jnp.sum(grad_h2 * normed2, axis=(0, 1))
        grad_shift2 = jnp.sum(grad_h2, axis=(0, 1))
        grad_mid = grad_top.astype(jnp.float32) + norm_back(grad_h2, normed2, inverse2, norm2_gain)
        grad_out_bias = jnp.sum(grad_mid, axis=(0, 1))
        grad_proj_bias = jnp.sum(grad_top.astype(jnp.float32), axis=(0, 1))
        grad_mid_full = lax.all_gather(grad_mid.astype(jnp.bfloat16), "tensor", axis=0, tiled=True)
        grad_out_w = jnp.einsum(
            "lbo,lbi->oi", grad_mid_full, mixed, preferred_element_type=jnp.float32
        )
        grad_mixed = jnp.einsum(
            "lbo,oi->lbi", grad_mid_full, out_full, preferred_element_type=jnp.float32
        )
        grad_mixed = grad_mixed.astype(jnp.bfloat16).reshape(length, batch, heads_local, HEAD_DIM)
        grad_queries, grad_keys, grad_values = attend_backward(
            queries, keys, values, log_totals, grad_mixed
        )
        grad_qkv = jnp.stack([grad_queries, grad_keys, grad_values], axis=2).astype(jnp.bfloat16)
        grad_qkv = grad_qkv.reshape(length, batch, 3, heads_local * HEAD_DIM)
        kind_sums = jnp.sum(grad_qkv.astype(jnp.float32), axis=(0, 1))
        grad_qv_bias = jnp.stack([kind_sums[0], kind_sums[2]])
        grad_qkv_w = jnp.einsum(
            "lbd,lbce->dce", hidden1_full, grad_qkv, preferred_element_type=jnp.float32
        )
        grad_h1 = lax.psum_scatter(
            jnp.einsum("lbce,dce->lbd", grad_qkv, qkv_full, preferred_element_type=jnp.float32),
            "tensor",
            scatter_dimension=0,
            tiled=True,
        )
        grad_gain1 = jnp.sum(grad_h1 * normed1, axis=(0, 1))
        grad_shift1 = jnp.sum(grad_h1, axis=(0, 1))
        grad_in = (grad_mid + norm_back(grad_h1, normed1, inverse1, norm1_gain)).astype(
            jnp.bfloat16
        )
        shards = (
            lax.psum_scatter(grad_qkv_w, "dp", scatter_dimension=0, tiled=True),
            lax.psum_scatter(grad_out_w, "dp", scatter_dimension=0, tiled=True),
            lax.psum_scatter(grad_fc, "dp", scatter_dimension=0, tiled=True),
            lax.psum_scatter(grad_proj, "dp", scatter_dimension=0, tiled=True),
        )
        weight_acc = tuple((total + extra for total, extra in zip(weight_acc, shards)))
        fresh = (
            grad_qv_bias,
            grad_fc_bias,
            grad_out_bias,
            grad_proj_bias,
            grad_gain1,
            grad_shift1,
            grad_gain2,
            grad_shift2,
        )
        small_acc = tuple((total + extra for total, extra in zip(small_acc, fresh)))
        outputs_all = lax.dynamic_update_index_in_dim(outputs_all, block_out, index, 0)
        in_grads_all = lax.dynamic_update_index_in_dim(in_grads_all, grad_in, index, 0)
        return (outputs_all, in_grads_all, weight_acc, small_acc)

    outputs_all, in_grads_all, weight_acc, small_acc = lax.fori_loop(
        0, micro, one_micro, (outputs_init, in_grads_init, weight_init, small_init)
    )
    head_sums = lax.psum((small_acc[0], small_acc[1]), "dp")
    feature_sums = lax.psum(
        (small_acc[2], small_acc[3], small_acc[4], small_acc[5], small_acc[6], small_acc[7]),
        ("dp", "tensor"),
    )
    return (
        outputs_all,
        in_grads_all,
        weight_acc[0],
        head_sums[0],
        weight_acc[1],
        feature_sums[0],
        weight_acc[2],
        head_sums[1],
        weight_acc[3],
        feature_sums[1],
        feature_sums[2],
        feature_sums[3],
        feature_sums[4],
        feature_sums[5],
    )


def solution(mesh):
    in_specs = (
        P(None, "tensor", "dp", None),
        P("dp", None, "tensor"),
        P(None, "tensor"),
        P("dp", "tensor"),
        P(),
        P("dp", "tensor"),
        P("tensor"),
        P("dp", "tensor"),
        P(),
        P(),
        P(),
        P(),
        P(),
        P(None, "tensor", "dp", None),
    )
    out_specs = (
        P(None, "tensor", "dp", None),
        P(None, "tensor", "dp", None),
        P("dp", None, "tensor"),
        P(None, "tensor"),
        P("dp", "tensor"),
        P(),
        P("dp", "tensor"),
        P("tensor"),
        P("dp", "tensor"),
        P(),
        P(),
        P(),
        P(),
        P(),
    )
    return jax.shard_map(
        per_device, mesh=mesh, in_specs=in_specs, out_specs=out_specs, check_vma=False
    )
```

profile of v0, /device:TPU:0, one launch (start us, length us, event | category | flops | bytes accessed | tf_op | source)
XLA Modules:
  0.0 1655.9 jit_solution(16337013425723476530)
XLA Ops:
  9.0 1577.2 %while.40 = (s32[]{:T(128)}, bf16[2,256,1,1024]{3,1,2,0:T(8,128)(2,1)}, bf16[2,256,1,1024]{3,1,2,0:T(8,128)(2,1)}, f32[128,3,256]{2,0,1:T(8,128)}, f32[128,256]{...) while((s32[]{:T(128)}, ...), condition=%wide.region_31.32_spmd.clone, body=%wide.region_0.31_spmd.clone.sunk | while | flops 22706915328 | bytes 673419584 | solution.py:265
  15.6 34.3 %all_gather.70 = bf16[1024,256]{1,0:T(8,128)(2,1)S(1)} all-gather(bf16[128,256]{1,0:T(8,128)(2,1)} %get-tuple-element.1049), channel_id=1, replica_groups=mesh['dp'=8,'tensor'=4] {'dp'}, dimensions={0}, use_global_device_ids=true | all-gather | bytes 589824 | tf_op jit(solution)/shard_map/while/body/eval_jaxpr/all_gather | solution.py:146
  50.3 11.2 all-gather.12.cloned.1.call-done
  61.5 22.7 %all-gather.14.cloned.1.call-done = bf16[1024,1,1024]{2,0,1:T(8,128)(2,1)} async-done(((bf16[256,1,1024]{2,0,1:T(8,128)(2,1)}), bf16[1024,1,1024]{2,0,1:T(8,128)(2,1)}) %all-gather.14.cloned.1.call-update) | async-done | bytes 2097168 | tf_op jit(solution)/shard_map/while/body/eval_jaxpr/all_gather | solution.py:152
  105.9 44.1 %reduce-scatter.9.cloned.1.call-done = f32[256,1,1024]{2,0,1:T(8,128)} async-done(((f32[1024,1,1024]{2,0,1:T(8,128)}), f32[256,1,1024]{2,0,1:T(8,128)}) %reduce-scatter.9.cloned.1.call-update) | async-done | bytes 1048592 | tf_op jit(solution)/shard_map/while/body/eval_jaxpr/reduce_scatter | solution.py:166
  154.9 46.2 %all-gather.18.cloned.1.call-done = bf16[1024,1024]{1,0:T(8,128)(2,1)} async-done(((bf16[128,1024]{1,0:T(8,128)(2,1)}), bf16[1024,1024]{1,0:T(8,128)(2,1)}) %all-gather.18.cloned.1.call-update) | async-done | bytes 2097168 | tf_op jit(solution)/shard_map/while/body/eval_jaxpr/all_gather | solution.py:147
  201.2 22.5 %all-gather.20.cloned.1.call-done = bf16[1024,1,1024]{2,0,1:T(8,128)(2,1)} async-done(((bf16[256,1,1024]{2,0,1:T(8,128)(2,1)}), bf16[1024,1,1024]{2,0,1:T(8,128)(2,1)}) %all-gather.20.cloned.1.call-update) | async-done | bytes 2097168 | tf_op jit(solution)/shard_map/while/body/eval_jaxpr/all_gather | solution.py:175
  230.2 17.5 %all-gather.22.cloned.1.call-done = bf16[1,1024,1,1024]{3,1,2,0:T(8,128)(2,1)} async-done(((bf16[1,256,1,1024]{3,1,2,0:T(8,128)(2,1)}), bf16[1,1024,1,1024]{3,1,2,0:T(8,128)(2,1)}) %all-gather.22.cloned.1.call-update) | async-done | bytes 2097168 | tf_op jit(solution)/shard_map/while/body/eval_jaxpr/all_gather | solution.py:190
  247.7 51.2 %all-gather.16.cloned.1.call-done = bf16[1024,1024]{1,0:T(8,128)(2,1)} async-done(((bf16[128,1024]{1,0:T(8,128)(2,1)}), bf16[1024,1024]{1,0:T(8,128)(2,1)}) %all-gather.16.cloned.1.call-update) | async-done | bytes 2097168 | tf_op jit(solution)/shard_map/while/body/eval_jaxpr/all_gather | solution.py:148
  299.0 9.6 convert_reduce_fusion.10
  314.2 43.2 %reduce-scatter.13.cloned.1.call-done = f32[256,1,1024]{2,0,1:T(8,128)} async-done(((f32[1024,1,1024]{2,0,1:T(8,128)}), f32[256,1,1024]{2,0,1:T(8,128)}) %reduce-scatter.13.cloned.1.call-update) | async-done | bytes 1048592 | tf_op jit(solution)/shard_map/while/body/eval_jaxpr/reduce_scatter | solution.py:203
  466.2 45.2 %reduce-scatter.23.cloned.1.call-done = f32[128,1024]{1,0:T(8,128)} async-done(((f32[1024,1024]{1,0:T(8,128)}), f32[128,1024]{1,0:T(8,128)}) %reduce-scatter.23.cloned.1.call-update) | async-done | bytes 524304 | tf_op jit(solution)/shard_map/while/body/eval_jaxpr/reduce_scatter | solution.py:247
  513.3 89.5 %reduce-scatter.21.cloned.1.call-done = f32[128,1024]{1,0:T(8,128)} async-done(((f32[1024,1024]{1,0:T(8,128)}), f32[128,1024]{1,0:T(8,128)}) %reduce-scatter.21.cloned.1.call-update) | async-done | bytes 524304 | tf_op jit(solution)/shard_map/while/body/eval_jaxpr/reduce_scatter | solution.py:246
  607.0 63.1 %reduce-scatter.19.cloned.1.call-done = f32[128,256]{1,0:T(8,128)} async-done(((f32[1024,256]{1,0:T(8,128)}), f32[128,256]{1,0:T(8,128)}) %reduce-scatter.19.cloned.1.call-update) | async-done | bytes 131088 | tf_op jit(solution)/shard_map/while/body/eval_jaxpr/reduce_scatter | solution.py:245
  671.0 76.5 %reduce-scatter.17.cloned.1.call-done = f32[128,3,256]{2,0,1:T(8,128)} async-done(((f32[1024,3,256]{2,0,1:T(8,128)}), f32[128,3,256]{2,0,1:T(8,128)}) %reduce-scatter.17.cloned.1.call-update) | async-done | bytes 393232 | tf_op jit(solution)/shard_map/while/body/eval_jaxpr/reduce_scatter | solution.py:244
  748.7 45.0 %reduce-scatter.15.cloned.1.call-done = f32[256,1,1024]{2,0,1:T(8,128)} async-done(((f32[1024,1,1024]{2,0,1:T(8,128)}), f32[256,1,1024]{2,0,1:T(8,128)}) %reduce-scatter.15.cloned.1.call-update) | async-done | bytes 1048592 | tf_op jit(solution)/shard_map/while/body/eval_jaxpr/reduce_scatter | solution.py:232
  804.8 32.8 %all_gather.70 = bf16[1024,256]{1,0:T(8,128)(2,1)S(1)} all-gather(bf16[128,256]{1,0:T(8,128)(2,1)} %get-tuple-element.1049), channel_id=1, replica_groups=mesh['dp'=8,'tensor'=4] {'dp'}, dimensions={0}, use_global_device_ids=true | all-gather | bytes 589824 | tf_op jit(solution)/shard_map/while/body/eval_jaxpr/all_gather | solution.py:146
  837.9 11.6 all-gather.12.cloned.1.call-done
  849.5 20.9 %all-gather.14.cloned.1.call-done = bf16[1024,1,1024]{2,0,1:T(8,128)(2,1)} async-done(((bf16[256,1,1024]{2,0,1:T(8,128)(2,1)}), bf16[1024,1,1024]{2,0,1:T(8,128)(2,1)}) %all-gather.14.cloned.1.call-update) | async-done | bytes 2097168 | tf_op jit(solution)/shard_map/while/body/eval_jaxpr/all_gather | solution.py:152
  892.4 43.9 %reduce-scatter.9.cloned.1.call-done = f32[256,1,1024]{2,0,1:T(8,128)} async-done(((f32[1024,1,1024]{2,0,1:T(8,128)}), f32[256,1,1024]{2,0,1:T(8,128)}) %reduce-scatter.9.cloned.1.call-update) | async-done | bytes 1048592 | tf_op jit(solution)/shard_map/while/body/eval_jaxpr/reduce_scatter | solution.py:166
  941.0 46.5 %all-gather.18.cloned.1.call-done = bf16[1024,1024]{1,0:T(8,128)(2,1)} async-done(((bf16[128,1024]{1,0:T(8,128)(2,1)}), bf16[1024,1024]{1,0:T(8,128)(2,1)}) %all-gather.18.cloned.1.call-update) | async-done | bytes 2097168 | tf_op jit(solution)/shard_map/while/body/eval_jaxpr/all_gather | solution.py:147
  987.5 22.5 %all-gather.20.cloned.1.call-done = bf16[1024,1,1024]{2,0,1:T(8,128)(2,1)} async-done(((bf16[256,1,1024]{2,0,1:T(8,128)(2,1)}), bf16[1024,1,1024]{2,0,1:T(8,128)(2,1)}) %all-gather.20.cloned.1.call-update) | async-done | bytes 2097168 | tf_op jit(solution)/shard_map/while/body/eval_jaxpr/all_gather | solution.py:175
  1016.6 17.7 %all-gather.22.cloned.1.call-done = bf16[1,1024,1,1024]{3,1,2,0:T(8,128)(2,1)} async-done(((bf16[1,256,1,1024]{3,1,2,0:T(8,128)(2,1)}), bf16[1,1024,1,1024]{3,1,2,0:T(8,128)(2,1)}) %all-gather.22.cloned.1.call-update) | async-done | bytes 2097168 | tf_op jit(solution)/shard_map/while/body/eval_jaxpr/all_gather | solution.py:190
  1034.2 51.2 %all-gather.16.cloned.1.call-done = bf16[1024,1024]{1,0:T(8,128)(2,1)} async-done(((bf16[128,1024]{1,0:T(8,128)(2,1)}), bf16[1024,1024]{1,0:T(8,128)(2,1)}) %all-gather.16.cloned.1.call-update) | async-done | bytes 2097168 | tf_op jit(solution)/shard_map/while/body/eval_jaxpr/all_gather | solution.py:148
  1100.8 43.2 %reduce-scatter.13.cloned.1.call-done = f32[256,1,1024]{2,0,1:T(8,128)} async-done(((f32[1024,1,1024]{2,0,1:T(8,128)}), f32[256,1,1024]{2,0,1:T(8,128)}) %reduce-scatter.13.cloned.1.call-update) | async-done | bytes 1048592 | tf_op jit(solution)/shard_map/while/body/eval_jaxpr/reduce_scatter | solution.py:203
  1254.5 43.4 %reduce-scatter.23.cloned.1.call-done = f32[128,1024]{1,0:T(8,128)} async-done(((f32[1024,1024]{1,0:T(8,128)}), f32[128,1024]{1,0:T(8,128)}) %reduce-scatter.23.cloned.1.call-update) | async-done | bytes 524304 | tf_op jit(solution)/shard_map/while/body/eval_jaxpr/reduce_scatter | solution.py:247
  1300.0 89.4 %reduce-scatter.21.cloned.1.call-done = f32[128,1024]{1,0:T(8,128)} async-done(((f32[1024,1024]{1,0:T(8,128)}), f32[128,1024]{1,0:T(8,128)}) %reduce-scatter.21.cloned.1.call-update) | async-done | bytes 524304 | tf_op jit(solution)/shard_map/while/body/eval_jaxpr/reduce_scatter | solution.py:246
  1394.4 62.3 %reduce-scatter.19.cloned.1.call-done = f32[128,256]{1,0:T(8,128)} async-done(((f32[1024,256]{1,0:T(8,128)}), f32[128,256]{1,0:T(8,128)}) %reduce-scatter.19.cloned.1.call-update) | async-done | bytes 131088 | tf_op jit(solution)/shard_map/while/body/eval_jaxpr/reduce_scatter | solution.py:245
  1457.6 76.5 %reduce-scatter.17.cloned.1.call-done = f32[128,3,256]{2,0,1:T(8,128)} async-done(((f32[1024,3,256]{2,0,1:T(8,128)}), f32[128,3,256]{2,0,1:T(8,128)}) %reduce-scatter.17.cloned.1.call-update) | async-done | bytes 393232 | tf_op jit(solution)/shard_map/while/body/eval_jaxpr/reduce_scatter | solution.py:244
  1535.3 44.9 %reduce-scatter.15.cloned.1.call-done = f32[256,1,1024]{2,0,1:T(8,128)} async-done(((f32[1024,1,1024]{2,0,1:T(8,128)}), f32[256,1,1024]{2,0,1:T(8,128)}) %reduce-scatter.15.cloned.1.call-update) | async-done | bytes 1048592 | tf_op jit(solution)/shard_map/while/body/eval_jaxpr/reduce_scatter | solution.py:232
  1586.2 40.2 %all-reduce = (f32[1024]{0:T(1024)}, f32[1024]{0:T(1024)}, f32[1024]{0:T(1024)}, f32[1024]{0:T(1024)}, f32[1024]{0:T(1024)}, /*index=5*/f32[1024]{0:T(1024)}) all-reduce(f32[1024]{0:T(1024)} %get-tuple-element.486, f32[1024]{0:T(1024)} %get-tuple-element.490, ...), channel_id=1, replica_groups=mesh['dp'=8,'tensor'=4] {'dp','tensor'}, use_global_device_ids=true, to_apply=%region_33.34 | all-reduce | flops 6144 | bytes 49152 | tf_op jit(solution)/shard_map/psum | solution.py:269
  1626.4 22.5 %all-reduce.1 = (f32[2,256]{1,0:T(2,128)}, f32[1024]{0:T(1024)}) all-reduce(f32[2,256]{1,0:T(2,128)} %get-tuple-element.484, f32[1024]{0:T(1024)} %get-tuple-element.488), channel_id=1, replica_groups=mesh['dp'=8,'tensor'=4] {'dp'}, use_global_device_ids=true, to_apply=%region_32.33 | all-reduce | flops 1536 | bytes 12288 | tf_op jit(solution)/shard_map/psum | solution.py:268
  (378 shorter events, 346.8 us)
Async XLA Ops:
  9.0 52.5 %all-gather.12.cloned.1.call-start = ((), (), s32[]{:S(2)}) async-start(), calls=%async_computation.8 | async-start | bytes 1769472 | tf_op jit(solution)/shard_map/while/body/eval_jaxpr/all_gather | solution.py:145
  9.7 74.5 %all-gather.14.cloned.1.call-start = ((), (), s32[]{:S(2)}) async-start(), calls=%async_computation.9 | async-start | bytes 2621440 | tf_op jit(solution)/shard_map/while/body/eval_jaxpr/all_gather | solution.py:152
  14.5 135.5 %reduce-scatter.9.cloned.1.call-start = ((), (), s32[]{:S(2)}) async-start(), calls=%async_computation.10 | async-start | bytes 5242880 | tf_op jit(solution)/shard_map/while/body/eval_jaxpr/reduce_scatter | solution.py:166
  105.3 95.8 %all-gather.18.cloned.1.call-start = ((), (), s32[]{:S(2)}) async-start(), calls=%async_computation.12 | async-start | bytes 2359296 | tf_op jit(solution)/shard_map/while/body/eval_jaxpr/all_gather | solution.py:147
  105.9 117.8 %all-gather.20.cloned.1.call-start = ((), (), s32[]{:S(2)}) async-start(), calls=%async_computation.13 | async-start | bytes 2621440 | tf_op jit(solution)/shard_map/while/body/eval_jaxpr/all_gather | solution.py:175
  152.8 94.9 %all-gather.22.cloned.1.call-start = ((), (), s32[]{:S(2)}) async-start(), calls=%async_computation.15 | async-start | bytes 2621440 | tf_op jit(solution)/shard_map/while/body/eval_jaxpr/all_gather | solution.py:190
  153.8 145.1 %all-gather.16.cloned.1.call-start = ((), (), s32[]{:S(2)}) async-start(), calls=%async_computation.11 | async-start | bytes 2359296 | tf_op jit(solution)/shard_map/while/body/eval_jaxpr/all_gather | solution.py:148
  154.6 202.9 %reduce-scatter.13.cloned.1.call-start = ((), (), s32[]{:S(2)}) async-start(), calls=%async_computation.16 | async-start | bytes 5242880 | tf_op jit(solution)/shard_map/while/body/eval_jaxpr/reduce_scatter | solution.py:203
  314.2 71.6 %all-gather.24.cloned.1.call-start = ((), (), s32[]{:S(2)}) async-start(), calls=%async_computation.17 | async-start | bytes 2621440 | tf_op jit(solution)/shard_map/while/body/eval_jaxpr/all_gather | solution.py:214
  363.0 99.3 %reduce-scatter.11.cloned.1.call-start = ((), (), s32[]{:S(2)}) async-start(), calls=%async_computation.14 | async-start | bytes 2621440 | tf_op jit(solution)/shard_map/while/body/eval_jaxpr/reduce_scatter | solution.py:181
  370.1 141.3 %reduce-scatter.23.cloned.1.call-start = ((), (), s32[]{:S(2)}) async-start(), calls=%async_computation.22 | async-start | bytes 4718592 | tf_op jit(solution)/shard_map/while/body/eval_jaxpr/reduce_scatter | solution.py:247
  378.3 224.5 %reduce-scatter.21.cloned.1.call-start = ((), (), s32[]{:S(2)}) async-start(), calls=%async_computation.21 | async-start | bytes 4718592 | tf_op jit(solution)/shard_map/while/body/eval_jaxpr/reduce_scatter | solution.py:246
  385.0 285.1 %reduce-scatter.19.cloned.1.call-start = ((), (), s32[]{:S(2)}) async-start(), calls=%async_computation.20 | async-start | bytes 1179648 | tf_op jit(solution)/shard_map/while/body/eval_jaxpr/reduce_scatter | solution.py:245
  405.3 342.2 %reduce-scatter.17.cloned.1.call-start = ((), (), s32[]{:S(2)}) async-start(), calls=%async_computation.19 | async-start | bytes 3538944 | tf_op jit(solution)/shard_map/while/body/eval_jaxpr/reduce_scatter | solution.py:244
  454.4 339.2 %reduce-scatter.15.cloned.1.call-start = ((), (), s32[]{:S(2)}) async-start(), calls=%async_computation.18 | async-start | bytes 5242880 | tf_op jit(solution)/shard_map/while/body/eval_jaxpr/reduce_scatter | solution.py:232
  462.3 331.3 %copy-start.16 = (f32[1024]{0:T(1024)S(1)}, f32[1024]{0:T(1024)}, u32[]{:S(2)}) copy-start(f32[1024]{0:T(1024)} %get-tuple-element.1045) | copy-start | bytes 12292 | tf_op jit(solution)/shard_map/while
  464.3 331.1 %copy-start.23 = (f32[1024]{0:T(1024)S(1)}, f32[1024]{0:T(1024)}, u32[]{:S(2)}) copy-start(f32[1024]{0:T(1024)} %get-tuple-element.1007) | copy-start | bytes 12292 | tf_op jit(solution)/shard_map/while
  798.3 51.2 %all-gather.12.cloned.1.call-start = ((), (), s32[]{:S(2)}) async-start(), calls=%async_computation.8 | async-start | bytes 1769472 | tf_op jit(solution)/shard_map/while/body/eval_jaxpr/all_gather | solution.py:145
  798.9 71.6 %all-gather.14.cloned.1.call-start = ((), (), s32[]{:S(2)}) async-start(), calls=%async_computation.9 | async-start | bytes 2621440 | tf_op jit(solution)/shard_map/while/body/eval_jaxpr/all_gather | solution.py:152
  803.7 132.6 %reduce-scatter.9.cloned.1.call-start = ((), (), s32[]{:S(2)}) async-start(), calls=%async_computation.10 | async-start | bytes 5242880 | tf_op jit(solution)/shard_map/while/body/eval_jaxpr/reduce_scatter | solution.py:166
  891.6 96.0 %all-gather.18.cloned.1.call-start = ((), (), s32[]{:S(2)}) async-start(), calls=%async_computation.12 | async-start | bytes 2359296 | tf_op jit(solution)/shard_map/while/body/eval_jaxpr/all_gather | solution.py:147
  892.3 117.8 %all-gather.20.cloned.1.call-start = ((), (), s32[]{:S(2)}) async-start(), calls=%async_computation.13 | async-start | bytes 2621440 | tf_op jit(solution)/shard_map/while/body/eval_jaxpr/all_gather | solution.py:175
  939.1 95.2 %all-gather.22.cloned.1.call-start = ((), (), s32[]{:S(2)}) async-start(), calls=%async_computation.15 | async-start | bytes 2621440 | tf_op jit(solution)/shard_map/while/body/eval_jaxpr/all_gather | solution.py:190
  940.0 145.5 %all-gather.16.cloned.1.call-start = ((), (), s32[]{:S(2)}) async-start(), calls=%async_computation.11 | async-start | bytes 2359296 | tf_op jit(solution)/shard_map/while/body/eval_jaxpr/all_gather | solution.py:148
  940.8 203.2 %reduce-scatter.13.cloned.1.call-start = ((), (), s32[]{:S(2)}) async-start(), calls=%async_computation.16 | async-start | bytes 5242880 | tf_op jit(solution)/shard_map/while/body/eval_jaxpr/reduce_scatter | solution.py:203
  1100.7 71.6 %all-gather.24.cloned.1.call-start = ((), (), s32[]{:S(2)}) async-start(), calls=%async_computation.17 | async-start | bytes 2621440 | tf_op jit(solution)/shard_map/while/body/eval_jaxpr/all_gather | solution.py:214
  1149.6 100.2 %reduce-scatter.11.cloned.1.call-start = ((), (), s32[]{:S(2)}) async-start(), calls=%async_computation.14 | async-start | bytes 2621440 | tf_op jit(solution)/shard_map/while/body/eval_jaxpr/reduce_scatter | solution.py:181
  1156.7 141.3 %reduce-scatter.23.cloned.1.call-start = ((), (), s32[]{:S(2)}) async-start(), calls=%async_computation.22 | async-start | bytes 4718592 | tf_op jit(solution)/shard_map/while/body/eval_jaxpr/reduce_scatter | solution.py:247
  1164.7 224.7 %reduce-scatter.21.cloned.1.call-start = ((), (), s32[]{:S(2)}) async-start(), calls=%async_computation.21 | async-start | bytes 4718592 | tf_op jit(solution)/shard_map/while/body/eval_jaxpr/reduce_scatter | solution.py:246
  1171.3 285.3 %reduce-scatter.19.cloned.1.call-start = ((), (), s32[]{:S(2)}) async-start(), calls=%async_computation.20 | async-start | bytes 1179648 | tf_op jit(solution)/shard_map/while/body/eval_jaxpr/reduce_scatter | solution.py:245
  1191.8 342.4 %reduce-scatter.17.cloned.1.call-start = ((), (), s32[]{:S(2)}) async-start(), calls=%async_computation.19 | async-start | bytes 3538944 | tf_op jit(solution)/shard_map/while/body/eval_jaxpr/reduce_scatter | solution.py:244
  1241.0 339.2 %reduce-scatter.15.cloned.1.call-start = ((), (), s32[]{:S(2)}) async-start(), calls=%async_computation.18 | async-start | bytes 5242880 | tf_op jit(solution)/shard_map/while/body/eval_jaxpr/reduce_scatter | solution.py:232
  (72 other events, 4441.9 us)
Sparse Core Ops, SparseCore 0:
  11.8 49.6 all-gather.11
  63.1 21.1 all-gather.13
  105.4 44.5 reduce-scatter.8
  152.0 49.0 all-gather.17
  202.6 21.0 all-gather.19
  225.1 22.5 all-gather.21
  249.8 49.0 all-gather.15
  314.3 43.1 reduce-scatter.12
  363.2 22.5 all-gather.23
  388.1 31.1 reduce-scatter.10
  423.0 88.3 reduce-scatter.22
  514.9 87.8 reduce-scatter.20
  606.2 63.8 reduce-scatter.18
  673.5 73.9 reduce-scatter.16
  749.9 43.6 reduce-scatter.14
  800.9 48.6 all-gather.11
  850.9 19.4 all-gather.13
  891.7 44.5 reduce-scatter.8
  938.4 49.1 all-gather.17
  989.0 21.0 all-gather.19
  1011.6 22.5 all-gather.21
  1036.4 49.0 all-gather.15
  1100.9 43.1 reduce-scatter.12
  1149.7 22.5 all-gather.23
  1174.8 31.1 reduce-scatter.10
  1209.5 88.3 reduce-scatter.22
  1301.4 87.9 reduce-scatter.20
  1392.8 63.8 reduce-scatter.18
  1460.3 73.8 reduce-scatter.16
  1536.5 43.6 reduce-scatter.14
where the time goes:
time: 1660 us
  waiting for transfers between devices  1160 us (70%)
  matrix products  217 us (13%)
  blocking collectives  130 us (8%)
  other arithmetic  95.9 us (6%)
  local copies, waits for them, and re-layouts  33.9 us (2%)
    reduce_scatter x2, waiting for transfers between devices, one_micro(): lax.psum_scatter(grad_fc, 'dp', scatter_dimension=0, tiled=True)  179 us
    reduce_scatter x2, waiting for transfers between devices, one_micro(): lax.psum_scatter(grad_qkv_w, 'dp', scatter_dimension=0, tiled=True)  153 us
    reduce_scatter x2, waiting for transfers between devices, one_micro(): lax.psum_scatter(grad_out_w, 'dp', scatter_dimension=0, tiled=True)  125 us
    all_gather x2, waiting for transfers between devices, one_micro(): lax.all_gather(proj_weight, 'dp', axis=0, tiled=True)  102 us
    all_gather x2, waiting for transfers between devices, one_micro(): lax.all_gather(fc_weight, 'dp', axis=0, tiled=True)  92.7 us
    reduce_scatter x2, waiting for transfers between devices, one_micro(): lax.psum_scatter(jnp.einsum('lbce,dce->lbd', grad_qkv, qkv_full, preferre...  89.9 us
    reduce_scatter x2, waiting for transfers between devices, one_micro(): lax.psum_scatter(grad_proj, 'dp', scatter_dimension=0, tiled=True)  88.6 us
    reduce_scatter x2, waiting for transfers between devices, one_micro(): lax.psum_scatter(jnp.einsum('lbi,oi->lbo', mixed, out_full, preferred_ele...  88 us
  transfers between devices with their start and end apart: 30, of which 28 were waited for; matrix products, arithmetic and copies ran while one was open for 15% of the time, Pallas kernels for 0%

commit v1 on v0

--- a/solution.py
+++ b/solution.py
@@ -116,12 +116,22 @@
 ):
     micro = block_input.shape[0]
     heads_local = qkv_weight.shape[2] // HEAD_DIM
-    weight_init = (
-        jnp.zeros(qkv_weight.shape, jnp.float32),
-        jnp.zeros(out_weight.shape, jnp.float32),
-        jnp.zeros(fc_weight.shape, jnp.float32),
-        jnp.zeros(proj_weight.shape, jnp.float32),
-    )
+    rows = qkv_weight.shape[0]
+    width_qkv = qkv_weight.shape[1] * qkv_weight.shape[2]
+    width_out = out_weight.shape[1]
+    width_fc = fc_weight.shape[1]
+    cuts = (width_qkv, width_qkv + width_out, width_qkv + width_out + width_fc)
+    packed = jnp.concatenate(
+        [qkv_weight.reshape(rows, width_qkv), out_weight, fc_weight, proj_weight], axis=1
+    )
+    packed_full = lax.all_gather(packed, "dp", axis=0, tiled=True)
+    depth = packed_full.shape[0]
+    qkv_full = packed_full[:, : cuts[0]].reshape(depth, 3, qkv_weight.shape[2])
+    out_full = packed_full[:, cuts[0] : cuts[1]]
+    fc_full = packed_full[:, cuts[1] : cuts[2]]
+    proj_full = packed_full[:, cuts[2] :]
+    grad_top_all = lax.all_gather(out_grad, "tensor", axis=1, tiled=True)
+    weight_init = jnp.zeros(packed_full.shape, jnp.float32)
     small_init = (
         jnp.zeros(qv_bias.shape, jnp.float32),
         jnp.zeros(fc_bias.shape, jnp.float32),
@@ -141,12 +151,7 @@
             jnp.float32
         )
         grad_top = lax.dynamic_index_in_dim(out_grad, index, 0, keepdims=False)
-        qkv_full, out_full, fc_full, proj_full = (
-            lax.all_gather(qkv_weight, "dp", axis=0, tiled=True),
-            lax.all_gather(out_weight, "dp", axis=0, tiled=True),
-            lax.all_gather(fc_weight, "dp", axis=0, tiled=True),
-            lax.all_gather(proj_weight, "dp", axis=0, tiled=True),
-        )
+        grad_top_full = lax.dynamic_index_in_dim(grad_top_all, index, 0, keepdims=False)
         normed1, inverse1 = norm_parts(resid_in)
         hidden1 = (normed1 * norm1_gain + norm1_shift).astype(jnp.bfloat16)
         hidden1_full = lax.all_gather(hidden1, "tensor", axis=0, tiled=True)
@@ -187,7 +192,6 @@
             tiled=True,
         ).astype(jnp.float32)
         block_out = (middle + mlp_branch + proj_bias).astype(jnp.bfloat16)
-        grad_top_full = lax.all_gather(grad_top, "tensor", axis=0, tiled=True)
         grad_proj = jnp.einsum(
             "lbo,lbf->of", grad_top_full, activated, preferred_element_type=jnp.float32
         )
@@ -240,13 +244,10 @@
         grad_in = (grad_mid + norm_back(grad_h1, normed1, inverse1, norm1_gain)).astype(
             jnp.bfloat16
         )
-        shards = (
-            lax.psum_scatter(grad_qkv_w, "dp", scatter_dimension=0, tiled=True),
-            lax.psum_scatter(grad_out_w, "dp", scatter_dimension=0, tiled=True),
-            lax.psum_scatter(grad_fc, "dp", scatter_dimension=0, tiled=True),
-            lax.psum_scatter(grad_proj, "dp", scatter_dimension=0, tiled=True),
-        )
-        weight_acc = tuple((total + extra for total, extra in zip(weight_acc, shards)))
+        fresh_weights = jnp.concatenate(
+            [grad_qkv_w.reshape(depth, width_qkv), grad_out_w, grad_fc, grad_proj], axis=1
+        )
+        weight_acc = weight_acc + fresh_weights
         fresh = (
             grad_qv_bias,
             grad_fc_bias,
@@ -265,26 +266,40 @@
     outputs_all, in_grads_all, weight_acc, small_acc = lax.fori_loop(
         0, micro, one_micro, (outputs_init, in_grads_init, weight_init, small_init)
     )
-    head_sums = lax.psum((small_acc[0], small_acc[1]), "dp")
-    feature_sums = lax.psum(
-        (small_acc[2], small_acc[3], small_acc[4], small_acc[5], small_acc[6], small_acc[7]),
-        ("dp", "tensor"),
-    )
+    weight_shard = lax.psum_scatter(weight_acc, "dp", scatter_dimension=0, tiled=True)
+    grad_qkv_w = weight_shard[:, : cuts[0]].reshape(qkv_weight.shape)
+    grad_out_w = weight_shard[:, cuts[0] : cuts[1]]
+    grad_fc_w = weight_shard[:, cuts[1] : cuts[2]]
+    grad_proj_w = weight_shard[:, cuts[2] :]
+    tensor_size = lax.psum(1, "tensor")
+    slot = lax.axis_index("tensor")
+    head_vec = jnp.concatenate([small_acc[0].reshape(-1), small_acc[1]])
+    head_slots = jnp.zeros((tensor_size, head_vec.shape[0]), jnp.float32)
+    head_slots = lax.dynamic_update_index_in_dim(head_slots, head_vec, slot, 0)
+    feature_vec = jnp.concatenate([item for item in small_acc[2:]])
+    total = lax.psum(jnp.concatenate([feature_vec, head_slots.reshape(-1)]), ("dp", "tensor"))
+    features = total[: feature_vec.shape[0]].reshape(6, -1)
+    head_total = lax.dynamic_index_in_dim(
+        total[feature_vec.shape[0] :].reshape(tensor_size, -1), slot, 0, keepdims=False
+    )
+    qv_size = small_acc[0].size
+    grad_qv_bias = head_total[:qv_size].reshape(small_acc[0].shape)
+    grad_fc_bias = head_total[qv_size:]
     return (
         outputs_all,
         in_grads_all,
-        weight_acc[0],
-        head_sums[0],
-        weight_acc[1],
-        feature_sums[0],
-        weight_acc[2],
-        head_sums[1],
-        weight_acc[3],
-        feature_sums[1],
-        feature_sums[2],
-        feature_sums[3],
-        feature_sums[4],
-        feature_sums[5],
+        grad_qkv_w,
+        grad_qv_bias,
+        grad_out_w,
+        features[0],
+        grad_fc_w,
+        grad_fc_bias,
+        grad_proj_w,
+        features[1],
+        features[2],
+        features[3],
+        features[4],
+        features[5],
     )
 
 

time: 1660 us -> 1000 us (0.60)
  waiting for transfers between devices: 1160 us -> 608 us
  blocking collectives: 130 us -> 43.1 us
  matrix products: 217 us -> 180 us
  local copies, waits for them, and re-layouts: 33.9 us -> 62.5 us
    reduce_scatter x8 -> x1, waiting for transfers between devices: 546 us -> 168 us  [per_device(): lax.psum_scatter(weight_acc, 'dp', scatter_dimension=0, tiled=True)]
    all_gather x8 -> x2, waiting for transfers between devices: 253 us -> 121 us  [the longest x1 101 us: per_device(): packed_full = lax.all_gather(packed, 'dp', axis=0, tiled=True)]
    reduce_scatter x2, waiting for transfers between devices: 89.9 us -> 18.6 us  [one_micro(): lax.psum_scatter(jnp.einsum('lbce,dce->lbd', grad_qkv, qkv_full, preferre...]
    all_gather x2 -> x0, blocking collectives: 67.1 us -> none  [one_micro(): lax.all_gather(out_weight, 'dp', axis=0, tiled=True)]
    all_gather x2, waiting for transfers between devices: 1.61 us -> 30.5 us  [one_micro(): lax.all_gather(grad_mid.astype(jnp.bfloat16), 'tensor', axis=0, tiled=True)]
    psum x2 -> x1, blocking collectives: 62.7 us -> 43.1 us  [per_device(): lax.psum(jnp.concatenate([feature_vec, head_slots.reshape(-1)]), ('dp', '...]
  transfers between devices with their start and end apart: 30 -> 17, of which waited for: 28 -> 15; matrix products, arithmetic and copies ran while one was open for 15% -> 21% of each run, Pallas kernels for 0% -> 0%
where the time goes in v1:
time: 1000 us; the launch traced here: 999 us
  waiting for transfers between devices  608 us (61%)
  matrix products  180 us (18%)
  other arithmetic  85.3 us (9%)
  local copies, waits for them, and re-layouts  62.5 us (6%)
  blocking collectives  43.1 us (4%)
  between operations  14.7 us (1%)
    reduce_scatter x1, waiting for transfers between devices, per_device(): lax.psum_scatter(weight_acc, 'dp', scatter_dimension=0, tiled=True)  168 us
    all_gather x1, waiting for transfers between devices, per_device(): packed_full = lax.all_gather(packed, 'dp', axis=0, tiled=True)  101 us
    reduce_scatter x2, waiting for transfers between devices, one_micro(): lax.psum_scatter(jnp.einsum('lbi,oi->lbo', mixed, out_full, preferred_ele...  89.4 us
    reduce_scatter x2, waiting for transfers between devices, one_micro(): lax.psum_scatter(jnp.einsum('lbf,df->lbd', grad_pre, fc_full, preferred_e...  89.3 us
    all_gather x2, waiting for transfers between devices, one_micro(): hidden1_full = lax.all_gather(hidden1, 'tensor', axis=0, tiled=True)  46.1 us
    all_gather x2, waiting for transfers between devices, one_micro(): hidden2_full = lax.all_gather(hidden2, 'tensor', axis=0, tiled=True)  44.6 us
    psum x1, blocking collectives, per_device(): lax.psum(jnp.concatenate([feature_vec, head_slots.reshape(-1)]), ('dp', '...  43.1 us
    all_gather x2, waiting for transfers between devices, one_micro(): lax.all_gather(grad_mid.astype(jnp.bfloat16), 'tensor', axis=0, tiled=True)  30.5 us
  transfers between devices with their start and end apart: 17, of which 15 were waited for; matrix products, arithmetic and copies ran while one was open for 21% of the time, Pallas kernels for 0%

profile of v1, /device:TPU:0, one launch (start us, length us, event | category | flops | bytes accessed | tf_op | source)
XLA Modules:
  0.0 999.4 jit_solution(10423390227295797122)
XLA Ops:
  13.4 101.5 %all-gather.6.cloned.1.call-done = bf16[1024,3072]{0,1:T(8,128)(2,1)} async-done(((bf16[128,3072]{0,1:T(8,128)(2,1)}), bf16[1024,3072]{0,1:T(8,128)(2,1)}) %all-gather.6.cloned.1.call-update) | async-done | bytes 6291472 | tf_op jit(solution)/shard_map/all_gather | solution.py:127
  130.1 19.0 %all-gather.8.cloned.1.call-done = bf16[2,1024,1,1024]{3,1,2,0:T(8,128)(2,1)} async-done(((bf16[2,256,1,1024]{3,1,2,0:T(8,128)(2,1)}), bf16[2,1024,1,1024]{3,1,2,0:T(8,128)(2,1)}) %all-gather.8.cloned.1.call-update) | async-done | bytes 4194320 | tf_op jit(solution)/shard_map/all_gather | solution.py:133
  149.1 623.7 %while.34 = (s32[]{:T(128)}, bf16[2,256,1,1024]{3,1,2,0:T(8,128)(2,1)}, bf16[2,256,1,1024]{3,1,2,0:T(8,128)(2,1)}, f32[1024,3072]{0,1:T(8,128)}, f32[2,256]{1,0:...) while((s32[]{:T(128)}, ...), condition=%wide.region_27.28_spmd.clone, body=%wide.region_0.27_spmd.clone.sunk | while | flops 22718711808 | bytes 744419392 | solution.py:266
  151.7 23.2 %all-gather.10.cloned.1.call-done = bf16[1024,1,1024]{2,0,1:T(8,128)(2,1)} async-done(((bf16[256,1,1024]{2,0,1:T(8,128)(2,1)}), bf16[1024,1,1024]{2,0,1:T(8,128)(2,1)}) %all-gather.10.cloned.1.call-update) | async-done | bytes 2097168 | tf_op jit(solution)/shard_map/while/body/eval_jaxpr/all_gather | solution.py:157
  196.7 44.7 %reduce-scatter.8.cloned.1.call-done = f32[256,1,1024]{2,0,1:T(8,128)} async-done(((f32[1024,1,1024]{2,0,1:T(8,128)}), f32[256,1,1024]{2,0,1:T(8,128)}) %reduce-scatter.8.cloned.1.call-update) | async-done | bytes 1048592 | tf_op jit(solution)/shard_map/while/body/eval_jaxpr/reduce_scatter | solution.py:171
  244.5 22.4 %all-gather.12.cloned.1.call-done = bf16[1024,1,1024]{2,0,1:T(8,128)(2,1)} async-done(((bf16[256,1,1024]{2,0,1:T(8,128)(2,1)}), bf16[1024,1,1024]{2,0,1:T(8,128)(2,1)}) %all-gather.12.cloned.1.call-update) | async-done | bytes 2097168 | tf_op jit(solution)/shard_map/while/body/eval_jaxpr/all_gather | solution.py:180
  271.6 5.7 convert_reduce_fusion.9
  283.1 44.7 %reduce-scatter.12.cloned.1.call-done = f32[256,1,1024]{2,0,1:T(8,128)} async-done(((f32[1024,1,1024]{2,0,1:T(8,128)}), f32[256,1,1024]{2,0,1:T(8,128)}) %reduce-scatter.12.cloned.1.call-update) | async-done | bytes 1048592 | tf_op jit(solution)/shard_map/while/body/eval_jaxpr/reduce_scatter | solution.py:207
  332.3 7.0 convert_bitcast_fusion.4
  339.8 15.1 %all-gather.14.cloned.1.call-done = bf16[1024,1,1024]{2,0,1:T(8,128)(2,1)} async-done(((bf16[256,1,1024]{2,0,1:T(8,128)(2,1)}), bf16[1024,1,1024]{2,0,1:T(8,128)(2,1)}) %all-gather.14.cloned.1.call-update) | async-done | bytes 2097168 | tf_op jit(solution)/shard_map/while/body/eval_jaxpr/all_gather | solution.py:218
  362.4 7.6 multiply_reduce_fusion.13
  374.6 6.8 multiply_convert_fusion.11
  384.3 5.5 multiply_reduce_fusion.14
  405.1 5.7 convolution_bitcast_fusion.8
  411.9 6.7 fusion.227
  438.5 5.7 maximum_add_fusion.4
  444.2 11.6 %reduce-scatter.14.cloned.1.call-done = f32[256,1,1024]{2,0,1:T(8,128)} async-done(((f32[1024,1,1024]{2,0,1:T(8,128)}), f32[256,1,1024]{2,0,1:T(8,128)}) %reduce-scatter.14.cloned.1.call-update) | async-done | bytes 1048592 | tf_op jit(solution)/shard_map/while/body/eval_jaxpr/reduce_scatter | solution.py:236
  462.6 22.9 %all-gather.10.cloned.1.call-done = bf16[1024,1,1024]{2,0,1:T(8,128)(2,1)} async-done(((bf16[256,1,1024]{2,0,1:T(8,128)(2,1)}), bf16[1024,1,1024]{2,0,1:T(8,128)(2,1)}) %all-gather.10.cloned.1.call-update) | async-done | bytes 2097168 | tf_op jit(solution)/shard_map/while/body/eval_jaxpr/all_gather | solution.py:157
  507.3 44.7 %reduce-scatter.8.cloned.1.call-done = f32[256,1,1024]{2,0,1:T(8,128)} async-done(((f32[1024,1,1024]{2,0,1:T(8,128)}), f32[256,1,1024]{2,0,1:T(8,128)}) %reduce-scatter.8.cloned.1.call-update) | async-done | bytes 1048592 | tf_op jit(solution)/shard_map/while/body/eval_jaxpr/reduce_scatter | solution.py:171
  555.3 22.2 %all-gather.12.cloned.1.call-done = bf16[1024,1,1024]{2,0,1:T(8,128)(2,1)} async-done(((bf16[256,1,1024]{2,0,1:T(8,128)(2,1)}), bf16[1024,1,1024]{2,0,1:T(8,128)(2,1)}) %all-gather.12.cloned.1.call-update) | async-done | bytes 2097168 | tf_op jit(solution)/shard_map/while/body/eval_jaxpr/all_gather | solution.py:180
  582.2 5.7 convert_reduce_fusion.9
  593.7 44.7 %reduce-scatter.12.cloned.1.call-done = f32[256,1,1024]{2,0,1:T(8,128)} async-done(((f32[1024,1,1024]{2,0,1:T(8,128)}), f32[256,1,1024]{2,0,1:T(8,128)}) %reduce-scatter.12.cloned.1.call-update) | async-done | bytes 1048592 | tf_op jit(solution)/shard_map/while/body/eval_jaxpr/reduce_scatter | solution.py:207
  642.9 7.0 convert_bitcast_fusion.4
  650.1 15.4 %all-gather.14.cloned.1.call-done = bf16[1024,1,1024]{2,0,1:T(8,128)(2,1)} async-done(((bf16[256,1,1024]{2,0,1:T(8,128)(2,1)}), bf16[1024,1,1024]{2,0,1:T(8,128)(2,1)}) %all-gather.14.cloned.1.call-update) | async-done | bytes 2097168 | tf_op jit(solution)/shard_map/while/body/eval_jaxpr/all_gather | solution.py:218
  673.0 7.6 multiply_reduce_fusion.13
  685.1 6.8 multiply_convert_fusion.11
  715.7 5.7 convolution_bitcast_fusion.8
  722.5 6.7 fusion.227
  749.2 10.1 %maximum_add_fusion.4 = f32[1024,3072]{0,1:T(8,128)} fusion(f32[1024,1024]{0,1:T(8,128)S(1)} %copy-done.11, f32[1024,1024]{0,1:T(8,128)S(1)} %copy-done.10, f32[1024,256]{0,1:T(8,128)S(1)} %fusion.228, f32[1024,768]{0,1:T(8,128)S(1)} %fusion.230, f32[1024,3072]{0,1:T(8,128)} %get-tuple-element.947, pred[]{:T(512)S(6)} %compare.3), kind=kLoop, calls=%fused_computation.clone.1 | loop fusion | flops 15728640 | bytes 37748736 | tf_op jit(solution)/shard_map/while/body/eval_jaxpr/add | solution.py:250
  759.3 7.1 reduce-scatter.14.cloned.1.call-done
  773.7 43.1 %psum.7 = f32[12288]{0:T(1024)S(1)} all-reduce(f32[12288]{0:T(1024)S(1)} %constant_dynamic-update-slice_fusion), channel_id=1, replica_groups=mesh['dp'=8,'tensor'=4] {'dp','tensor'}, use_global_device_ids=true, to_apply=%region_29.30 | all-reduce | flops 12288 | bytes 98304 | tf_op jit(solution)/shard_map/psum | solution.py:280
  818.7 167.7 %reduce-scatter.6.cloned.1.call-done = f32[128,3072]{0,1:T(8,128)} async-done(((f32[1024,3072]{0,1:T(8,128)}), f32[128,3072]{0,1:T(8,128)}) %reduce-scatter.6.cloned.1.call-update) | async-done | bytes 1572880 | tf_op jit(solution)/shard_map/reduce_scatter | solution.py:269
  (354 shorter events, 230.4 us)
Async XLA Ops:
  7.2 107.7 %all-gather.6.cloned.1.call-start = ((), (), s32[]{:S(2)}) async-start(), calls=%async_computation.5 | async-start | bytes 7077888 | tf_op jit(solution)/shard_map/all_gather | solution.py:127
  12.5 136.6 %all-gather.8.cloned.1.call-start = ((), (), s32[]{:S(2)}) async-start(), calls=%async_computation.6 | async-start | bytes 5242880 | tf_op jit(solution)/shard_map/all_gather | solution.py:133
  122.7 26.3 %copy-start.5 = (bf16[2,256,1,1024]{3,1,2,0:T(8,128)(2,1)S(1)}, bf16[2,256,1,1024]{3,1,2,0:T(8,128)(2,1)}, u32[]{:S(2)}) copy-start(bf16[2,256,1,1024]{3,1,2,0:T(8,128)(2,1)} %param.16) | copy-start | bytes 3145732
  122.7 26.3 %copy-start.20 = (f32[1024]{0:T(1024)S(1)}, f32[1024]{0:T(1024)}, u32[]{:S(2)}) copy-start(f32[1024]{0:T(1024)} %param.25) | copy-start | bytes 12292
  122.7 26.3 %copy-start.21 = (f32[1024]{0:T(1024)S(1)}, f32[1024]{0:T(1024)}, u32[]{:S(2)}) copy-start(f32[1024]{0:T(1024)} %param.27) | copy-start | bytes 12292
  122.7 26.3 %copy-start.22 = (f32[1024]{0:T(1024)S(1)}, f32[1024]{0:T(1024)}, u32[]{:S(2)}) copy-start(f32[1024]{0:T(1024)} %param.26) | copy-start | bytes 12292
  122.8 26.3 %copy-start.23 = (f32[1024]{0:T(1024)S(1)}, f32[1024]{0:T(1024)}, u32[]{:S(2)}) copy-start(f32[1024]{0:T(1024)} %param.20) | copy-start | bytes 12292
  122.8 26.3 %copy-start.24 = (f32[1024]{0:T(1024)S(1)}, f32[1024]{0:T(1024)}, u32[]{:S(2)}) copy-start(f32[1024]{0:T(1024)} %param.28) | copy-start | bytes 12292
  122.8 26.3 %copy-start.25 = (f32[1024]{0:T(1024)S(1)}, f32[1024]{0:T(1024)}, u32[]{:S(2)}) copy-start(f32[1024]{0:T(1024)} %param.24) | copy-start | bytes 12292
  122.8 26.3 %copy-start.26 = (f32[2,256]{1,0:T(2,128)S(1)}, f32[2,256]{1,0:T(2,128)}, u32[]{:S(2)}) copy-start(f32[2,256]{1,0:T(2,128)} %param.18) | copy-start | bytes 6148
  122.8 26.3 %copy-start.30 = (f32[1024]{0:T(1024)S(1)}, f32[1024]{0:T(1024)}, u32[]{:S(2)}) copy-start(f32[1024]{0:T(1024)} %param.22) | copy-start | bytes 12292
  149.4 43.9 %copy-start.16 = (bf16[1024,256]{1,0:T(8,128)(2,1)}, bf16[1024,256]{1,0:T(8,128)(2,1)S(1)}, u32[]{:S(2)}) copy-start(bf16[1024,256]{1,0:T(8,128)(2,1)S(1)} %get-tuple-element.992) | copy-start | bytes 1572868 | tf_op jit(solution)/shard_map/while
  149.4 25.5 %all-gather.10.cloned.1.call-start = ((), (), s32[]{:S(2)}) async-start(), calls=%async_computation.8 | async-start | bytes 2621440 | tf_op jit(solution)/shard_map/while/body/eval_jaxpr/all_gather | solution.py:157
  151.0 90.4 %reduce-scatter.8.cloned.1.call-start = ((), (), s32[]{:S(2)}) async-start(), calls=%async_computation.9 | async-start | bytes 5242880 | tf_op jit(solution)/shard_map/while/body/eval_jaxpr/reduce_scatter | solution.py:171
  196.6 70.3 %all-gather.12.cloned.1.call-start = ((), (), s32[]{:S(2)}) async-start(), calls=%async_computation.10 | async-start | bytes 2621440 | tf_op jit(solution)/shard_map/while/body/eval_jaxpr/all_gather | solution.py:180
  244.1 83.6 %reduce-scatter.12.cloned.1.call-start = ((), (), s32[]{:S(2)}) async-start(), calls=%async_computation.12 | async-start | bytes 5242880 | tf_op jit(solution)/shard_map/while/body/eval_jaxpr/reduce_scatter | solution.py:207
  283.0 71.9 %all-gather.14.cloned.1.call-start = ((), (), s32[]{:S(2)}) async-start(), calls=%async_computation.13 | async-start | bytes 2621440 | tf_op jit(solution)/shard_map/while/body/eval_jaxpr/all_gather | solution.py:218
  332.2 91.3 %reduce-scatter.10.cloned.1.call-start = ((), (), s32[]{:S(2)}) async-start(), calls=%async_computation.11 | async-start | bytes 2621440 | tf_op jit(solution)/shard_map/while/body/eval_jaxpr/reduce_scatter | solution.py:186
  339.3 116.5 %reduce-scatter.14.cloned.1.call-start = ((), (), s32[]{:S(2)}) async-start(), calls=%async_computation.14 | async-start | bytes 5242880 | tf_op jit(solution)/shard_map/while/body/eval_jaxpr/reduce_scatter | solution.py:236
  357.4 12.7 %slice-start.2 = ((s8[8388608]{0:T(1024)(128)(4,1)}), s8[4194304]{0:T(1024)(128)(4,1)S(1)}, s32[]{:S(2)}) async-start(s8[8388608]{0:T(1024)(128)(4,1)} %bitcast.324), calls=%async_computation.17 | async-start | bytes 8388608 | tf_op jit(solution)/shard_map/while
  444.2 15.8 %copy-start.17 = (bf16[1024,256]{1,0:T(8,128)(2,1)S(1)}, bf16[1024,256]{1,0:T(8,128)(2,1)}, u32[]{:S(2)}) copy-start(bf16[1024,256]{1,0:T(8,128)(2,1)} %copy-done.16) | copy-start | bytes 1572868 | tf_op jit(solution)/shard_map/while
  460.3 43.6 %copy-start.16 = (bf16[1024,256]{1,0:T(8,128)(2,1)}, bf16[1024,256]{1,0:T(8,128)(2,1)S(1)}, u32[]{:S(2)}) copy-start(bf16[1024,256]{1,0:T(8,128)(2,1)S(1)} %get-tuple-element.992) | copy-start | bytes 1572868 | tf_op jit(solution)/shard_map/while
  460.3 25.2 %all-gather.10.cloned.1.call-start = ((), (), s32[]{:S(2)}) async-start(), calls=%async_computation.8 | async-start | bytes 2621440 | tf_op jit(solution)/shard_map/while/body/eval_jaxpr/all_gather | solution.py:157
  461.9 90.1 %reduce-scatter.8.cloned.1.call-start = ((), (), s32[]{:S(2)}) async-start(), calls=%async_computation.9 | async-start | bytes 5242880 | tf_op jit(solution)/shard_map/while/body/eval_jaxpr/reduce_scatter | solution.py:171
  507.2 70.3 %all-gather.12.cloned.1.call-start = ((), (), s32[]{:S(2)}) async-start(), calls=%async_computation.10 | async-start | bytes 2621440 | tf_op jit(solution)/shard_map/while/body/eval_jaxpr/all_gather | solution.py:180
  554.8 83.6 %reduce-scatter.12.cloned.1.call-start = ((), (), s32[]{:S(2)}) async-start(), calls=%async_computation.12 | async-start | bytes 5242880 | tf_op jit(solution)/shard_map/while/body/eval_jaxpr/reduce_scatter | solution.py:207
  593.6 71.9 %all-gather.14.cloned.1.call-start = ((), (), s32[]{:S(2)}) async-start(), calls=%async_computation.13 | async-start | bytes 2621440 | tf_op jit(solution)/shard_map/while/body/eval_jaxpr/all_gather | solution.py:218
  642.8 91.3 %reduce-scatter.10.cloned.1.call-start = ((), (), s32[]{:S(2)}) async-start(), calls=%async_computation.11 | async-start | bytes 2621440 | tf_op jit(solution)/shard_map/while/body/eval_jaxpr/reduce_scatter | solution.py:186
  649.9 116.5 %reduce-scatter.14.cloned.1.call-start = ((), (), s32[]{:S(2)}) async-start(), calls=%async_computation.14 | async-start | bytes 5242880 | tf_op jit(solution)/shard_map/while/body/eval_jaxpr/reduce_scatter | solution.py:236
  668.0 12.7 %slice-start.2 = ((s8[8388608]{0:T(1024)(128)(4,1)}), s8[4194304]{0:T(1024)(128)(4,1)S(1)}, s32[]{:S(2)}) async-start(s8[8388608]{0:T(1024)(128)(4,1)} %bitcast.324), calls=%async_computation.17 | async-start | bytes 8388608 | tf_op jit(solution)/shard_map/while
  759.3 11.3 %copy-start.17 = (bf16[1024,256]{1,0:T(8,128)(2,1)S(1)}, bf16[1024,256]{1,0:T(8,128)(2,1)}, u32[]{:S(2)}) copy-start(bf16[1024,256]{1,0:T(8,128)(2,1)} %copy-done.16) | copy-start | bytes 1572868 | tf_op jit(solution)/shard_map/while
  772.8 213.5 %reduce-scatter.6.cloned.1.call-start = ((), (), s32[]{:S(2)}) async-start(), calls=%async_computation.7 | async-start | bytes 14155776 | tf_op jit(solution)/shard_map/reduce_scatter | solution.py:269
  (54 other events, 267.1 us)
Sparse Core Ops, SparseCore 0:
  12.6 102.1 all-gather.5
  116.4 32.6 all-gather.7
  152.3 22.5 all-gather.9
  196.7 44.5 reduce-scatter.7
  244.3 22.5 all-gather.11
  283.1 44.5 reduce-scatter.11
  332.3 22.5 all-gather.13
  357.4 31.1 reduce-scatter.9
  410.9 44.8 reduce-scatter.13
  462.9 22.5 all-gather.9
  507.3 44.5 reduce-scatter.7
  554.9 22.5 all-gather.11
  593.7 44.5 reduce-scatter.11
  642.9 22.5 all-gather.13
  667.9 31.1 reduce-scatter.9
  721.5 44.8 reduce-scatter.13
  776.9 209.3 reduce-scatter.5

commit v2 on v1

--- a/solution.py
+++ b/solution.py
@@ -96,6 +96,36 @@
             preferred_element_type=jnp.float32,
         )
     return (jnp.concatenate(grad_queries, 0), grad_keys, grad_values)
+
+
+SWAP = [(0, 1), (1, 0)]
+
+
+def tensor_gather(block):
+    across = lax.axis_index("tx")
+    core = lax.axis_index("tc")
+    other = lax.ppermute(block, "tx", SWAP)
+    pair = jnp.where(across == 0, jnp.stack([block, other]), jnp.stack([other, block]))
+    pair_other = lax.ppermute(pair, "tc", SWAP)
+    full = jnp.where(
+        core == 0, jnp.stack([pair, pair_other], 1), jnp.stack([pair_other, pair], 1)
+    )
+    return full.reshape((4 * block.shape[0],) + block.shape[1:])
+
+
+def tensor_scatter(parts, send_dtype):
+    across = lax.axis_index("tx")
+    core = lax.axis_index("tc")
+    rows = parts.shape[0] // 4
+    grid = parts.reshape((2, 2, rows) + parts.shape[1:])
+    keep = lax.dynamic_index_in_dim(grid, core, 1, keepdims=False)
+    send = lax.dynamic_index_in_dim(grid, 1 - core, 1, keepdims=False)
+    got = lax.ppermute(send.astype(send_dtype), "tc", SWAP)
+    chip = keep + got.astype(jnp.float32)
+    keep2 = lax.dynamic_index_in_dim(chip, across, 0, keepdims=False)
+    send2 = lax.dynamic_index_in_dim(chip, 1 - across, 0, keepdims=False)
+    got2 = lax.ppermute(send2.astype(send_dtype), "tx", SWAP)
+    return keep2 + got2.astype(jnp.float32)
 
 
 def per_device(
@@ -130,7 +160,7 @@
     out_full = packed_full[:, cuts[0] : cuts[1]]
     fc_full = packed_full[:, cuts[1] : cuts[2]]
     proj_full = packed_full[:, cuts[2] :]
-    grad_top_all = lax.all_gather(out_grad, "tensor", axis=1, tiled=True)
+    grad_top_all = jnp.swapaxes(tensor_gather(jnp.swapaxes(out_grad, 0, 1)), 0, 1)
     weight_init = jnp.zeros(packed_full.shape, jnp.float32)
     small_init = (
         jnp.zeros(qv_bias.shape, jnp.float32),
@@ -154,7 +184,7 @@
         grad_top_full = lax.dynamic_index_in_dim(grad_top_all, index, 0, keepdims=False)
         normed1, inverse1 = norm_parts(resid_in)
         hidden1 = (normed1 * norm1_gain + norm1_shift).astype(jnp.bfloat16)
-        hidden1_full = lax.all_gather(hidden1, "tensor", axis=0, tiled=True)
+        hidden1_full = tensor_gather(hidden1)
         length = hidden1_full.shape[0]
         batch = hidden1_full.shape[1]
         projected = jnp.einsum(
@@ -168,29 +198,23 @@
         values = split[:, :, 2]
         attended, log_totals = attend_forward(queries, keys, values)
         mixed = attended.astype(jnp.bfloat16).reshape(length, batch, heads_local * HEAD_DIM)
-        attn_branch = lax.psum_scatter(
+        attn_branch = tensor_scatter(
             jnp.einsum("lbi,oi->lbo", mixed, out_full, preferred_element_type=jnp.float32),
-            "tensor",
-            scatter_dimension=0,
-            tiled=True,
+            jnp.float32,
         )
         middle = resid_in + attn_branch + out_bias
         normed2, inverse2 = norm_parts(middle)
         hidden2 = (normed2 * norm2_gain + norm2_shift).astype(jnp.bfloat16)
-        hidden2_full = lax.all_gather(hidden2, "tensor", axis=0, tiled=True)
+        hidden2_full = tensor_gather(hidden2)
         pre_act = (
             jnp.einsum("lbd,df->lbf", hidden2_full, fc_full, preferred_element_type=jnp.float32)
             + fc_bias
         )
         activated = gelu_tanh(pre_act).astype(jnp.bfloat16)
-        mlp_branch = lax.psum_scatter(
-            jnp.einsum(
-                "lbf,of->lbo", activated, proj_full, preferred_element_type=jnp.float32
-            ).astype(jnp.bfloat16),
-            "tensor",
-            scatter_dimension=0,
-            tiled=True,
-        ).astype(jnp.float32)
+        mlp_branch = tensor_scatter(
+            jnp.einsum("lbf,of->lbo", activated, proj_full, preferred_element_type=jnp.float32),
+            jnp.bfloat16,
+        )
         block_out = (middle + mlp_branch + proj_bias).astype(jnp.bfloat16)
         grad_proj = jnp.einsum(
             "lbo,lbf->of", grad_top_full, activated, preferred_element_type=jnp.float32
@@ -204,18 +228,16 @@
         grad_fc = jnp.einsum(
             "lbd,lbf->df", hidden2_full, grad_pre, preferred_element_type=jnp.float32
         )
-        grad_h2 = lax.psum_scatter(
+        grad_h2 = tensor_scatter(
             jnp.einsum("lbf,df->lbd", grad_pre, fc_full, preferred_element_type=jnp.float32),
-            "tensor",
-            scatter_dimension=0,
-            tiled=True,
+            jnp.float32,
         )
         grad_gain2 = jnp.sum(grad_h2 * normed2, axis=(0, 1))
         grad_shift2 = jnp.sum(grad_h2, axis=(0, 1))
         grad_mid = grad_top.astype(jnp.float32) + norm_back(grad_h2, normed2, inverse2, norm2_gain)
         grad_out_bias = jnp.sum(grad_mid, axis=(0, 1))
         grad_proj_bias = jnp.sum(grad_top.astype(jnp.float32), axis=(0, 1))
-        grad_mid_full = lax.all_gather(grad_mid.astype(jnp.bfloat16), "tensor", axis=0, tiled=True)
+        grad_mid_full = tensor_gather(grad_mid.astype(jnp.bfloat16))
         grad_out_w = jnp.einsum(
             "lbo,lbi->oi", grad_mid_full, mixed, preferred_element_type=jnp.float32
         )
@@ -233,11 +255,9 @@
         grad_qkv_w = jnp.einsum(
             "lbd,lbce->dce", hidden1_full, grad_qkv, preferred_element_type=jnp.float32
         )
-        grad_h1 = lax.psum_scatter(
+        grad_h1 = tensor_scatter(
             jnp.einsum("lbce,dce->lbd", grad_qkv, qkv_full, preferred_element_type=jnp.float32),
-            "tensor",
-            scatter_dimension=0,
-            tiled=True,
+            jnp.float32,
         )
         grad_gain1 = jnp.sum(grad_h1 * normed1, axis=(0, 1))
         grad_shift1 = jnp.sum(grad_h1, axis=(0, 1))
@@ -271,13 +291,13 @@
     grad_out_w = weight_shard[:, cuts[0] : cuts[1]]
     grad_fc_w = weight_shard[:, cuts[1] : cuts[2]]
     grad_proj_w = weight_shard[:, cuts[2] :]
-    tensor_size = lax.psum(1, "tensor")
-    slot = lax.axis_index("tensor")
+    tensor_size = 4
+    slot = lax.axis_index("tx") * 2 + lax.axis_index("tc")
     head_vec = jnp.concatenate([small_acc[0].reshape(-1), small_acc[1]])
     head_slots = jnp.zeros((tensor_size, head_vec.shape[0]), jnp.float32)
     head_slots = lax.dynamic_update_index_in_dim(head_slots, head_vec, slot, 0)
     feature_vec = jnp.concatenate([item for item in small_acc[2:]])
-    total = lax.psum(jnp.concatenate([feature_vec, head_slots.reshape(-1)]), ("dp", "tensor"))
+    total = lax.psum(jnp.concatenate([feature_vec, head_slots.reshape(-1)]), ("dp", "tx", "tc"))
     features = total[: feature_vec.shape[0]].reshape(6, -1)
     head_total = lax.dynamic_index_in_dim(
         total[feature_vec.shape[0] :].reshape(tensor_size, -1), slot, 0, keepdims=False
@@ -304,32 +324,35 @@
 
 
 def solution(mesh):
+    assert mesh.shape["tensor"] == 4
+    devices = mesh.devices.reshape(mesh.shape["dp"], 2, 2)
+    mesh = jax.sharding.Mesh(devices, ("dp", "tx", "tc"))
     in_specs = (
-        P(None, "tensor", "dp", None),
-        P("dp", None, "tensor"),
-        P(None, "tensor"),
-        P("dp", "tensor"),
-        P(),
-        P("dp", "tensor"),
-        P("tensor"),
-        P("dp", "tensor"),
-        P(),
-        P(),
-        P(),
-        P(),
-        P(),
-        P(None, "tensor", "dp", None),
+        P(None, ("tx", "tc"), "dp", None),
+        P("dp", None, ("tx", "tc")),
+        P(None, ("tx", "tc")),
+        P("dp", ("tx", "tc")),
+        P(),
+        P("dp", ("tx", "tc")),
+        P(("tx", "tc")),
+        P("dp", ("tx", "tc")),
+        P(),
+        P(),
+        P(),
+        P(),
+        P(),
+        P(None, ("tx", "tc"), "dp", None),
     )
     out_specs = (
-        P(None, "tensor", "dp", None),
-        P(None, "tensor", "dp", None),
-        P("dp", None, "tensor"),
-        P(None, "tensor"),
-        P("dp", "tensor"),
-        P(),
-        P("dp", "tensor"),
-        P("tensor"),
-        P("dp", "tensor"),
+        P(None, ("tx", "tc"), "dp", None),
+        P(None, ("tx", "tc"), "dp", None),
+        P("dp", None, ("tx", "tc")),
+        P(None, ("tx", "tc")),
+        P("dp", ("tx", "tc")),
+        P(),
+        P("dp", ("tx", "tc")),
+        P(("tx", "tc")),
+        P("dp", ("tx", "tc")),
         P(),
         P(),
         P(),

time: 1000 us -> 858 us (0.86)
  waiting for transfers between devices: 608 us -> 446 us
  matrix products: 180 us -> 129 us
  local copies, waits for them, and re-layouts: 62.5 us -> 112 us
  starting transfers between devices: 2.08 us -> 19.7 us
    ppermute x0 -> x30, waiting for transfers between devices: none -> 219 us  [the longest x8 115 us: tensor_scatter(): got2 = lax.ppermute(send2.astype(send_dtype), 'tx', SWAP)]
    reduce_scatter x8 -> x0, waiting for transfers between devices: 197 us -> none  [the longest x2 89.4 us: one_micro(): lax.psum_scatter(jnp.einsum('lbi,oi->lbo', mixed, out_full, preferred_ele...]
    all_gather x7 -> x0, waiting for transfers between devices: 140 us -> none  [the longest x2 46.1 us: one_micro(): hidden1_full = lax.all_gather(hidden1, 'tensor', axis=0, tiled=True)]
    all_gather x1, waiting for transfers between devices: 101 us -> 65.5 us  [per_device(): packed_full = lax.all_gather(packed, 'dp', axis=0, tiled=True)]
    while x116 -> x232, local copies, waits for them, and re-layouts: 16.9 us -> 38.2 us
    ppermute x0 -> x30, starting transfers between devices: none -> 19.7 us  [the longest x7 9.53 us: tensor_gather(): other = lax.ppermute(block, 'tx', SWAP)]
    another operation x6 -> x12, local copies, waits for them, and re-layouts: 12.3 us -> 25.9 us  [one_micro(): jnp.stack([grad_queries, grad_keys, grad_values], axis=2)]
    select_n x0 -> x21, other arithmetic: none -> 13.4 us  [the longest x7 9.03 us: tensor_gather(): jnp.where(core == 0, jnp.stack([pair, pair_other], 1), jnp.stack([pair_ot...]
  transfers between devices with their start and end apart: 17 -> 32, of which waited for: 15 -> 25; matrix products, arithmetic and copies ran while one was open for 21% -> 20% of each run, Pallas kernels for 0% -> 0%
where the time goes in v2:
time: 858 us; the launch traced here: 853 us
  waiting for transfers between devices  446 us (52%)
  matrix products  129 us (15%)
  local copies, waits for them, and re-layouts  112 us (13%)
  other arithmetic  81.9 us (10%)
  blocking collectives  43.7 us (5%)
  starting transfers between devices  19.7 us (2%)
  between operations  14.9 us (2%)
    reduce_scatter x1, waiting for transfers between devices, per_device(): lax.psum_scatter(weight_acc, 'dp', scatter_dimension=0, tiled=True)  162 us
    ppermute x8, waiting for transfers between devices, tensor_scatter(): got2 = lax.ppermute(send2.astype(send_dtype), 'tx', SWAP)  115 us
    ppermute x7, waiting for transfers between devices, tensor_gather(): other = lax.ppermute(block, 'tx', SWAP)  82.2 us
    all_gather x1, waiting for transfers between devices, per_device(): packed_full = lax.all_gather(packed, 'dp', axis=0, tiled=True)  65.5 us
    psum x1, blocking collectives, per_device(): lax.psum(jnp.concatenate([feature_vec, head_slots.reshape(-1)]), ('dp', '...  43.7 us
    while x232, local copies, waits for them, and re-layouts  38.2 us
    another operation x12, local copies, waits for them, and re-layouts, one_micro(): jnp.stack([grad_queries, grad_keys, grad_values], axis=2)  25.9 us
    unnamed x43, local copies, waits for them, and re-layouts  17.6 us
  transfers between devices with their start and end apart: 32, of which 25 were waited for; matrix products, arithmetic and copies ran while one was open for 20% of the time, Pallas kernels for 0%

profile of v2, /device:TPU:0, one launch (start us, length us, event | category | flops | bytes accessed | tf_op | source)
XLA Modules:
  0.0 853.0 jit_solution(11172533885046716041)
XLA Ops:
  15.7 23.2 %collective-permute-done.14 = bf16[256,2,1,1024]{3,0,1,2:T(8,128)(2,1)S(1)} collective-permute-done((bf16[256,2,1,1024]{3,0,1,2:T(8,128)(2,1)S(1)}, bf16[256,2,1,1024]{3,0,1,2:T(8,128)(2,1)S(1)}, u32[]{:S(2)}, u32[]{:S(2)}) %collective-permute-start.14) | collective-permute-done | bytes 1048608 | tf_op jit(solution)/shard_map/ppermute | solution.py:107
  45.0 4.5 maximum_select_fusion.7
  49.5 65.5 %all-gather.2.cloned.1.call-done = bf16[1024,3072]{0,1:T(8,128)(2,1)} async-done(((bf16[128,3072]{0,1:T(8,128)(2,1)}), bf16[1024,3072]{0,1:T(8,128)(2,1)}) %all-gather.2.cloned.1.call-update) | async-done | bytes 6291472 | tf_op jit(solution)/shard_map/all_gather | solution.py:157
  129.5 502.4 %while.37 = (s32[]{:T(128)}, bf16[2,256,1,1024]{3,1,2,0:T(8,128)(2,1)}, bf16[2,256,1,1024]{3,1,2,0:T(8,128)(2,1)}, f32[1024,3072]{0,1:T(8,128)}, f32[2,256]{1,0:...) while((s32[]{:T(128)}, ...), condition=%wide.region_23.24_spmd.clone, body=%wide.region_0.23_spmd.clone.sunk | while | flops 22742042624 | bytes 1015114624 | solution.py:286
  133.4 10.0 %collective-permute-done = bf16[256,1,1024]{2,0,1:T(8,128)(2,1)S(1)} collective-permute-done((bf16[256,1,1024]{2,0,1:T(8,128)(2,1)S(1)}, bf16[256,1,1024]{2,0,1:T(8,128)(2,1)S(1)}, u32[]{:S(2)}, u32[]{:S(2)}) %collective-permute-start) | collective-permute-done | bytes 524320 | tf_op jit(solution)/shard_map/while/body/eval_jaxpr/ppermute | solution.py:107
  180.9 23.6 %collective-permute-done.3 = f32[256,1,1024]{2,0,1:T(8,128)S(1)} collective-permute-done((f32[256,1,1024]{2,0,1:T(8,128)S(1)}, f32[256,1,1024]{2,0,1:T(8,128)S(1)}, u32[]{:S(2)}, u32[]{:S(2)}) %collective-permute-start.3) | collective-permute-done | bytes 1048608 | tf_op jit(solution)/shard_map/while/body/eval_jaxpr/ppermute | solution.py:127
  208.4 11.3 %collective-permute-done.4 = bf16[256,1,1024]{2,0,1:T(8,128)(2,1)S(1)} collective-permute-done((bf16[256,1,1024]{2,0,1:T(8,128)(2,1)S(1)}, bf16[256,1,1024]{2,0,1:T(8,128)(2,1)S(1)}, u32[]{:S(2)}, u32[]{:S(2)}) %collective-permute-start.4) | collective-permute-done | bytes 524320 | tf_op jit(solution)/shard_map/while/body/eval_jaxpr/ppermute | solution.py:107
  225.3 4.5 multiply_convert_fusion.6
  229.9 5.9 convert_reduce_fusion.9
  253.2 4.4 fusion.271
  257.6 15.3 %collective-permute-done.9 = f32[256,1,1024]{2,0,1:T(8,128)S(1)} collective-permute-done((f32[256,1,1024]{2,0,1:T(8,128)S(1)}, f32[256,1,1024]{2,0,1:T(8,128)S(1)}, u32[]{:S(2)}, u32[]{:S(2)}) %collective-permute-start.9) | collective-permute-done | bytes 1048608 | tf_op jit(solution)/shard_map/while/body/eval_jaxpr/ppermute | solution.py:127
  275.6 4.4 fusion.270
  280.2 7.0 collective-permute-done.10
  297.4 4.4 multiply_reduce_fusion.14
  316.7 6.8 multiply_convert_fusion.8
  354.3 4.3 maximum_add_fusion.4
  358.6 18.2 %collective-permute-done.13 = f32[256,1,1024]{2,0,1:T(8,128)} collective-permute-done((f32[256,1,1024]{2,0,1:T(8,128)}, f32[256,1,1024]{2,0,1:T(8,128)}, u32[]{:S(2)}, u32[]{:S(2)}) %collective-permute-start.13) | collective-permute-done | bytes 1048608 | tf_op jit(solution)/shard_map/while/body/eval_jaxpr/ppermute | solution.py:127
  382.9 11.3 %collective-permute-done = bf16[256,1,1024]{2,0,1:T(8,128)(2,1)S(1)} collective-permute-done((bf16[256,1,1024]{2,0,1:T(8,128)(2,1)S(1)}, bf16[256,1,1024]{2,0,1:T(8,128)(2,1)S(1)}, u32[]{:S(2)}, u32[]{:S(2)}) %collective-permute-start) | collective-permute-done | bytes 524320 | tf_op jit(solution)/shard_map/while/body/eval_jaxpr/ppermute | solution.py:107
  430.4 24.7 %collective-permute-done.3 = f32[256,1,1024]{2,0,1:T(8,128)S(1)} collective-permute-done((f32[256,1,1024]{2,0,1:T(8,128)S(1)}, f32[256,1,1024]{2,0,1:T(8,128)S(1)}, u32[]{:S(2)}, u32[]{:S(2)}) %collective-permute-start.3) | collective-permute-done | bytes 1048608 | tf_op jit(solution)/shard_map/while/body/eval_jaxpr/ppermute | solution.py:127
  458.0 12.4 %collective-permute-done.4 = bf16[256,1,1024]{2,0,1:T(8,128)(2,1)S(1)} collective-permute-done((bf16[256,1,1024]{2,0,1:T(8,128)(2,1)S(1)}, bf16[256,1,1024]{2,0,1:T(8,128)(2,1)S(1)}, u32[]{:S(2)}, u32[]{:S(2)}) %collective-permute-start.4) | collective-permute-done | bytes 524320 | tf_op jit(solution)/shard_map/while/body/eval_jaxpr/ppermute | solution.py:107
  475.9 4.5 multiply_convert_fusion.6
  480.4 6.2 convert_reduce_fusion.9
  503.9 4.4 fusion.271
  508.3 15.4 %collective-permute-done.9 = f32[256,1,1024]{2,0,1:T(8,128)S(1)} collective-permute-done((f32[256,1,1024]{2,0,1:T(8,128)S(1)}, f32[256,1,1024]{2,0,1:T(8,128)S(1)}, u32[]{:S(2)}, u32[]{:S(2)}) %collective-permute-start.9) | collective-permute-done | bytes 1048608 | tf_op jit(solution)/shard_map/while/body/eval_jaxpr/ppermute | solution.py:127
  526.5 4.4 fusion.270
  531.0 7.0 collective-permute-done.10
  547.2 4.4 multiply_reduce_fusion.14
  566.5 6.8 multiply_convert_fusion.8
  603.9 4.3 maximum_add_fusion.4
  608.2 18.2 %collective-permute-done.13 = f32[256,1,1024]{2,0,1:T(8,128)} collective-permute-done((f32[256,1,1024]{2,0,1:T(8,128)}, f32[256,1,1024]{2,0,1:T(8,128)}, u32[]{:S(2)}, u32[]{:S(2)}) %collective-permute-start.13) | collective-permute-done | bytes 1048608 | tf_op jit(solution)/shard_map/while/body/eval_jaxpr/ppermute | solution.py:127
  632.6 43.7 %psum.7 = f32[12288]{0:T(1024)S(1)} all-reduce(f32[12288]{0:T(1024)S(1)} %constant_dynamic-update-slice_fusion), channel_id=1, replica_groups=mesh['dp'=8,'tx'=2,'tc'=2] {'dp','tx','tc'}, use_global_device_ids=true, to_apply=%region_25.26 | all-reduce | flops 12288 | bytes 98304 | tf_op jit(solution)/shard_map/psum | solution.py:300
  678.2 161.6 %reduce-scatter.2.cloned.1.call-done = f32[128,3072]{0,1:T(8,128)} async-done(((f32[1024,3072]{0,1:T(8,128)}), f32[128,3072]{0,1:T(8,128)}) %reduce-scatter.2.cloned.1.call-update) | async-done | bytes 1572880 | tf_op jit(solution)/shard_map/reduce_scatter | solution.py:289
  (571 shorter events, 291.0 us)
Async XLA Ops:
  7.2 107.7 %all-gather.2.cloned.1.call-start = ((), (), s32[]{:S(2)}) async-start(), calls=%async_computation.1 | async-start | bytes 7077888 | tf_op jit(solution)/shard_map/all_gather | solution.py:157
  12.6 827.3 %reduce-scatter.2.cloned.1.call-start = ((), (), s32[]{:S(2)}) async-start(), calls=%async_computation.2 | async-start | bytes 14155776 | tf_op jit(solution)/shard_map/reduce_scatter | solution.py:289
  12.6 26.2 %collective-permute-start.14 = (bf16[256,2,1,1024]{3,0,1,2:T(8,128)(2,1)S(1)}, bf16[256,2,1,1024]{3,0,1,2:T(8,128)(2,1)S(1)}, u32[]{:S(2)}, u32[]{:S(2)}) collective-permute-start(bf16[256,2,1,1024]{3,0,1,2:T(8,128)(2,1)S(1)} %bitcast.562), channel_id=1, source_target_pairs={{0,2},{2,0},{1,3},{3,1},{4,6},{6,4},{5,7},{7,5},{8,10},{10,8},{9,1... | collective-permute-start | bytes 3145736 | tf_op jit(solution)/shard_map/ppermute | solution.py:107
  40.5 4.5 collective-permute-start.15
  130.5 13.0 %collective-permute-start = (bf16[256,1,1024]{2,0,1:T(8,128)(2,1)S(1)}, bf16[256,1,1024]{2,0,1:T(8,128)(2,1)S(1)}, u32[]{:S(2)}, u32[]{:S(2)}) collective-permute-start(bf16[256,1,1024]{2,0,1:T(8,128)(2,1)S(1)} %fusion.237), channel_id=1, source_target_pairs={{0,2},{2,0},{1,3},{3,1},{4,6},{6,4},{5,7},{7,5},{8,10},{10,8},{9,1... | collective-permute-start | bytes 1572872 | tf_op jit(solution)/shard_map/while/body/eval_jaxpr/ppermute | solution.py:107
  143.7 2.7 collective-permute-start.1
  171.5 4.4 collective-permute-start.2
  179.3 25.3 %collective-permute-start.3 = (f32[256,1,1024]{2,0,1:T(8,128)S(1)}, f32[256,1,1024]{2,0,1:T(8,128)S(1)}, u32[]{:S(2)}, u32[]{:S(2)}) collective-permute-start(f32[256,1,1024]{2,0,1:T(8,128)S(1)} %dynamic-slice_bitcast_fusion.13), channel_id=1, source_target_pairs={{0,2},{2,0},{1,3},{3,1},{4,6},{6,4},{5,7},{7,5},{8,10},{10,8},{9,1... | collective-permute-start | bytes 3145736 | tf_op jit(solution)/shard_map/while/body/eval_jaxpr/ppermute | solution.py:127
  206.6 13.2 %collective-permute-start.4 = (bf16[256,1,1024]{2,0,1:T(8,128)(2,1)S(1)}, bf16[256,1,1024]{2,0,1:T(8,128)(2,1)S(1)}, u32[]{:S(2)}, u32[]{:S(2)}) collective-permute-start(bf16[256,1,1024]{2,0,1:T(8,128)(2,1)S(1)} %add_convert_fusion.5), channel_id=1, source_target_pairs={{0,2},{2,0},{1,3},{3,1},{4,6},{6,4},{5,7},{7,5},{8,10},{10,8},{9,1... | collective-permute-start | bytes 1572872 | tf_op jit(solution)/shard_map/while/body/eval_jaxpr/ppermute | solution.py:107
  219.9 2.7 collective-permute-start.5
  240.8 4.5 collective-permute-start.8
  247.6 25.3 %collective-permute-start.9 = (f32[256,1,1024]{2,0,1:T(8,128)S(1)}, f32[256,1,1024]{2,0,1:T(8,128)S(1)}, u32[]{:S(2)}, u32[]{:S(2)}) collective-permute-start(f32[256,1,1024]{2,0,1:T(8,128)S(1)} %dynamic-slice_bitcast_fusion.15), channel_id=1, source_target_pairs={{0,2},{2,0},{1,3},{3,1},{4,6},{6,4},{5,7},{7,5},{8,10},{10,8},{9,1... | collective-permute-start | bytes 3145736 | tf_op jit(solution)/shard_map/while/body/eval_jaxpr/ppermute | solution.py:127
  251.7 35.7 %collective-permute-start.6 = (bf16[2,256,1,1024]{3,1,0,2:T(8,128)(2,1)S(1)}, bf16[2,256,1,1024]{3,1,0,2:T(8,128)(2,1)S(1)}, u32[]{:S(2)}, u32[]{:S(2)}) collective-permute-start(bf16[2,256,1,1024]{3,1,0,2:T(8,128)(2,1)S(1)} %fusion.256), channel_id=1, source_target_pairs={{0,1},{1,0},{2,3},{3,2},{4,5},{5,4},{6,7},{7,6},{8,9},{9,8},{10,11... | collective-permute-start | bytes 3145736 | tf_op jit(solution)/shard_map/while/body/eval_jaxpr/ppermute | solution.py:123
  274.0 13.2 %collective-permute-start.10 = (bf16[256,1,1024]{2,0,1:T(8,128)(2,1)S(1)}, bf16[256,1,1024]{2,0,1:T(8,128)(2,1)S(1)}, u32[]{:S(2)}, u32[]{:S(2)}) collective-permute-start(bf16[256,1,1024]{2,0,1:T(8,128)(2,1)S(1)} %convert_element_type.658), channel_id=1, source_target_pairs={{0,2},{2,0},{1,3},{3,1},{4,6},{6,4},{5,7},{7,5},{8,10},{10,8},{9,1... | collective-permute-start | bytes 1572872 | tf_op jit(solution)/shard_map/while/body/eval_jaxpr/ppermute | solution.py:107
  287.3 3.5 collective-permute-start.11
  288.8 53.6 %collective-permute-start.7 = (bf16[256,1,1024]{2,0,1:T(8,128)(2,1)}, bf16[256,1,1024]{2,0,1:T(8,128)(2,1)}, u32[]{:S(2)}, u32[]{:S(2)}) collective-permute-start(bf16[256,1,1024]{2,0,1:T(8,128)(2,1)} %fusion.257), channel_id=1, source_target_pairs={{0,2},{2,0},{1,3},{3,1},{4,6},{6,4},{5,7},{7,5},{8,10},{10,8},{9,1... | collective-permute-start | bytes 1572872 | tf_op jit(solution)/shard_map/while/body/eval_jaxpr/ppermute | solution.py:127
  342.1 7.7 collective-permute-start.12
  351.3 25.6 %collective-permute-start.13 = (f32[256,1,1024]{2,0,1:T(8,128)}, f32[256,1,1024]{2,0,1:T(8,128)}, u32[]{:S(2)}, u32[]{:S(2)}) collective-permute-start(f32[256,1,1024]{2,0,1:T(8,128)} %dynamic-slice_bitcast_fusion.17), channel_id=1, source_target_pairs={{0,2},{2,0},{1,3},{3,1},{4,6},{6,4},{5,7},{7,5},{8,10},{10,8},{9,1... | collective-permute-start | bytes 3145736 | tf_op jit(solution)/shard_map/while/body/eval_jaxpr/ppermute | solution.py:127
  381.0 13.2 %collective-permute-start = (bf16[256,1,1024]{2,0,1:T(8,128)(2,1)S(1)}, bf16[256,1,1024]{2,0,1:T(8,128)(2,1)S(1)}, u32[]{:S(2)}, u32[]{:S(2)}) collective-permute-start(bf16[256,1,1024]{2,0,1:T(8,128)(2,1)S(1)} %fusion.237), channel_id=1, source_target_pairs={{0,2},{2,0},{1,3},{3,1},{4,6},{6,4},{5,7},{7,5},{8,10},{10,8},{9,1... | collective-permute-start | bytes 1572872 | tf_op jit(solution)/shard_map/while/body/eval_jaxpr/ppermute | solution.py:107
  394.4 2.7 collective-permute-start.1
  422.1 4.4 collective-permute-start.2
  429.9 25.3 %collective-permute-start.3 = (f32[256,1,1024]{2,0,1:T(8,128)S(1)}, f32[256,1,1024]{2,0,1:T(8,128)S(1)}, u32[]{:S(2)}, u32[]{:S(2)}) collective-permute-start(f32[256,1,1024]{2,0,1:T(8,128)S(1)} %dynamic-slice_bitcast_fusion.13), channel_id=1, source_target_pairs={{0,2},{2,0},{1,3},{3,1},{4,6},{6,4},{5,7},{7,5},{8,10},{10,8},{9,1... | collective-permute-start | bytes 3145736 | tf_op jit(solution)/shard_map/while/body/eval_jaxpr/ppermute | solution.py:127
  457.1 13.2 %collective-permute-start.4 = (bf16[256,1,1024]{2,0,1:T(8,128)(2,1)S(1)}, bf16[256,1,1024]{2,0,1:T(8,128)(2,1)S(1)}, u32[]{:S(2)}, u32[]{:S(2)}) collective-permute-start(bf16[256,1,1024]{2,0,1:T(8,128)(2,1)S(1)} %add_convert_fusion.5), channel_id=1, source_target_pairs={{0,2},{2,0},{1,3},{3,1},{4,6},{6,4},{5,7},{7,5},{8,10},{10,8},{9,1... | collective-permute-start | bytes 1572872 | tf_op jit(solution)/shard_map/while/body/eval_jaxpr/ppermute | solution.py:107
  470.5 2.7 collective-permute-start.5
  491.6 4.5 collective-permute-start.8
  498.4 25.3 %collective-permute-start.9 = (f32[256,1,1024]{2,0,1:T(8,128)S(1)}, f32[256,1,1024]{2,0,1:T(8,128)S(1)}, u32[]{:S(2)}, u32[]{:S(2)}) collective-permute-start(f32[256,1,1024]{2,0,1:T(8,128)S(1)} %dynamic-slice_bitcast_fusion.15), channel_id=1, source_target_pairs={{0,2},{2,0},{1,3},{3,1},{4,6},{6,4},{5,7},{7,5},{8,10},{10,8},{9,1... | collective-permute-start | bytes 3145736 | tf_op jit(solution)/shard_map/while/body/eval_jaxpr/ppermute | solution.py:127
  502.4 35.8 %collective-permute-start.6 = (bf16[2,256,1,1024]{3,1,0,2:T(8,128)(2,1)S(1)}, bf16[2,256,1,1024]{3,1,0,2:T(8,128)(2,1)S(1)}, u32[]{:S(2)}, u32[]{:S(2)}) collective-permute-start(bf16[2,256,1,1024]{3,1,0,2:T(8,128)(2,1)S(1)} %fusion.256), channel_id=1, source_target_pairs={{0,1},{1,0},{2,3},{3,2},{4,5},{5,4},{6,7},{7,6},{8,9},{9,8},{10,11... | collective-permute-start | bytes 3145736 | tf_op jit(solution)/shard_map/while/body/eval_jaxpr/ppermute | solution.py:123
  524.8 13.2 %collective-permute-start.10 = (bf16[256,1,1024]{2,0,1:T(8,128)(2,1)S(1)}, bf16[256,1,1024]{2,0,1:T(8,128)(2,1)S(1)}, u32[]{:S(2)}, u32[]{:S(2)}) collective-permute-start(bf16[256,1,1024]{2,0,1:T(8,128)(2,1)S(1)} %convert_element_type.658), channel_id=1, source_target_pairs={{0,2},{2,0},{1,3},{3,1},{4,6},{6,4},{5,7},{7,5},{8,10},{10,8},{9,1... | collective-permute-start | bytes 1572872 | tf_op jit(solution)/shard_map/while/body/eval_jaxpr/ppermute | solution.py:107
  538.1 2.7 collective-permute-start.11
  539.6 52.3 %collective-permute-start.7 = (bf16[256,1,1024]{2,0,1:T(8,128)(2,1)}, bf16[256,1,1024]{2,0,1:T(8,128)(2,1)}, u32[]{:S(2)}, u32[]{:S(2)}) collective-permute-start(bf16[256,1,1024]{2,0,1:T(8,128)(2,1)} %fusion.257), channel_id=1, source_target_pairs={{0,2},{2,0},{1,3},{3,1},{4,6},{6,4},{5,7},{7,5},{8,10},{10,8},{9,1... | collective-permute-start | bytes 1572872 | tf_op jit(solution)/shard_map/while/body/eval_jaxpr/ppermute | solution.py:127
  591.7 7.7 collective-permute-start.12
  600.8 25.6 %collective-permute-start.13 = (f32[256,1,1024]{2,0,1:T(8,128)}, f32[256,1,1024]{2,0,1:T(8,128)}, u32[]{:S(2)}, u32[]{:S(2)}) collective-permute-start(f32[256,1,1024]{2,0,1:T(8,128)} %dynamic-slice_bitcast_fusion.17), channel_id=1, source_target_pairs={{0,2},{2,0},{1,3},{3,1},{4,6},{6,4},{5,7},{7,5},{8,10},{10,8},{9,1... | collective-permute-start | bytes 3145736 | tf_op jit(solution)/shard_map/while/body/eval_jaxpr/ppermute | solution.py:127
  (130 other events, 643.0 us)
Sparse Core Ops, SparseCore 0:
  12.7 102.1 all-gather.1
  632.1 207.7 reduce-scatter.1

commit v3 on v2

v3 whole, which is shorter than its diff:
```python
import jax
import jax.numpy as jnp
from jax import lax
from jax.sharding import PartitionSpec as P

HEAD_DIM = 64


norm_eps = 1e-05
tanh_coef = 0.7978845608028654
cube_coef = 0.044715
block_rows = 512


def gelu_tanh(values):
    return (
        0.5 * values * (1.0 + jnp.tanh(tanh_coef * (values + cube_coef * values * values * values)))
    )


def norm_parts(rows):
    center = rows - jnp.mean(rows, axis=-1, keepdims=True)
    spread = jnp.mean(center * center, axis=-1, keepdims=True)
    inverse = lax.rsqrt(spread + norm_eps)
    return (center * inverse, inverse)


def norm_back(grad_out, normed, inverse, gain):
    grad_normed = grad_out * gain
    first = jnp.mean(grad_normed, axis=-1, keepdims=True)
    second = jnp.mean(grad_normed * normed, axis=-1, keepdims=True)
    return inverse * (grad_normed - first - normed * second)


def causal_scores(query_block, keys, offset):
    scores = jnp.einsum(
        "qbhe,kbhe->bhqk", query_block, keys, preferred_element_type=jnp.float32
    ) * HEAD_DIM ** (-0.5)
    height = query_block.shape[0]
    length = keys.shape[0]
    row_pos = lax.broadcasted_iota(jnp.int32, (height, length), 0) + offset
    col_pos = lax.broadcasted_iota(jnp.int32, (height, length), 1)
    return jnp.where(col_pos <= row_pos, scores, -1e30)


def attend_forward(queries, keys, values):
    length = keys.shape[0]
    span = min(block_rows, length)
    outputs = []
    totals = []
    for offset in range(0, length, span):
        scores = causal_scores(queries[offset : offset + span], keys, offset)
        peak = jnp.max(scores, axis=-1, keepdims=True)
        raised = jnp.exp(scores - peak)
        total = jnp.sum(raised, axis=-1, keepdims=True)
        weights = (raised / total).astype(jnp.bfloat16)
        outputs.append(
            jnp.einsum("bhqk,kbhe->qbhe", weights, values, preferred_element_type=jnp.float32)
        )
        totals.append(peak + jnp.log(total))
    return (jnp.concatenate(outputs, 0), jnp.concatenate(totals, 2))


def attend_backward(queries, keys, values, log_totals, grad_out):
    length = keys.shape[0]
    span = min(block_rows, length)
    scale = HEAD_DIM ** (-0.5)
    grad_queries = []
    grad_keys = jnp.zeros(keys.shape, jnp.float32)
    grad_values = jnp.zeros(values.shape, jnp.float32)
    for offset in range(0, length, span):
        query_block = queries[offset : offset + span]
        grad_block = grad_out[offset : offset + span]
        scores = causal_scores(query_block, keys, offset)
        probs = jnp.exp(scores - log_totals[:, :, offset : offset + span])
        grad_probs = jnp.einsum(
            "qbhe,kbhe->bhqk", grad_block, values, preferred_element_type=jnp.float32
        )
        inner = jnp.sum(probs * grad_probs, axis=-1, keepdims=True)
        grad_scores = (probs * (grad_probs - inner)).astype(jnp.bfloat16)
        grad_queries.append(
            jnp.einsum("bhqk,kbhe->qbhe", grad_scores, keys, preferred_element_type=jnp.float32)
            * scale
        )
        grad_keys = (
            grad_keys
            + jnp.einsum(
                "bhqk,qbhe->kbhe", grad_scores, query_block, preferred_element_type=jnp.float32
            )
            * scale
        )
        grad_values = grad_values + jnp.einsum(
            "bhqk,qbhe->kbhe",
            probs.astype(jnp.bfloat16),
            grad_block,
            preferred_element_type=jnp.float32,
        )
    return (jnp.concatenate(grad_queries, 0), grad_keys, grad_values)


SWAP = [(0, 1), (1, 0)]


def tensor_gather(block):
    across = lax.axis_index("tx")
    core = lax.axis_index("tc")
    other = lax.ppermute(block, "tx", SWAP)
    pair = jnp.where(across == 0, jnp.stack([block, other]), jnp.stack([other, block]))
    pair_other = lax.ppermute(pair, "tc", SWAP)
    full = jnp.where(
        core == 0, jnp.stack([pair, pair_other], 1), jnp.stack([pair_other, pair], 1)
    )
    return full.reshape((4 * block.shape[0],) + block.shape[1:])


def tensor_scatter(parts, send_dtype):
    across = lax.axis_index("tx")
    core = lax.axis_index("tc")
    rows = parts.shape[0] // 4
    grid = parts.reshape((2, 2, rows) + parts.shape[1:])
    keep = lax.dynamic_index_in_dim(grid, core, 1, keepdims=False)
    send = lax.dynamic_index_in_dim(grid, 1 - core, 1, keepdims=False)
    got = lax.ppermute(send.astype(send_dtype), "tc", SWAP)
    chip = keep + got.astype(jnp.float32)
    keep2 = lax.dynamic_index_in_dim(chip, across, 0, keepdims=False)
    send2 = lax.dynamic_index_in_dim(chip, 1 - across, 0, keepdims=False)
    got2 = lax.ppermute(send2.astype(send_dtype), "tx", SWAP)
    return keep2 + got2.astype(jnp.float32)


def tensor_sum(vector):
    vector = vector + lax.ppermute(vector, "tc", SWAP)
    return vector + lax.ppermute(vector, "tx", SWAP)


def one_micro(resid_in, grad_top, grad_top_full, weights, params):
    qkv_full, out_full, fc_full, proj_full = weights
    qv_bias, out_bias, fc_bias, proj_bias, norm1_gain, norm1_shift, norm2_gain, norm2_shift = params
    heads_local = qkv_full.shape[2] // HEAD_DIM
    normed1, inverse1 = norm_parts(resid_in)
    hidden1 = (normed1 * norm1_gain + norm1_shift).astype(jnp.bfloat16)
    hidden1_full = tensor_gather(hidden1)
    length = hidden1_full.shape[0]
    batch = hidden1_full.shape[1]
    projected = jnp.einsum(
        "lbd,dce->lbce", hidden1_full, qkv_full, preferred_element_type=jnp.float32
    )
    qkv_bias = jnp.stack([qv_bias[0], jnp.zeros_like(qv_bias[0]), qv_bias[1]])
    qkv_values = (projected + qkv_bias).astype(jnp.bfloat16)
    split = qkv_values.reshape(length, batch, 3, heads_local, HEAD_DIM)
    queries = split[:, :, 0]
    keys = split[:, :, 1]
    values = split[:, :, 2]
    attended, log_totals = attend_forward(queries, keys, values)
    mixed = attended.astype(jnp.bfloat16).reshape(length, batch, heads_local * HEAD_DIM)
    attn_branch = tensor_scatter(
        jnp.einsum("lbi,oi->lbo", mixed, out_full, preferred_element_type=jnp.float32),
        jnp.float32,
    )
    middle = resid_in + attn_branch + out_bias
    normed2, inverse2 = norm_parts(middle)
    hidden2 = (normed2 * norm2_gain + norm2_shift).astype(jnp.bfloat16)
    hidden2_full = tensor_gather(hidden2)
    pre_act = (
        jnp.einsum("lbd,df->lbf", hidden2_full, fc_full, preferred_element_type=jnp.float32)
        + fc_bias
    )
    activated = gelu_tanh(pre_act).astype(jnp.bfloat16)
    mlp_branch = tensor_scatter(
        jnp.einsum("lbf,of->lbo", activated, proj_full, preferred_element_type=jnp.float32),
        jnp.bfloat16,
    )
    block_out = (middle + mlp_branch + proj_bias).astype(jnp.bfloat16)
    grad_proj = jnp.einsum(
        "lbo,lbf->of", grad_top_full, activated, preferred_element_type=jnp.float32
    )
    grad_act = jnp.einsum(
        "lbo,of->lbf", grad_top_full, proj_full, preferred_element_type=jnp.float32
    )
    _, gelu_pull = jax.vjp(gelu_tanh, pre_act)
    grad_pre = gelu_pull(grad_act)[0].astype(jnp.bfloat16)
    grad_fc_bias = jnp.sum(grad_pre.astype(jnp.float32), axis=(0, 1))
    grad_fc = jnp.einsum(
        "lbd,lbf->df", hidden2_full, grad_pre, preferred_element_type=jnp.float32
    )
    grad_h2 = tensor_scatter(
        jnp.einsum("lbf,df->lbd", grad_pre, fc_full, preferred_element_type=jnp.float32),
        jnp.float32,
    )
    grad_gain2 = jnp.sum(grad_h2 * normed2, axis=(0, 1))
    grad_shift2 = jnp.sum(grad_h2, axis=(0, 1))
    grad_mid = grad_top.astype(jnp.float32) + norm_back(grad_h2, normed2, inverse2, norm2_gain)
    grad_out_bias = jnp.sum(grad_mid, axis=(0, 1))
    grad_proj_bias = jnp.sum(grad_top.astype(jnp.float32), axis=(0, 1))
    grad_mid_full = tensor_gather(grad_mid.astype(jnp.bfloat16))
    grad_out_w = jnp.einsum(
        "lbo,lbi->oi", grad_mid_full, mixed, preferred_element_type=jnp.float32
    )
    grad_mixed = jnp.einsum(
        "lbo,oi->lbi", grad_mid_full, out_full, preferred_element_type=jnp.float32
    )
    grad_mixed = grad_mixed.astype(jnp.bfloat16).reshape(length, batch, heads_local, HEAD_DIM)
    grad_queries, grad_keys, grad_values = attend_backward(
        queries, keys, values, log_totals, grad_mixed
    )
    grad_qkv = jnp.stack([grad_queries, grad_keys, grad_values], axis=2).astype(jnp.bfloat16)
    grad_qkv = grad_qkv.reshape(length, batch, 3, heads_local * HEAD_DIM)
    kind_sums = jnp.sum(grad_qkv.astype(jnp.float32), axis=(0, 1))
    grad_qv_bias = jnp.stack([kind_sums[0], kind_sums[2]])
    grad_qkv_w = jnp.einsum(
        "lbd,lbce->dce", hidden1_full, grad_qkv, preferred_element_type=jnp.float32
    )
    grad_h1 = tensor_scatter(
        jnp.einsum("lbce,dce->lbd", grad_qkv, qkv_full, preferred_element_type=jnp.float32),
        jnp.float32,
    )
    grad_gain1 = jnp.sum(grad_h1 * normed1, axis=(0, 1))
    grad_shift1 = jnp.sum(grad_h1, axis=(0, 1))
    grad_in = (grad_mid + norm_back(grad_h1, normed1, inverse1, norm1_gain)).astype(
        jnp.bfloat16
    )
    depth = qkv_full.shape[0]
    mlp_grads = jnp.concatenate([grad_fc, grad_proj], axis=1)
    attn_grads = jnp.concatenate([grad_qkv_w.reshape(depth, -1), grad_out_w], axis=1)
    head_sums = jnp.concatenate([grad_qv_bias.reshape(-1), grad_fc_bias])
    feature_sums = jnp.concatenate(
        [grad_out_bias, grad_proj_bias, grad_gain1, grad_shift1, grad_gain2, grad_shift2]
    )
    return block_out, grad_in, mlp_grads, attn_grads, head_sums, feature_sums


def per_device(
    block_input,
    qkv_weight,
    qv_bias,
    out_weight,
    out_bias,
    fc_weight,
    fc_bias,
    proj_weight,
    proj_bias,
    norm1_gain,
    norm1_shift,
    norm2_gain,
    norm2_shift,
    out_grad,
):
    micro = block_input.shape[0]
    rows = qkv_weight.shape[0]
    width_qkv = qkv_weight.shape[1] * qkv_weight.shape[2]
    width_fc = fc_weight.shape[1]
    attn_pack = jnp.concatenate([qkv_weight.reshape(rows, width_qkv), out_weight], axis=1)
    mlp_pack = jnp.concatenate([fc_weight, proj_weight], axis=1)
    attn_full = lax.all_gather(attn_pack, "dp", axis=0, tiled=True)
    mlp_full = lax.all_gather(mlp_pack, "dp", axis=0, tiled=True)
    depth = attn_full.shape[0]
    weights = (
        attn_full[:, :width_qkv].reshape(depth, 3, qkv_weight.shape[2]),
        attn_full[:, width_qkv:],
        mlp_full[:, :width_fc],
        mlp_full[:, width_fc:],
    )
    params = (qv_bias, out_bias, fc_bias, proj_bias, norm1_gain, norm1_shift, norm2_gain, norm2_shift)
    grad_top_all = jnp.swapaxes(tensor_gather(jnp.swapaxes(out_grad, 0, 1)), 0, 1)
    outputs, in_grads = [], []
    mlp_acc = attn_acc = head_acc = feature_acc = None
    for index in range(micro):
        block_out, grad_in, mlp_grads, attn_grads, head_sums, feature_sums = one_micro(
            block_input[index].astype(jnp.float32),
            out_grad[index],
            grad_top_all[index],
            weights,
            params,
        )
        outputs.append(block_out)
        in_grads.append(grad_in)
        if index == 0:
            mlp_acc, attn_acc, head_acc, feature_acc = mlp_grads, attn_grads, head_sums, feature_sums
        else:
            mlp_acc = mlp_acc + mlp_grads
            attn_acc = attn_acc + attn_grads
            head_acc = head_acc + head_sums
            feature_acc = feature_acc + feature_sums
    mlp_shard = lax.psum_scatter(mlp_acc, "dp", scatter_dimension=0, tiled=True)
    small = jnp.concatenate([tensor_sum(feature_acc), head_acc])
    width_attn = attn_acc.shape[1]
    small_rows = -(-small.shape[0] // width_attn)
    small = jnp.pad(small, (0, small_rows * width_attn - small.shape[0])).reshape(
        small_rows, width_attn
    )
    blocks = depth // rows
    attn_rows = jnp.concatenate(
        [
            attn_acc.reshape(blocks, rows, width_attn),
            jnp.broadcast_to(small, (blocks, small_rows, width_attn)),
        ],
        axis=1,
    ).reshape(blocks * (rows + small_rows), width_attn)
    attn_shard = lax.psum_scatter(attn_rows, "dp", scatter_dimension=0, tiled=True)
    small_total = attn_shard[rows:].reshape(-1)
    features = small_total[: feature_acc.shape[0]].reshape(6, -1)
    head_total = small_total[feature_acc.shape[0] : feature_acc.shape[0] + head_acc.shape[0]]
    qv_size = qv_bias.size
    return (
        jnp.stack(outputs),
        jnp.stack(in_grads),
        attn_shard[:rows, :width_qkv].reshape(qkv_weight.shape),
        head_total[:qv_size].reshape(qv_bias.shape),
        attn_shard[:rows, width_qkv:],
        features[0],
        mlp_shard[:, :width_fc],
        head_total[qv_size:],
        mlp_shard[:, width_fc:],
        features[1],
        features[2],
        features[3],
        features[4],
        features[5],
    )


def solution(mesh):
    assert mesh.shape["tensor"] == 4
    devices = mesh.devices.reshape(mesh.shape["dp"], 2, 2)
    mesh = jax.sharding.Mesh(devices, ("dp", "tx", "tc"))
    in_specs = (
        P(None, ("tx", "tc"), "dp", None),
        P("dp", None, ("tx", "tc")),
        P(None, ("tx", "tc")),
        P("dp", ("tx", "tc")),
        P(),
        P("dp", ("tx", "tc")),
        P(("tx", "tc")),
        P("dp", ("tx", "tc")),
        P(),
        P(),
        P(),
        P(),
        P(),
        P(None, ("tx", "tc"), "dp", None),
    )
    out_specs = (
        P(None, ("tx", "tc"), "dp", None),
        P(None, ("tx", "tc"), "dp", None),
        P("dp", None, ("tx", "tc")),
        P(None, ("tx", "tc")),
        P("dp", ("tx", "tc")),
        P(),
        P("dp", ("tx", "tc")),
        P(("tx", "tc")),
        P("dp", ("tx", "tc")),
        P(),
        P(),
        P(),
        P(),
        P(),
    )
    return jax.shard_map(
        per_device, mesh=mesh, in_specs=in_specs, out_specs=out_specs, check_vma=False
    )
```

time: 858 us -> 682 us (0.79)
  waiting for transfers between devices: 446 us -> 297 us
  blocking collectives: 43.7 us -> 0 us
  local copies, waits for them, and re-layouts: 112 us -> 85.8 us
  other arithmetic: 81.9 us -> 106 us
  matrix products: 129 us -> 150 us
    reduce_scatter x1, waiting for transfers between devices: 162 us -> 0.01 us  [per_device(): mlp_shard = lax.psum_scatter(mlp_acc, 'dp', scatter_dimension=0, tiled=True)]
    unnamed x2 -> x5, waiting for transfers between devices: 0.03 us -> 82.2 us
    all_gather x1 -> x2, waiting for transfers between devices: 65.5 us -> 11.5 us  [the longest x1 11.5 us: per_device(): attn_full = lax.all_gather(attn_pack, 'dp', axis=0, tiled=True)]
    psum x1 -> x0, blocking collectives: 43.7 us -> none  [per_device(): lax.psum(jnp.concatenate([feature_vec, head_slots.reshape(-1)]), ('dp', '...]
    while x232 -> x0, local copies, waits for them, and re-layouts: 38.2 us -> none
    another operation x12, local copies, waits for them, and re-layouts: 25.9 us -> 9.34 us  [one_micro(): jnp.stack([grad_queries, grad_keys, grad_values], axis=2)]
    dot_general x0 -> x4, local copies, waits for them, and re-layouts: none -> 14.5 us  [the longest x2 8 us: one_micro(): jnp.einsum('lbo,lbi->oi', grad_mid_full, mixed, preferred_element_type=jn...]
    ppermute x8, waiting for transfers between devices: 10.5 us -> 0.02 us  [tensor_scatter(): got = lax.ppermute(send.astype(send_dtype), 'tc', SWAP)]
  transfers between devices with their start and end apart: 32 -> 36, of which waited for: 25 -> 17; matrix products, arithmetic and copies ran while one was open for 20% -> 35% of each run, Pallas kernels for 0% -> 0%
where the time goes in v3:
time: 682 us; the launch traced here: 677 us
  waiting for transfers between devices  297 us (44%)
  matrix products  150 us (22%)
  other arithmetic  106 us (16%)
  local copies, waits for them, and re-layouts  85.8 us (13%)
  starting transfers between devices  21.2 us (3%)
  between operations  16.1 us (2%)
    ppermute x8, waiting for transfers between devices, tensor_scatter(): got2 = lax.ppermute(send2.astype(send_dtype), 'tx', SWAP)  124 us
    unnamed x5, waiting for transfers between devices  82.2 us
    ppermute x7, waiting for transfers between devices, tensor_gather(): other = lax.ppermute(block, 'tx', SWAP)  75.3 us
    unnamed x243, local copies, waits for them, and re-layouts  23.8 us
    dot_general x4, matrix products, attend_forward(): jnp.einsum('bhqk,kbhe->qbhe', weights, values, preferred_element_type=jnp...  17.4 us
    dot_general x4, matrix products, causal_scores(): jnp.einsum('qbhe,kbhe->bhqk', query_block, keys, preferred_element_type=j...  17.1 us
    reduce_sum x4, other arithmetic, attend_forward(): total = jnp.sum(raised, axis=-1, keepdims=True)  15.3 us
    dot_general x4, matrix products, attend_backward(): jnp.einsum('qbhe,kbhe->bhqk', grad_block, values, preferred_element_type=...  15.2 us
  transfers between devices with their start and end apart: 36, of which 17 were waited for; matrix products, arithmetic and copies ran while one was open for 35% of the time, Pallas kernels for 0%

profile of v3, /device:TPU:0, one launch (start us, length us, event | category | flops | bytes accessed | tf_op | source)
XLA Modules:
  0.0 676.6 jit_solution(7567761976600985752)
XLA Ops:
  20.1 11.3 %collective-permute-done = bf16[256,1,1024]{2,0,1:T(8,128)(2,1)S(1)} collective-permute-done((bf16[256,1,1024]{2,0,1:T(8,128)(2,1)}, bf16[256,1,1024]{2,0,1:T(8,128)(2,1)S(1)}, u32[]{:S(2)}, u32[]{:S(2)}) %collective-permute-start) | collective-permute-done | bytes 524320 | tf_op jit(solution)/shard_map/ppermute | solution.py:107
  32.7 9.1 %collective-permute-done.8 = bf16[256,1,1024]{2,0,1:T(8,128)(2,1)S(1)} collective-permute-done((bf16[256,1,1024]{2,0,1:T(8,128)(2,1)}, bf16[256,1,1024]{2,0,1:T(8,128)(2,1)S(1)}, u32[]{:S(2)}, u32[]{:S(2)}) %collective-permute-start.8) | collective-permute-done | bytes 524320 | tf_op jit(solution)/shard_map/ppermute | solution.py:107
  51.0 11.5 %all-gather.3.cloned.1.call-done = bf16[1024,1024]{1,0:T(8,128)(2,1)} async-done(((bf16[128,1024]{1,0:T(8,128)(2,1)}), bf16[1024,1024]{1,0:T(8,128)(2,1)}) %all-gather.3.cloned.1.call-update) | async-done | bytes 2097168 | tf_op jit(solution)/shard_map/all_gather | solution.py:254
  73.4 5.4 fusion.193
  78.8 4.9 fusion.192
  83.8 4.9 fusion.194
  97.4 5.1 fusion.35
  107.6 6.1 fusion.32
  120.8 4.8 fusion.2
  149.3 14.5 %collective-permute-done.16 = bf16[256,2,1,1024]{3,0,1,2:T(8,128)(2,1)S(1)} collective-permute-done((bf16[256,2,1,1024]{3,0,1,2:T(8,128)(2,1)S(1)}, bf16[256,2,1,1024]{3,0,1,2:T(8,128)(2,1)S(1)}, u32[]{:S(2)}, u32[]{:S(2)}) %collective-permute-start.16) | collective-permute-done | bytes 1048608 | tf_op jit(solution)/shard_map/ppermute | solution.py:107
  174.9 11.5 %collective-permute-done.3 = f32[256,1,1024]{2,0,1:T(8,128)} collective-permute-done((f32[256,1,1024]{2,0,1:T(8,128)}, f32[256,1,1024]{2,0,1:T(8,128)}, u32[]{:S(2)}, u32[]{:S(2)}) %collective-permute-start.3) | collective-permute-done | bytes 1048608 | tf_op jit(solution)/shard_map/ppermute | solution.py:127
  186.4 22.0 %collective-permute-done.11 = f32[256,1,1024]{2,0,1:T(8,128)} collective-permute-done((f32[256,1,1024]{2,0,1:T(8,128)}, f32[256,1,1024]{2,0,1:T(8,128)}, u32[]{:S(2)}, u32[]{:S(2)}) %collective-permute-start.11) | collective-permute-done | bytes 1048608 | tf_op jit(solution)/shard_map/ppermute | solution.py:127
  214.1 4.5 maximum_select_fusion
  218.6 8.3 %collective-permute-done.4 = bf16[256,1,1024]{2,0,1:T(8,128)(2,1)S(1)} collective-permute-done((bf16[256,1,1024]{2,0,1:T(8,128)(2,1)S(1)}, bf16[256,1,1024]{2,0,1:T(8,128)(2,1)S(1)}, u32[]{:S(2)}, u32[]{:S(2)}) %collective-permute-start.4) | collective-permute-done | bytes 524320 | tf_op jit(solution)/shard_map/ppermute | solution.py:107
  227.1 9.6 %collective-permute-done.12 = bf16[256,1,1024]{2,0,1:T(8,128)(2,1)S(1)} collective-permute-done((bf16[256,1,1024]{2,0,1:T(8,128)(2,1)S(1)}, bf16[256,1,1024]{2,0,1:T(8,128)(2,1)S(1)}, u32[]{:S(2)}, u32[]{:S(2)}) %collective-permute-start.12) | collective-permute-done | bytes 524320 | tf_op jit(solution)/shard_map/ppermute | solution.py:107
  241.4 4.7 fusion.70
  246.2 6.3 convert_reduce_fusion
  259.8 6.0 multiply_convert_fusion.5
  271.5 8.0 %convert_reduce_fusion.1 = (f32[1024]{0:T(1024)}, bf16[1024,1024]{1,0:T(8,128)(2,1)S(1)}) fusion(bf16[1024,2048]{1,0:T(8,128)(2,1)S(1)} %copy-done.93, bf16[2,1024,1,1024]{3,1,0,2:T(8,128)(2,1)S(1)} %bitcast.663, f32[1024,1024]{1,0:T(8,128)} %get-tuple-element.162, f32[1024]{0:T(1024)S(1)} %copy-done.94), kind=kOutput, calls=%fused_computation.61 | convolution fusion | flops 2175794176 | bytes 10493952 | tf_op jit(solution)/shard_map/lbo,of->lbf/dot_general | solution.py:177
  307.1 4.8 maximum_add_fusion
  312.0 51.3 %collective-permute-done.7 = bf16[256,1,1024]{2,0,1:T(8,128)(2,1)} collective-permute-done((bf16[256,1,1024]{2,0,1:T(8,128)(2,1)}, bf16[256,1,1024]{2,0,1:T(8,128)(2,1)}, u32[]{:S(2)}, u32[]{:S(2)}) %collective-permute-start.7) | collective-permute-done | bytes 524320 | tf_op jit(solution)/shard_map/ppermute | solution.py:127
  363.3 5.5 multiply_reduce_fusion.4
  373.4 22.4 %collective-permute-done.20 = bf16[256,1,1024]{2,0,1:T(8,128)(2,1)S(1)} collective-permute-done((bf16[256,1,1024]{2,0,1:T(8,128)(2,1)S(1)}, bf16[256,1,1024]{2,0,1:T(8,128)(2,1)S(1)}, u32[]{:S(2)}, u32[]{:S(2)}) %collective-permute-start.20) | collective-permute-done | bytes 524320 | tf_op jit(solution)/shard_map/ppermute | solution.py:107
  413.9 5.0 fusion.20
  422.2 5.0 multiply_reduce_fusion.1
  427.3 4.6 multiply_convert_fusion.1
  455.6 5.1 multiply_reduce_fusion.3
  481.9 5.5 convolution_bitcast_fusion.1
  518.4 16.9 %collective-permute-done.29 = f32[256,1,1024]{2,0,1:T(8,128)} collective-permute-done((f32[256,1,1024]{2,0,1:T(8,128)}, f32[256,1,1024]{2,0,1:T(8,128)}, u32[]{:S(2)}, u32[]{:S(2)}) %collective-permute-start.29) | collective-permute-done | bytes 1048608 | tf_op jit(solution)/shard_map/ppermute | solution.py:127
  535.3 21.9 %collective-permute-done.23 = f32[256,1,1024]{2,0,1:T(8,128)} collective-permute-done((f32[256,1,1024]{2,0,1:T(8,128)}, f32[256,1,1024]{2,0,1:T(8,128)}, u32[]{:S(2)}, u32[]{:S(2)}) %collective-permute-start.23) | collective-permute-done | bytes 1048608 | tf_op jit(solution)/shard_map/ppermute | solution.py:127
  566.2 4.9 pad_maximum_fusion
  580.4 82.1 %reduce-scatter.7.cloned.1.call-done = f32[136,1024]{1,0:T(8,128)} async-done(((f32[1088,1024]{1,0:T(8,128)}), f32[136,1024]{1,0:T(8,128)}) %reduce-scatter.7.cloned.1.call-update) | async-done | bytes 557072
  (509 shorter events, 266.8 us)
Async XLA Ops:
  7.2 55.3 %all-gather.3.cloned.1.call-start = ((), (), s32[]{:S(2)}) async-start(), calls=%async_computation.2 | async-start | bytes 2359296 | tf_op jit(solution)/shard_map/all_gather | solution.py:254
  10.2 231.3 %all-gather.5.cloned.1.call-start = ((), (), s32[]{:S(2)}) async-start(), calls=%async_computation.3 | async-start | bytes 4718592 | tf_op jit(solution)/shard_map/all_gather | solution.py:255
  15.5 15.9 %collective-permute-start = (bf16[256,1,1024]{2,0,1:T(8,128)(2,1)}, bf16[256,1,1024]{2,0,1:T(8,128)(2,1)S(1)}, u32[]{:S(2)}, u32[]{:S(2)}) collective-permute-start(bf16[256,1,1024]{2,0,1:T(8,128)(2,1)} %get-tuple-element.110), channel_id=1, source_target_pairs={{0,2},{2,0},{1,3},{3,1},{4,6},{6,4},{5,7},{7,5},{8,10},{10,8},{9,1... | collective-permute-start | bytes 1572872 | tf_op jit(solution)/shard_map/ppermute | solution.py:107
  18.4 23.4 %collective-permute-start.8 = (bf16[256,1,1024]{2,0,1:T(8,128)(2,1)}, bf16[256,1,1024]{2,0,1:T(8,128)(2,1)S(1)}, u32[]{:S(2)}, u32[]{:S(2)}) collective-permute-start(bf16[256,1,1024]{2,0,1:T(8,128)(2,1)} %get-tuple-element.111), channel_id=1, source_target_pairs={{0,2},{2,0},{1,3},{3,1},{4,6},{6,4},{5,7},{7,5},{8,10},{10,8},{9,1... | collective-permute-start | bytes 1572872 | tf_op jit(solution)/shard_map/ppermute | solution.py:107
  32.5 11.2 %collective-permute-start.1 = (bf16[2,256,1,1024]{3,1,2,0:T(8,128)(2,1)}, bf16[2,256,1,1024]{3,1,2,0:T(8,128)(2,1)}, u32[]{:S(2)}, u32[]{:S(2)}) collective-permute-start(bf16[2,256,1,1024]{3,1,2,0:T(8,128)(2,1)} %maximum_select_fusion.7), channel_id=1, source_target_pairs={{0,1},{1,0},{2,3},{3,2},{4,5},{5,4},{6,7},{7,6},{8,9},{9,8},{10,11... | collective-permute-start | bytes 3145736 | tf_op jit(solution)/shard_map/ppermute | solution.py:109
  42.0 6.7 collective-permute-start.9
  120.8 18.5 %collective-permute-start.2 = (f32[2,256,1,1024]{3,1,0,2:T(8,128)}, f32[2,256,1,1024]{3,1,0,2:T(8,128)}, u32[]{:S(2)}, u32[]{:S(2)}) collective-permute-start(f32[2,256,1,1024]{3,1,0,2:T(8,128)} %dynamic-slice_bitcast_fusion.5), channel_id=1, source_target_pairs={{0,1},{1,0},{2,3},{3,2},{4,5},{5,4},{6,7},{7,6},{8,9},{9,8},{10,11... | collective-permute-start | bytes 6291464 | tf_op jit(solution)/shard_map/ppermute | solution.py:123
  136.6 7.2 %collective-permute-start.10 = (f32[2,256,1,1024]{3,1,2,0:T(8,128)}, f32[2,256,1,1024]{3,1,2,0:T(8,128)}, u32[]{:S(2)}, u32[]{:S(2)}) collective-permute-start(f32[2,256,1,1024]{3,1,2,0:T(8,128)} %dynamic-slice_bitcast_fusion.4), channel_id=1, source_target_pairs={{0,1},{1,0},{2,3},{3,2},{4,5},{5,4},{6,7},{7,6},{8,9},{9,8},{10,11... | collective-permute-start | bytes 6291464 | tf_op jit(solution)/shard_map/ppermute | solution.py:123
  137.5 439.4 %reduce-scatter.5.cloned.1.call-start = ((), (), s32[]{:S(2)}) async-start(), calls=%async_computation.4 | async-start | bytes 9437184 | tf_op jit(solution)/shard_map/reduce_scatter | solution.py:284
  137.8 26.1 %collective-permute-start.16 = (bf16[256,2,1,1024]{3,0,1,2:T(8,128)(2,1)S(1)}, bf16[256,2,1,1024]{3,0,1,2:T(8,128)(2,1)S(1)}, u32[]{:S(2)}, u32[]{:S(2)}) collective-permute-start(bf16[256,2,1,1024]{3,0,1,2:T(8,128)(2,1)S(1)} %bitcast.603), channel_id=1, source_target_pairs={{0,2},{2,0},{1,3},{3,1},{4,6},{6,4},{5,7},{7,5},{8,10},{10,8},{9,1... | collective-permute-start | bytes 3145736 | tf_op jit(solution)/shard_map/ppermute | solution.py:107
  143.2 43.2 %collective-permute-start.3 = (f32[256,1,1024]{2,0,1:T(8,128)}, f32[256,1,1024]{2,0,1:T(8,128)}, u32[]{:S(2)}, u32[]{:S(2)}) collective-permute-start(f32[256,1,1024]{2,0,1:T(8,128)} %dynamic-slice_bitcast_fusion.11), channel_id=1, source_target_pairs={{0,2},{2,0},{1,3},{3,1},{4,6},{6,4},{5,7},{7,5},{8,10},{10,8},{9,1... | collective-permute-start | bytes 3145736 | tf_op jit(solution)/shard_map/ppermute | solution.py:127
  147.6 60.8 %collective-permute-start.11 = (f32[256,1,1024]{2,0,1:T(8,128)}, f32[256,1,1024]{2,0,1:T(8,128)}, u32[]{:S(2)}, u32[]{:S(2)}) collective-permute-start(f32[256,1,1024]{2,0,1:T(8,128)} %dynamic-slice_bitcast_fusion.10), channel_id=1, source_target_pairs={{0,2},{2,0},{1,3},{3,1},{4,6},{6,4},{5,7},{7,5},{8,10},{10,8},{9,1... | collective-permute-start | bytes 3145736 | tf_op jit(solution)/shard_map/ppermute | solution.py:127
  165.5 48.6 %collective-permute-start.17 = (bf16[2,256,2,1,1024]{4,1,0,2,3:T(8,128)(2,1)}, bf16[2,256,2,1,1024]{4,1,0,2,3:T(8,128)(2,1)}, u32[]{:S(2)}, u32[]{:S(2)}) collective-permute-start(bf16[2,256,2,1,1024]{4,1,0,2,3:T(8,128)(2,1)} %maximum_select_fusion.3), channel_id=1, source_target_pairs={{0,1},{1,0},{2,3},{3,2},{4,5},{5,4},{6,7},{7,6},{8,9},{9,8},{10,11... | collective-permute-start | bytes 6291464 | tf_op jit(solution)/shard_map/ppermute | solution.py:109
  212.0 14.9 %collective-permute-start.4 = (bf16[256,1,1024]{2,0,1:T(8,128)(2,1)S(1)}, bf16[256,1,1024]{2,0,1:T(8,128)(2,1)S(1)}, u32[]{:S(2)}, u32[]{:S(2)}) collective-permute-start(bf16[256,1,1024]{2,0,1:T(8,128)(2,1)S(1)} %get-tuple-element.144), channel_id=1, source_target_pairs={{0,2},{2,0},{1,3},{3,1},{4,6},{6,4},{5,7},{7,5},{8,10},{10,8},{9,1... | collective-permute-start | bytes 1572872 | tf_op jit(solution)/shard_map/ppermute | solution.py:107
  213.5 23.2 %collective-permute-start.12 = (bf16[256,1,1024]{2,0,1:T(8,128)(2,1)S(1)}, bf16[256,1,1024]{2,0,1:T(8,128)(2,1)S(1)}, u32[]{:S(2)}, u32[]{:S(2)}) collective-permute-start(bf16[256,1,1024]{2,0,1:T(8,128)(2,1)S(1)} %get-tuple-element.145), channel_id=1, source_target_pairs={{0,2},{2,0},{1,3},{3,1},{4,6},{6,4},{5,7},{7,5},{8,10},{10,8},{9,1... | collective-permute-start | bytes 1572872 | tf_op jit(solution)/shard_map/ppermute | solution.py:107
  227.0 10.4 %collective-permute-start.5 = (bf16[2,256,1,1024]{3,1,2,0:T(8,128)(2,1)S(1)}, bf16[2,256,1,1024]{3,1,2,0:T(8,128)(2,1)S(1)}, u32[]{:S(2)}, u32[]{:S(2)}) collective-permute-start(bf16[2,256,1,1024]{3,1,2,0:T(8,128)(2,1)S(1)} %maximum_select_fusion.9), channel_id=1, source_target_pairs={{0,1},{1,0},{2,3},{3,2},{4,5},{5,4},{6,7},{7,6},{8,9},{9,8},{10,11... | collective-permute-start | bytes 3145736 | tf_op jit(solution)/shard_map/ppermute | solution.py:109
  258.9 36.8 %collective-permute-start.24 = (f32[2,256,1,1024]{3,1,2,0:T(8,128)}, f32[2,256,1,1024]{3,1,2,0:T(8,128)S(1)}, u32[]{:S(2)}, u32[]{:S(2)}) collective-permute-start(f32[2,256,1,1024]{3,1,2,0:T(8,128)} %dynamic-slice_bitcast_fusion.1), channel_id=1, source_target_pairs={{0,1},{1,0},{2,3},{3,2},{4,5},{5,4},{6,7},{7,6},{8,9},{9,8},{10,11... | collective-permute-start | bytes 6291464 | tf_op jit(solution)/shard_map/ppermute | solution.py:123
  268.3 21.8 %collective-permute-start.14 = (bf16[2,256,1,1024]{3,1,2,0:T(8,128)(2,1)S(1)}, bf16[2,256,1,1024]{3,1,2,0:T(8,128)(2,1)}, u32[]{:S(2)}, u32[]{:S(2)}) collective-permute-start(bf16[2,256,1,1024]{3,1,2,0:T(8,128)(2,1)S(1)} %fusion.139), channel_id=1, source_target_pairs={{0,1},{1,0},{2,3},{3,2},{4,5},{5,4},{6,7},{7,6},{8,9},{9,8},{10,11... | collective-permute-start | bytes 3145736 | tf_op jit(solution)/shard_map/ppermute | solution.py:123
  271.1 23.0 %collective-permute-start.6 = (bf16[2,256,1,1024]{3,1,0,2:T(8,128)(2,1)S(1)}, bf16[2,256,1,1024]{3,1,0,2:T(8,128)(2,1)}, u32[]{:S(2)}, u32[]{:S(2)}) collective-permute-start(bf16[2,256,1,1024]{3,1,0,2:T(8,128)(2,1)S(1)} %fusion.138), channel_id=1, source_target_pairs={{0,1},{1,0},{2,3},{3,2},{4,5},{5,4},{6,7},{7,6},{8,9},{9,8},{10,11... | collective-permute-start | bytes 3145736 | tf_op jit(solution)/shard_map/ppermute | solution.py:123
  283.4 14.6 %collective-permute-start.18 = (f32[2,256,1,1024]{3,1,2,0:T(8,128)}, f32[2,256,1,1024]{3,1,2,0:T(8,128)}, u32[]{:S(2)}, u32[]{:S(2)}) collective-permute-start(f32[2,256,1,1024]{3,1,2,0:T(8,128)} %dynamic-slice_bitcast_fusion.3), channel_id=1, source_target_pairs={{0,1},{1,0},{2,3},{3,2},{4,5},{5,4},{6,7},{7,6},{8,9},{9,8},{10,11... | collective-permute-start | bytes 6291464 | tf_op jit(solution)/shard_map/ppermute | solution.py:123
  292.6 19.4 %collective-permute-start.15 = (bf16[256,1,1024]{2,0,1:T(8,128)(2,1)}, bf16[256,1,1024]{2,0,1:T(8,128)(2,1)}, u32[]{:S(2)}, u32[]{:S(2)}) collective-permute-start(bf16[256,1,1024]{2,0,1:T(8,128)(2,1)} %fusion.151), channel_id=1, source_target_pairs={{0,2},{2,0},{1,3},{3,1},{4,6},{6,4},{5,7},{7,5},{8,10},{10,8},{9,1... | collective-permute-start | bytes 1572872 | tf_op jit(solution)/shard_map/ppermute | solution.py:127
  297.5 65.9 %collective-permute-start.25 = (f32[256,1,1024]{2,0,1:T(8,128)}, f32[256,1,1024]{2,0,1:T(8,128)}, u32[]{:S(2)}, u32[]{:S(2)}) collective-permute-start(f32[256,1,1024]{2,0,1:T(8,128)} %dynamic-slice_bitcast_fusion.7), channel_id=1, source_target_pairs={{0,2},{2,0},{1,3},{3,1},{4,6},{6,4},{5,7},{7,5},{8,10},{10,8},{9,1... | collective-permute-start | bytes 3145736 | tf_op jit(solution)/shard_map/ppermute | solution.py:127
  301.7 61.6 %collective-permute-start.19 = (f32[256,1,1024]{2,0,1:T(8,128)}, f32[256,1,1024]{2,0,1:T(8,128)}, u32[]{:S(2)}, u32[]{:S(2)}) collective-permute-start(f32[256,1,1024]{2,0,1:T(8,128)} %dynamic-slice_bitcast_fusion.9), channel_id=1, source_target_pairs={{0,2},{2,0},{1,3},{3,1},{4,6},{6,4},{5,7},{7,5},{8,10},{10,8},{9,1... | collective-permute-start | bytes 3145736 | tf_op jit(solution)/shard_map/ppermute | solution.py:127
  304.0 59.3 %collective-permute-start.7 = (bf16[256,1,1024]{2,0,1:T(8,128)(2,1)}, bf16[256,1,1024]{2,0,1:T(8,128)(2,1)}, u32[]{:S(2)}, u32[]{:S(2)}) collective-permute-start(bf16[256,1,1024]{2,0,1:T(8,128)(2,1)} %fusion.150), channel_id=1, source_target_pairs={{0,2},{2,0},{1,3},{3,1},{4,6},{6,4},{5,7},{7,5},{8,10},{10,8},{9,1... | collective-permute-start | bytes 1572872 | tf_op jit(solution)/shard_map/ppermute | solution.py:127
  311.9 350.5 %reduce-scatter.7.cloned.1.call-start = ((), (), s32[]{:S(2)}) async-start(), calls=%async_computation.5 | async-start | bytes 5013504
  371.2 25.1 %collective-permute-start.26 = (bf16[256,1,1024]{2,0,1:T(8,128)(2,1)S(1)}, bf16[256,1,1024]{2,0,1:T(8,128)(2,1)S(1)}, u32[]{:S(2)}, u32[]{:S(2)}) collective-permute-start(bf16[256,1,1024]{2,0,1:T(8,128)(2,1)S(1)} %convert_element_type.431), channel_id=1, source_target_pairs={{0,2},{2,0},{1,3},{3,1},{4,6},{6,4},{5,7},{7,5},{8,10},{10,8},{9,1... | collective-permute-start | bytes 1572872 | tf_op jit(solution)/shard_map/ppermute | solution.py:107
  372.7 23.1 %collective-permute-start.20 = (bf16[256,1,1024]{2,0,1:T(8,128)(2,1)S(1)}, bf16[256,1,1024]{2,0,1:T(8,128)(2,1)S(1)}, u32[]{:S(2)}, u32[]{:S(2)}) collective-permute-start(bf16[256,1,1024]{2,0,1:T(8,128)(2,1)S(1)} %convert_element_type.421), channel_id=1, source_target_pairs={{0,2},{2,0},{1,3},{3,1},{4,6},{6,4},{5,7},{7,5},{8,10},{10,8},{9,1... | collective-permute-start | bytes 1572872 | tf_op jit(solution)/shard_map/ppermute | solution.py:107
  397.4 12.1 %collective-permute-start.27 = (bf16[2,256,1,1024]{3,1,2,0:T(8,128)(2,1)}, bf16[2,256,1,1024]{3,1,2,0:T(8,128)(2,1)}, u32[]{:S(2)}, u32[]{:S(2)}) collective-permute-start(bf16[2,256,1,1024]{3,1,2,0:T(8,128)(2,1)} %maximum_select_fusion.15), channel_id=1, source_target_pairs={{0,1},{1,0},{2,3},{3,2},{4,5},{5,4},{6,7},{7,6},{8,9},{9,8},{10,11... | collective-permute-start | bytes 3145736 | tf_op jit(solution)/shard_map/ppermute | solution.py:109
  455.5 50.3 %collective-permute-start.28 = (f32[2,256,1,1024]{3,1,2,0:T(8,128)}, f32[2,256,1,1024]{3,1,2,0:T(8,128)}, u32[]{:S(2)}, u32[]{:S(2)}) collective-permute-start(f32[2,256,1,1024]{3,1,2,0:T(8,128)} %dynamic-slice_bitcast_fusion), channel_id=1, source_target_pairs={{0,1},{1,0},{2,3},{3,2},{4,5},{5,4},{6,7},{7,6},{8,9},{9,8},{10,11... | collective-permute-start | bytes 6291464 | tf_op jit(solution)/shard_map/ppermute | solution.py:123
  497.3 13.2 %collective-permute-start.22 = (f32[2,256,1,1024]{3,1,2,0:T(8,128)S(1)}, f32[2,256,1,1024]{3,1,2,0:T(8,128)S(1)}, u32[]{:S(2)}, u32[]{:S(2)}) collective-permute-start(f32[2,256,1,1024]{3,1,2,0:T(8,128)S(1)} %dynamic-slice_bitcast_fusion.2), channel_id=1, source_target_pairs={{0,1},{1,0},{2,3},{3,2},{4,5},{5,4},{6,7},{7,6},{8,9},{9,8},{10,11... | collective-permute-start | bytes 6291464 | tf_op jit(solution)/shard_map/ppermute | solution.py:123
  509.0 26.3 %collective-permute-start.29 = (f32[256,1,1024]{2,0,1:T(8,128)}, f32[256,1,1024]{2,0,1:T(8,128)}, u32[]{:S(2)}, u32[]{:S(2)}) collective-permute-start(f32[256,1,1024]{2,0,1:T(8,128)} %dynamic-slice_bitcast_fusion.6), channel_id=1, source_target_pairs={{0,2},{2,0},{1,3},{3,1},{4,6},{6,4},{5,7},{7,5},{8,10},{10,8},{9,1... | collective-permute-start | bytes 3145736 | tf_op jit(solution)/shard_map/ppermute | solution.py:127
  512.1 45.2 %collective-permute-start.23 = (f32[256,1,1024]{2,0,1:T(8,128)}, f32[256,1,1024]{2,0,1:T(8,128)}, u32[]{:S(2)}, u32[]{:S(2)}) collective-permute-start(f32[256,1,1024]{2,0,1:T(8,128)} %dynamic-slice_bitcast_fusion.8), channel_id=1, source_target_pairs={{0,2},{2,0},{1,3},{3,1},{4,6},{6,4},{5,7},{7,5},{8,10},{10,8},{9,1... | collective-permute-start | bytes 3145736 | tf_op jit(solution)/shard_map/ppermute | solution.py:127
  (117 other events, 1368.7 us)
Sparse Core Ops, SparseCore 0:
  10.7 51.7 all-gather.2
  137.6 71.4 all-gather.4
  312.0 146.3 reduce-scatter.4
  571.3 91.1 reduce-scatter.6

commit v4 on v3

--- a/solution.py
+++ b/solution.py
@@ -32,24 +32,23 @@
     return inverse * (grad_normed - first - normed * second)
 
 
-def causal_scores(query_block, keys, offset):
+def causal_scores(query_block, keys, positions, offset):
     scores = jnp.einsum(
         "qbhe,kbhe->bhqk", query_block, keys, preferred_element_type=jnp.float32
     ) * HEAD_DIM ** (-0.5)
     height = query_block.shape[0]
-    length = keys.shape[0]
-    row_pos = lax.broadcasted_iota(jnp.int32, (height, length), 0) + offset
-    col_pos = lax.broadcasted_iota(jnp.int32, (height, length), 1)
+    row_pos = lax.dynamic_slice_in_dim(positions, offset, height)[:, None]
+    col_pos = positions[None, :]
     return jnp.where(col_pos <= row_pos, scores, -1e30)
 
 
-def attend_forward(queries, keys, values):
+def attend_forward(queries, keys, values, positions):
     length = keys.shape[0]
     span = min(block_rows, length)
     outputs = []
     totals = []
     for offset in range(0, length, span):
-        scores = causal_scores(queries[offset : offset + span], keys, offset)
+        scores = causal_scores(queries[offset : offset + span], keys, positions, offset)
         peak = jnp.max(scores, axis=-1, keepdims=True)
         raised = jnp.exp(scores - peak)
         total = jnp.sum(raised, axis=-1, keepdims=True)
@@ -61,7 +60,7 @@
     return (jnp.concatenate(outputs, 0), jnp.concatenate(totals, 2))
 
 
-def attend_backward(queries, keys, values, log_totals, grad_out):
+def attend_backward(queries, keys, values, log_totals, grad_out, positions):
     length = keys.shape[0]
     span = min(block_rows, length)
     scale = HEAD_DIM ** (-0.5)
@@ -71,7 +70,7 @@
     for offset in range(0, length, span):
         query_block = queries[offset : offset + span]
         grad_block = grad_out[offset : offset + span]
-        scores = causal_scores(query_block, keys, offset)
+        scores = causal_scores(query_block, keys, positions, offset)
         probs = jnp.exp(scores - log_totals[:, :, offset : offset + span])
         grad_probs = jnp.einsum(
             "qbhe,kbhe->bhqk", grad_block, values, preferred_element_type=jnp.float32
@@ -101,31 +100,26 @@
 SWAP = [(0, 1), (1, 0)]
 
 
+BLOCK_XOR = (0, 2, 1, 3)
+
+
 def tensor_gather(block):
-    across = lax.axis_index("tx")
-    core = lax.axis_index("tc")
-    other = lax.ppermute(block, "tx", SWAP)
-    pair = jnp.where(across == 0, jnp.stack([block, other]), jnp.stack([other, block]))
-    pair_other = lax.ppermute(pair, "tc", SWAP)
-    full = jnp.where(
-        core == 0, jnp.stack([pair, pair_other], 1), jnp.stack([pair_other, pair], 1)
-    )
-    return full.reshape((4 * block.shape[0],) + block.shape[1:])
+    pair = jnp.concatenate([block, lax.ppermute(block, "tx", SWAP)])
+    return jnp.concatenate([pair, lax.ppermute(pair, "tc", SWAP)])
 
 
 def tensor_scatter(parts, send_dtype):
-    across = lax.axis_index("tx")
-    core = lax.axis_index("tc")
     rows = parts.shape[0] // 4
-    grid = parts.reshape((2, 2, rows) + parts.shape[1:])
-    keep = lax.dynamic_index_in_dim(grid, core, 1, keepdims=False)
-    send = lax.dynamic_index_in_dim(grid, 1 - core, 1, keepdims=False)
-    got = lax.ppermute(send.astype(send_dtype), "tc", SWAP)
-    chip = keep + got.astype(jnp.float32)
-    keep2 = lax.dynamic_index_in_dim(chip, across, 0, keepdims=False)
-    send2 = lax.dynamic_index_in_dim(chip, 1 - across, 0, keepdims=False)
-    got2 = lax.ppermute(send2.astype(send_dtype), "tx", SWAP)
-    return keep2 + got2.astype(jnp.float32)
+    got = lax.ppermute(parts[2 * rows :].astype(send_dtype), "tc", SWAP)
+    chip = parts[: 2 * rows] + got.astype(jnp.float32)
+    got2 = lax.ppermute(chip[rows:].astype(send_dtype), "tx", SWAP)
+    return chip[:rows] + got2.astype(jnp.float32)
+
+
+def block_positions(rows):
+    own = lax.axis_index("tx") * 2 + lax.axis_index("tc")
+    starts = jnp.bitwise_xor(own, jnp.array(BLOCK_XOR, jnp.int32)) * rows
+    return (starts[:, None] + jnp.arange(rows, dtype=jnp.int32)[None, :]).reshape(-1)
 
 
 def tensor_sum(vector):
@@ -151,7 +145,8 @@
     queries = split[:, :, 0]
     keys = split[:, :, 1]
     values = split[:, :, 2]
-    attended, log_totals = attend_forward(queries, keys, values)
+    positions = block_positions(resid_in.shape[0])
+    attended, log_totals = attend_forward(queries, keys, values, positions)
     mixed = attended.astype(jnp.bfloat16).reshape(length, batch, heads_local * HEAD_DIM)
     attn_branch = tensor_scatter(
         jnp.einsum("lbi,oi->lbo", mixed, out_full, preferred_element_type=jnp.float32),
@@ -201,7 +196,7 @@
     )
     grad_mixed = grad_mixed.astype(jnp.bfloat16).reshape(length, batch, heads_local, HEAD_DIM)
     grad_queries, grad_keys, grad_values = attend_backward(
-        queries, keys, values, log_totals, grad_mixed
+        queries, keys, values, log_totals, grad_mixed, positions
     )
     grad_qkv = jnp.stack([grad_queries, grad_keys, grad_values], axis=2).astype(jnp.bfloat16)
     grad_qkv = grad_qkv.reshape(length, batch, 3, heads_local * HEAD_DIM)

time: 682 us -> 683 us (level)
  local copies, waits for them, and re-layouts: 85.8 us -> 62.4 us
  matrix products: 150 us -> 163 us
    select_n x21 -> x0, other arithmetic: 20.5 us -> none  [the longest x7 13.3 us: tensor_gather(): jnp.where(core == 0, jnp.stack([pair, pair_other], 1), jnp.stack([pair_ot...]
    squeeze x12 -> x0, local copies, waits for them, and re-layouts: 16.1 us -> none  [the longest x6 9.31 us: tensor_scatter(): send = lax.dynamic_index_in_dim(grid, 1 - core, 1, keepdims=False)]
    dot_general x0 -> x6, other arithmetic: none -> 13.6 us  [the longest x4 10.6 us: one_micro(): jnp.einsum('lbd,lbce->dce', hidden1_full, grad_qkv, preferred_element_typ...]
    all_gather x1, waiting for transfers between devices: 11.5 us -> 21.4 us  [per_device(): attn_full = lax.all_gather(attn_pack, 'dp', axis=0, tiled=True)]
    slice x0 -> x14, local copies, waits for them, and re-layouts: none -> 9.65 us  [the longest x6 6.23 us: tensor_scatter(): got = lax.ppermute(parts[2 * rows:].astype(send_dtype), 'tc', SWAP)]
    concatenate x0 -> x7, other arithmetic: none -> 7.41 us  [tensor_gather(): pair = jnp.concatenate([block, lax.ppermute(block, 'tx', SWAP)])]
    unnamed x243 -> x262, local copies, waits for them, and re-layouts: 23.8 us -> 19.4 us
  transfers between devices with their start and end apart: 36 -> 36, of which waited for: 17 -> 18; matrix products, arithmetic and copies ran while one was open for 35% -> 41% of each run, Pallas kernels for 0% -> 0%
where the time goes in v4:
time: 683 us; the launch traced here: 673 us
  waiting for transfers between devices  303 us (44%)
  matrix products  163 us (24%)
  other arithmetic  107 us (16%)
  local copies, waits for them, and re-layouts  62.4 us (9%)
  starting transfers between devices  20.6 us (3%)
  between operations  16.1 us (2%)
    ppermute x8, waiting for transfers between devices, tensor_scatter(): got2 = lax.ppermute(chip[rows:].astype(send_dtype), 'tx', SWAP)  132 us
    unnamed x5, waiting for transfers between devices  80.4 us
    ppermute x7, waiting for transfers between devices, tensor_gather(): pair = jnp.concatenate([block, lax.ppermute(block, 'tx', SWAP)])  65.4 us
    all_gather x1, waiting for transfers between devices, per_device(): attn_full = lax.all_gather(attn_pack, 'dp', axis=0, tiled=True)  21.4 us
    unnamed x262, local copies, waits for them, and re-layouts  19.4 us
    dot_general x4, matrix products, attend_backward(): jnp.einsum('qbhe,kbhe->bhqk', grad_block, values, preferred_element_type=...  18.8 us
    dot_general x4, matrix products, causal_scores(): jnp.einsum('qbhe,kbhe->bhqk', query_block, keys, preferred_element_type=j...  17.4 us
    dot_general x4, matrix products, attend_forward(): jnp.einsum('bhqk,kbhe->qbhe', weights, values, preferred_element_type=jnp...  15.8 us
  transfers between devices with their start and end apart: 36, of which 18 were waited for; matrix products, arithmetic and copies ran while one was open for 41% of the time, Pallas kernels for 0%

profile of v4, /device:TPU:0, one launch (start us, length us, event | category | flops | bytes accessed | tf_op | source)
XLA Modules:
  0.0 672.6 jit_solution(891029747867883550)
XLA Ops:
  18.1 12.6 %collective-permute-done = bf16[256,1,1024]{2,0,1:T(8,128)(2,1)S(1)} collective-permute-done((bf16[256,1,1024]{2,0,1:T(8,128)(2,1)S(1)}, bf16[256,1,1024]{2,0,1:T(8,128)(2,1)S(1)}, u32[]{:S(2)}, u32[]{:S(2)}) %collective-permute-start) | collective-permute-done | bytes 524320 | tf_op jit(solution)/shard_map/ppermute | solution.py:107
  32.7 8.4 %collective-permute-done.8 = bf16[256,1,1024]{2,0,1:T(8,128)(2,1)S(1)} collective-permute-done((bf16[256,1,1024]{2,0,1:T(8,128)(2,1)S(1)}, bf16[256,1,1024]{2,0,1:T(8,128)(2,1)S(1)}, u32[]{:S(2)}, u32[]{:S(2)}) %collective-permute-start.8) | collective-permute-done | bytes 524320 | tf_op jit(solution)/shard_map/ppermute | solution.py:107
  42.2 21.4 %all-gather.3.cloned.1.call-done = bf16[1024,1024]{0,1:T(8,128)(2,1)} async-done(((bf16[128,1024]{0,1:T(8,128)(2,1)}), bf16[1024,1024]{0,1:T(8,128)(2,1)}) %all-gather.3.cloned.1.call-update) | async-done | bytes 2097168 | tf_op jit(solution)/shard_map/all_gather | solution.py:249
  70.9 5.3 fusion.209
  79.7 4.9 fusion.210
  84.6 5.3 fusion.211
  100.0 5.8 fusion.119
  123.9 5.1 fusion.117
  142.5 19.1 %collective-permute-done.16 = bf16[256,2,1,1024]{3,0,2,1:T(8,128)(2,1)S(1)} collective-permute-done((bf16[256,2,1,1024]{3,0,2,1:T(8,128)(2,1)S(1)}, bf16[256,2,1,1024]{3,0,2,1:T(8,128)(2,1)S(1)}, u32[]{:S(2)}, u32[]{:S(2)}) %collective-permute-start.16) | collective-permute-done | bytes 1048608 | tf_op jit(solution)/shard_map/ppermute | solution.py:107
  163.3 20.8 %collective-permute-done.3 = f32[256,1,1024]{2,0,1:T(8,128)S(1)} collective-permute-done((f32[256,1,1024]{2,0,1:T(8,128)S(1)}, f32[256,1,1024]{2,0,1:T(8,128)S(1)}, u32[]{:S(2)}, u32[]{:S(2)}) %collective-permute-start.3) | collective-permute-done | bytes 1048608 | tf_op jit(solution)/shard_map/ppermute | solution.py:115
  184.0 22.0 %collective-permute-done.11 = f32[256,1,1024]{2,0,1:T(8,128)S(1)} collective-permute-done((f32[256,1,1024]{2,0,1:T(8,128)S(1)}, f32[256,1,1024]{2,0,1:T(8,128)S(1)}, u32[]{:S(2)}, u32[]{:S(2)}) %collective-permute-start.11) | collective-permute-done | bytes 1048608 | tf_op jit(solution)/shard_map/ppermute | solution.py:115
  231.8 12.5 %collective-permute-done.12 = bf16[256,1,1024]{2,0,1:T(8,128)(2,1)S(1)} collective-permute-done((bf16[256,1,1024]{2,0,1:T(8,128)(2,1)S(1)}, bf16[256,1,1024]{2,0,1:T(8,128)(2,1)S(1)}, u32[]{:S(2)}, u32[]{:S(2)}) %collective-permute-start.12) | collective-permute-done | bytes 524320 | tf_op jit(solution)/shard_map/ppermute | solution.py:107
  250.2 6.3 convert_reduce_fusion.1
  263.6 6.3 convert_reduce_fusion
  273.2 5.0 fusion.66
  278.4 5.6 fusion.64
  294.9 6.3 collective-permute-done.7
  301.1 22.4 %collective-permute-done.19 = f32[256,1,1024]{2,0,1:T(8,128)S(1)} collective-permute-done((f32[256,1,1024]{2,0,1:T(8,128)S(1)}, f32[256,1,1024]{2,0,1:T(8,128)S(1)}, u32[]{:S(2)}, u32[]{:S(2)}) %collective-permute-start.19) | collective-permute-done | bytes 1048608 | tf_op jit(solution)/shard_map/ppermute | solution.py:115
  323.5 22.5 %collective-permute-done.25 = f32[256,1,1024]{2,0,1:T(8,128)S(1)} collective-permute-done((f32[256,1,1024]{2,0,1:T(8,128)S(1)}, f32[256,1,1024]{2,0,1:T(8,128)S(1)}, u32[]{:S(2)}, u32[]{:S(2)}) %collective-permute-start.25) | collective-permute-done | bytes 1048608 | tf_op jit(solution)/shard_map/ppermute | solution.py:115
  349.3 7.0 %collective-permute-done.15 = bf16[256,1,1024]{2,0,1:T(8,128)(2,1)S(1)} collective-permute-done((bf16[256,1,1024]{2,0,1:T(8,128)(2,1)S(1)}, bf16[256,1,1024]{2,0,1:T(8,128)(2,1)S(1)}, u32[]{:S(2)}, u32[]{:S(2)}) %collective-permute-start.15) | collective-permute-done | bytes 524320 | tf_op jit(solution)/shard_map/ppermute | solution.py:115
  367.0 5.3 collective-permute-done.20
  372.4 5.7 fusion.152
  378.8 6.0 maximum_add_fusion
  384.9 7.6 %collective-permute-done.26 = bf16[256,1,1024]{2,0,1:T(8,128)(2,1)S(1)} collective-permute-done((bf16[256,1,1024]{2,0,1:T(8,128)(2,1)S(1)}, bf16[256,1,1024]{2,0,1:T(8,128)(2,1)S(1)}, u32[]{:S(2)}, u32[]{:S(2)}) %collective-permute-start.26) | collective-permute-done | bytes 524320 | tf_op jit(solution)/shard_map/ppermute | solution.py:107
  396.0 5.1 fusion.24
  408.6 6.9 %multiply_convert_fusion.3 = bf16[4,512,1024]{2,1,0:T(8,128)(2,1)S(1)} fusion(f32[4,512,1024]{2,1,0:T(8,128)} %get-tuple-element.158, f32[4,512,1024]{2,1,0:T(8,128)} %get-tuple-element.152, f32[4,512]{1,0:T(4,128)S(1)} %get-tuple-element.157, f32[4,512]{1,0:T(4,128)S(1)} %log_add_fusion.3), kind=kLoop, calls=%fused_computation.10 | loop fusion | flops 8388608 | bytes 20987904 | tf_op jit(solution)/shard_map/convert_element_type | solution.py:79
  418.4 5.5 multiply_reduce_fusion.2
  449.1 5.9 multiply_reduce_fusion.1
  524.6 9.1 %collective-permute-done.23 = f32[256,1,1024]{2,0,1:T(8,128)} collective-permute-done((f32[256,1,1024]{2,0,1:T(8,128)}, f32[256,1,1024]{2,0,1:T(8,128)}, u32[]{:S(2)}, u32[]{:S(2)}) %collective-permute-start.23) | collective-permute-done | bytes 1048608 | tf_op jit(solution)/shard_map/ppermute | solution.py:115
  533.7 21.7 %collective-permute-done.29 = f32[256,1,1024]{2,0,1:T(8,128)} collective-permute-done((f32[256,1,1024]{2,0,1:T(8,128)}, f32[256,1,1024]{2,0,1:T(8,128)}, u32[]{:S(2)}, u32[]{:S(2)}) %collective-permute-start.29) | collective-permute-done | bytes 1048608 | tf_op jit(solution)/shard_map/ppermute | solution.py:115
  564.1 5.0 pad_maximum_fusion
  578.2 80.4 %reduce-scatter.7.cloned.1.call-done = f32[136,1024]{1,0:T(8,128)} async-done(((f32[1088,1024]{1,0:T(8,128)}), f32[136,1024]{1,0:T(8,128)}) %reduce-scatter.7.cloned.1.call-update) | async-done | bytes 557072
  (495 shorter events, 267.9 us)
Async XLA Ops:
  7.2 56.4 %all-gather.3.cloned.1.call-start = ((), (), s32[]{:S(2)}) async-start(), calls=%async_computation.2 | async-start | bytes 2359296 | tf_op jit(solution)/shard_map/all_gather | solution.py:249
  10.0 235.3 %all-gather.5.cloned.1.call-start = ((), (), s32[]{:S(2)}) async-start(), calls=%async_computation.3 | async-start | bytes 4718592 | tf_op jit(solution)/shard_map/all_gather | solution.py:250
  14.9 15.8 %collective-permute-start = (bf16[256,1,1024]{2,0,1:T(8,128)(2,1)S(1)}, bf16[256,1,1024]{2,0,1:T(8,128)(2,1)S(1)}, u32[]{:S(2)}, u32[]{:S(2)}) collective-permute-start(bf16[256,1,1024]{2,0,1:T(8,128)(2,1)S(1)} %get-tuple-element.106), channel_id=1, source_target_pairs={{0,2},{2,0},{1,3},{3,1},{4,6},{6,4},{5,7},{7,5},{8,10},{10,8},{9,1... | collective-permute-start | bytes 1572872 | tf_op jit(solution)/shard_map/ppermute | solution.py:107
  17.9 23.2 %collective-permute-start.8 = (bf16[256,1,1024]{2,0,1:T(8,128)(2,1)S(1)}, bf16[256,1,1024]{2,0,1:T(8,128)(2,1)S(1)}, u32[]{:S(2)}, u32[]{:S(2)}) collective-permute-start(bf16[256,1,1024]{2,0,1:T(8,128)(2,1)S(1)} %get-tuple-element.107), channel_id=1, source_target_pairs={{0,2},{2,0},{1,3},{3,1},{4,6},{6,4},{5,7},{7,5},{8,10},{10,8},{9,1... | collective-permute-start | bytes 1572872 | tf_op jit(solution)/shard_map/ppermute | solution.py:107
  30.8 34.4 %collective-permute-start.1 = (bf16[512,1,1024]{2,0,1:T(8,128)(2,1)S(1)}, bf16[512,1,1024]{2,0,1:T(8,128)(2,1)}, u32[]{:S(2)}, u32[]{:S(2)}) collective-permute-start(bf16[512,1,1024]{2,0,1:T(8,128)(2,1)S(1)} %pad_maximum_fusion.8), channel_id=1, source_target_pairs={{0,1},{1,0},{2,3},{3,2},{4,5},{5,4},{6,7},{7,6},{8,9},{9,8},{10,11... | collective-permute-start | bytes 3145736 | tf_op jit(solution)/shard_map/ppermute | solution.py:108
  42.2 34.1 %collective-permute-start.9 = (bf16[512,1,1024]{2,0,1:T(8,128)(2,1)}, bf16[512,1,1024]{2,0,1:T(8,128)(2,1)}, u32[]{:S(2)}, u32[]{:S(2)}) collective-permute-start(bf16[512,1,1024]{2,0,1:T(8,128)(2,1)} %pad_maximum_fusion.10), channel_id=1, source_target_pairs={{0,1},{1,0},{2,3},{3,2},{4,5},{5,4},{6,7},{7,6},{8,9},{9,8},{10,11... | collective-permute-start | bytes 3145736 | tf_op jit(solution)/shard_map/ppermute | solution.py:108
  112.3 24.7 %collective-permute-start.2 = (f32[512,1,1024]{2,0,1:T(8,128)}, f32[512,1,1024]{2,0,1:T(8,128)}, u32[]{:S(2)}, u32[]{:S(2)}) collective-permute-start(f32[512,1,1024]{2,0,1:T(8,128)} %slice_bitcast_fusion.14), channel_id=1, source_target_pairs={{0,1},{1,0},{2,3},{3,2},{4,5},{5,4},{6,7},{7,6},{8,9},{9,8},{10,11... | collective-permute-start | bytes 6291464 | tf_op jit(solution)/shard_map/ppermute | solution.py:113
  135.4 439.6 %reduce-scatter.5.cloned.1.call-start = ((), (), s32[]{:S(2)}) async-start(), calls=%async_computation.4 | async-start | bytes 9437184 | tf_op jit(solution)/shard_map/reduce_scatter | solution.py:279
  135.5 26.1 %collective-permute-start.16 = (bf16[256,2,1,1024]{3,0,2,1:T(8,128)(2,1)S(1)}, bf16[256,2,1,1024]{3,0,2,1:T(8,128)(2,1)S(1)}, u32[]{:S(2)}, u32[]{:S(2)}) collective-permute-start(bf16[256,2,1,1024]{3,0,2,1:T(8,128)(2,1)S(1)} %bitcast.446), channel_id=1, source_target_pairs={{0,2},{2,0},{1,3},{3,1},{4,6},{6,4},{5,7},{7,5},{8,10},{10,8},{9,1... | collective-permute-start | bytes 3145736 | tf_op jit(solution)/shard_map/ppermute | solution.py:107
  139.8 44.2 %collective-permute-start.3 = (f32[256,1,1024]{2,0,1:T(8,128)S(1)}, f32[256,1,1024]{2,0,1:T(8,128)S(1)}, u32[]{:S(2)}, u32[]{:S(2)}) collective-permute-start(f32[256,1,1024]{2,0,1:T(8,128)S(1)} %slice.408), channel_id=1, source_target_pairs={{0,2},{2,0},{1,3},{3,1},{4,6},{6,4},{5,7},{7,5},{8,10},{10,8},{9,1... | collective-permute-start | bytes 3145736 | tf_op jit(solution)/shard_map/ppermute | solution.py:115
  141.3 64.8 %collective-permute-start.11 = (f32[256,1,1024]{2,0,1:T(8,128)S(1)}, f32[256,1,1024]{2,0,1:T(8,128)S(1)}, u32[]{:S(2)}, u32[]{:S(2)}) collective-permute-start(f32[256,1,1024]{2,0,1:T(8,128)S(1)} %slice.422), channel_id=1, source_target_pairs={{0,2},{2,0},{1,3},{3,1},{4,6},{6,4},{5,7},{7,5},{8,10},{10,8},{9,1... | collective-permute-start | bytes 3145736 | tf_op jit(solution)/shard_map/ppermute | solution.py:115
  163.3 63.0 %collective-permute-start.17 = (bf16[512,2,1,1024]{3,0,2,1:T(8,128)(2,1)}, bf16[512,2,1,1024]{3,0,2,1:T(8,128)(2,1)}, u32[]{:S(2)}, u32[]{:S(2)}) collective-permute-start(bf16[512,2,1,1024]{3,0,2,1:T(8,128)(2,1)} %pad_maximum_fusion.3), channel_id=1, source_target_pairs={{0,1},{1,0},{2,3},{3,2},{4,5},{5,4},{6,7},{7,6},{8,9},{9,8},{10,11... | collective-permute-start | bytes 6291464 | tf_op jit(solution)/shard_map/ppermute | solution.py:108
  208.5 15.6 %collective-permute-start.4 = (bf16[256,1,1024]{2,0,1:T(8,128)(2,1)}, bf16[256,1,1024]{2,0,1:T(8,128)(2,1)}, u32[]{:S(2)}, u32[]{:S(2)}) collective-permute-start(bf16[256,1,1024]{2,0,1:T(8,128)(2,1)} %get-tuple-element.130), channel_id=1, source_target_pairs={{0,2},{2,0},{1,3},{3,1},{4,6},{6,4},{5,7},{7,5},{8,10},{10,8},{9,1... | collective-permute-start | bytes 1572872 | tf_op jit(solution)/shard_map/ppermute | solution.py:107
  226.3 19.1 %collective-permute-start.5 = (bf16[512,1,1024]{2,0,1:T(8,128)(2,1)}, bf16[512,1,1024]{2,0,1:T(8,128)(2,1)}, u32[]{:S(2)}, u32[]{:S(2)}) collective-permute-start(bf16[512,1,1024]{2,0,1:T(8,128)(2,1)} %pad_maximum_fusion.9), channel_id=1, source_target_pairs={{0,1},{1,0},{2,3},{3,2},{4,5},{5,4},{6,7},{7,6},{8,9},{9,8},{10,11... | collective-permute-start | bytes 3145736 | tf_op jit(solution)/shard_map/ppermute | solution.py:108
  229.9 14.3 %collective-permute-start.12 = (bf16[256,1,1024]{2,0,1:T(8,128)(2,1)S(1)}, bf16[256,1,1024]{2,0,1:T(8,128)(2,1)S(1)}, u32[]{:S(2)}, u32[]{:S(2)}) collective-permute-start(bf16[256,1,1024]{2,0,1:T(8,128)(2,1)S(1)} %copy-done.49), channel_id=1, source_target_pairs={{0,2},{2,0},{1,3},{3,1},{4,6},{6,4},{5,7},{7,5},{8,10},{10,8},{9,1... | collective-permute-start | bytes 1572872 | tf_op jit(solution)/shard_map/ppermute | solution.py:107
  245.4 14.3 %collective-permute-start.13 = (bf16[512,1,1024]{2,0,1:T(8,128)(2,1)}, bf16[512,1,1024]{2,0,1:T(8,128)(2,1)}, u32[]{:S(2)}, u32[]{:S(2)}) collective-permute-start(bf16[512,1,1024]{2,0,1:T(8,128)(2,1)} %pad_maximum_fusion.11), channel_id=1, source_target_pairs={{0,1},{1,0},{2,3},{3,2},{4,5},{5,4},{6,7},{7,6},{8,9},{9,8},{10,11... | collective-permute-start | bytes 3145736 | tf_op jit(solution)/shard_map/ppermute | solution.py:108
  259.1 27.5 %collective-permute-start.18 = (f32[512,1,1024]{2,0,1:T(8,128)S(1)}, f32[512,1,1024]{2,0,1:T(8,128)S(1)}, u32[]{:S(2)}, u32[]{:S(2)}) collective-permute-start(f32[512,1,1024]{2,0,1:T(8,128)S(1)} %slice_bitcast_fusion.7), channel_id=1, source_target_pairs={{0,1},{1,0},{2,3},{3,2},{4,5},{5,4},{6,7},{7,6},{8,9},{9,8},{10,11... | collective-permute-start | bytes 6291464 | tf_op jit(solution)/shard_map/ppermute | solution.py:113
  272.6 16.1 %collective-permute-start.24 = (f32[512,1,1024]{2,0,1:T(8,128)S(1)}, f32[512,1,1024]{2,0,1:T(8,128)S(1)}, u32[]{:S(2)}, u32[]{:S(2)}) collective-permute-start(f32[512,1,1024]{2,0,1:T(8,128)S(1)} %slice_bitcast_fusion.2), channel_id=1, source_target_pairs={{0,1},{1,0},{2,3},{3,2},{4,5},{5,4},{6,7},{7,6},{8,9},{9,8},{10,11... | collective-permute-start | bytes 6291464 | tf_op jit(solution)/shard_map/ppermute | solution.py:113
  284.2 8.6 %collective-permute-start.14 = (bf16[512,1,1024]{2,0,1:T(8,128)(2,1)S(1)}, bf16[512,1,1024]{2,0,1:T(8,128)(2,1)S(1)}, u32[]{:S(2)}, u32[]{:S(2)}) collective-permute-start(bf16[512,1,1024]{2,0,1:T(8,128)(2,1)S(1)} %fusion.143), channel_id=1, source_target_pairs={{0,1},{1,0},{2,3},{3,2},{4,5},{5,4},{6,7},{7,6},{8,9},{9,8},{10,11... | collective-permute-start | bytes 3145736 | tf_op jit(solution)/shard_map/ppermute | solution.py:113
  286.0 15.1 %collective-permute-start.7 = (bf16[256,1,1024]{2,0,1:T(8,128)(2,1)}, bf16[256,1,1024]{2,0,1:T(8,128)(2,1)}, u32[]{:S(2)}, u32[]{:S(2)}) collective-permute-start(bf16[256,1,1024]{2,0,1:T(8,128)(2,1)} %slice.618), channel_id=1, source_target_pairs={{0,2},{2,0},{1,3},{3,1},{4,6},{6,4},{5,7},{7,5},{8,10},{10,8},{9,1... | collective-permute-start | bytes 1572872 | tf_op jit(solution)/shard_map/ppermute | solution.py:115
  287.1 36.4 %collective-permute-start.19 = (f32[256,1,1024]{2,0,1:T(8,128)S(1)}, f32[256,1,1024]{2,0,1:T(8,128)S(1)}, u32[]{:S(2)}, u32[]{:S(2)}) collective-permute-start(f32[256,1,1024]{2,0,1:T(8,128)S(1)} %slice.431), channel_id=1, source_target_pairs={{0,2},{2,0},{1,3},{3,1},{4,6},{6,4},{5,7},{7,5},{8,10},{10,8},{9,1... | collective-permute-start | bytes 3145736 | tf_op jit(solution)/shard_map/ppermute | solution.py:115
  289.2 56.8 %collective-permute-start.25 = (f32[256,1,1024]{2,0,1:T(8,128)S(1)}, f32[256,1,1024]{2,0,1:T(8,128)S(1)}, u32[]{:S(2)}, u32[]{:S(2)}) collective-permute-start(f32[256,1,1024]{2,0,1:T(8,128)S(1)} %slice.442), channel_id=1, source_target_pairs={{0,2},{2,0},{1,3},{3,1},{4,6},{6,4},{5,7},{7,5},{8,10},{10,8},{9,1... | collective-permute-start | bytes 3145736 | tf_op jit(solution)/shard_map/ppermute | solution.py:115
  293.3 62.9 %collective-permute-start.15 = (bf16[256,1,1024]{2,0,1:T(8,128)(2,1)S(1)}, bf16[256,1,1024]{2,0,1:T(8,128)(2,1)S(1)}, u32[]{:S(2)}, u32[]{:S(2)}) collective-permute-start(bf16[256,1,1024]{2,0,1:T(8,128)(2,1)S(1)} %slice.617), channel_id=1, source_target_pairs={{0,2},{2,0},{1,3},{3,1},{4,6},{6,4},{5,7},{7,5},{8,10},{10,8},{9,1... | collective-permute-start | bytes 1572872 | tf_op jit(solution)/shard_map/ppermute | solution.py:115
  359.2 13.1 %collective-permute-start.20 = (bf16[256,1,1024]{2,0,1:T(8,128)(2,1)S(1)}, bf16[256,1,1024]{2,0,1:T(8,128)(2,1)S(1)}, u32[]{:S(2)}, u32[]{:S(2)}) collective-permute-start(bf16[256,1,1024]{2,0,1:T(8,128)(2,1)S(1)} %convert_element_type.337), channel_id=1, source_target_pairs={{0,2},{2,0},{1,3},{3,1},{4,6},{6,4},{5,7},{7,5},{8,10},{10,8},{9,1... | collective-permute-start | bytes 1572872 | tf_op jit(solution)/shard_map/ppermute | solution.py:107
  372.3 21.3 %collective-permute-start.21 = (bf16[512,1,1024]{2,0,1:T(8,128)(2,1)S(1)}, bf16[512,1,1024]{2,0,1:T(8,128)(2,1)}, u32[]{:S(2)}, u32[]{:S(2)}) collective-permute-start(bf16[512,1,1024]{2,0,1:T(8,128)(2,1)S(1)} %pad_maximum_fusion.13), channel_id=1, source_target_pairs={{0,1},{1,0},{2,3},{3,2},{4,5},{5,4},{6,7},{7,6},{8,9},{9,8},{10,11... | collective-permute-start | bytes 3145736 | tf_op jit(solution)/shard_map/ppermute | solution.py:108
  378.1 14.4 %collective-permute-start.26 = (bf16[256,1,1024]{2,0,1:T(8,128)(2,1)S(1)}, bf16[256,1,1024]{2,0,1:T(8,128)(2,1)S(1)}, u32[]{:S(2)}, u32[]{:S(2)}) collective-permute-start(bf16[256,1,1024]{2,0,1:T(8,128)(2,1)S(1)} %convert_element_type.347), channel_id=1, source_target_pairs={{0,2},{2,0},{1,3},{3,1},{4,6},{6,4},{5,7},{7,5},{8,10},{10,8},{9,1... | collective-permute-start | bytes 1572872 | tf_op jit(solution)/shard_map/ppermute | solution.py:107
  384.8 273.8 %reduce-scatter.7.cloned.1.call-start = ((), (), s32[]{:S(2)}) async-start(), calls=%async_computation.5 | async-start | bytes 5013504
  393.6 46.6 %collective-permute-start.27 = (bf16[512,1,1024]{2,0,1:T(8,128)(2,1)}, bf16[512,1,1024]{2,0,1:T(8,128)(2,1)}, u32[]{:S(2)}, u32[]{:S(2)}) collective-permute-start(bf16[512,1,1024]{2,0,1:T(8,128)(2,1)} %pad_maximum_fusion.14), channel_id=1, source_target_pairs={{0,1},{1,0},{2,3},{3,2},{4,5},{5,4},{6,7},{7,6},{8,9},{9,8},{10,11... | collective-permute-start | bytes 3145736 | tf_op jit(solution)/shard_map/ppermute | solution.py:108
  439.5 64.7 %collective-permute-start.22 = (f32[512,1,1024]{2,0,1:T(8,128)}, f32[512,1,1024]{2,0,1:T(8,128)}, u32[]{:S(2)}, u32[]{:S(2)}) collective-permute-start(f32[512,1,1024]{2,0,1:T(8,128)} %slice_bitcast_fusion.5), channel_id=1, source_target_pairs={{0,1},{1,0},{2,3},{3,2},{4,5},{5,4},{6,7},{7,6},{8,9},{9,8},{10,11... | collective-permute-start | bytes 6291464 | tf_op jit(solution)/shard_map/ppermute | solution.py:113
  479.9 28.2 %collective-permute-start.28 = (f32[512,1,1024]{2,0,1:T(8,128)}, f32[512,1,1024]{2,0,1:T(8,128)}, u32[]{:S(2)}, u32[]{:S(2)}) collective-permute-start(f32[512,1,1024]{2,0,1:T(8,128)} %slice_bitcast_fusion), channel_id=1, source_target_pairs={{0,1},{1,0},{2,3},{3,2},{4,5},{5,4},{6,7},{7,6},{8,9},{9,8},{10,11... | collective-permute-start | bytes 6291464 | tf_op jit(solution)/shard_map/ppermute | solution.py:113
  507.3 26.3 %collective-permute-start.23 = (f32[256,1,1024]{2,0,1:T(8,128)}, f32[256,1,1024]{2,0,1:T(8,128)}, u32[]{:S(2)}, u32[]{:S(2)}) collective-permute-start(f32[256,1,1024]{2,0,1:T(8,128)} %slice.437), channel_id=1, source_target_pairs={{0,2},{2,0},{1,3},{3,1},{4,6},{6,4},{5,7},{7,5},{8,10},{10,8},{9,1... | collective-permute-start | bytes 3145736 | tf_op jit(solution)/shard_map/ppermute | solution.py:115
  512.5 42.9 %collective-permute-start.29 = (f32[256,1,1024]{2,0,1:T(8,128)}, f32[256,1,1024]{2,0,1:T(8,128)}, u32[]{:S(2)}, u32[]{:S(2)}) collective-permute-start(f32[256,1,1024]{2,0,1:T(8,128)} %slice.448), channel_id=1, source_target_pairs={{0,2},{2,0},{1,3},{3,1},{4,6},{6,4},{5,7},{7,5},{8,10},{10,8},{9,1... | collective-permute-start | bytes 3145736 | tf_op jit(solution)/shard_map/ppermute | solution.py:115
  (123 other events, 1496.6 us)
Sparse Core Ops, SparseCore 0:
  10.6 52.9 all-gather.2
  135.5 71.0 all-gather.4
  384.9 146.0 reduce-scatter.4
  569.3 89.2 reduce-scatter.6

commit v5 on v4

--- a/solution.py
+++ b/solution.py
@@ -150,7 +150,7 @@
     mixed = attended.astype(jnp.bfloat16).reshape(length, batch, heads_local * HEAD_DIM)
     attn_branch = tensor_scatter(
         jnp.einsum("lbi,oi->lbo", mixed, out_full, preferred_element_type=jnp.float32),
-        jnp.float32,
+        jnp.bfloat16,
     )
     middle = resid_in + attn_branch + out_bias
     normed2, inverse2 = norm_parts(middle)
@@ -180,7 +180,7 @@
     )
     grad_h2 = tensor_scatter(
         jnp.einsum("lbf,df->lbd", grad_pre, fc_full, preferred_element_type=jnp.float32),
-        jnp.float32,
+        jnp.bfloat16,
     )
     grad_gain2 = jnp.sum(grad_h2 * normed2, axis=(0, 1))
     grad_shift2 = jnp.sum(grad_h2, axis=(0, 1))
@@ -207,7 +207,7 @@
     )
     grad_h1 = tensor_scatter(
         jnp.einsum("lbce,dce->lbd", grad_qkv, qkv_full, preferred_element_type=jnp.float32),
-        jnp.float32,
+        jnp.bfloat16,
     )
     grad_gain1 = jnp.sum(grad_h1 * normed1, axis=(0, 1))
     grad_shift1 = jnp.sum(grad_h1, axis=(0, 1))

time: 683 us -> 771 us (1.13)
  waiting for transfers between devices: 303 us -> 426 us
  matrix products: 163 us -> 143 us
  local copies, waits for them, and re-layouts: 62.4 us -> 52.9 us
  other arithmetic: 107 us -> 98.5 us
    reduce_scatter x1, waiting for transfers between devices: 0.01 us -> 144 us  [per_device(): mlp_shard = lax.psum_scatter(mlp_acc, 'dp', scatter_dimension=0, tiled=True)]
    ppermute x8, waiting for transfers between devices: 132 us -> 80.2 us  [tensor_scatter(): got2 = lax.ppermute(chip[rows:].astype(send_dtype), 'tx', SWAP)]
    ppermute x7, waiting for transfers between devices: 65.4 us -> 88.5 us  [tensor_gather(): pair = jnp.concatenate([block, lax.ppermute(block, 'tx', SWAP)])]
    unnamed x5, waiting for transfers between devices: 80.4 us -> 65.6 us
    all_gather x1, waiting for transfers between devices: 21.4 us -> 32.7 us  [per_device(): attn_full = lax.all_gather(attn_pack, 'dp', axis=0, tiled=True)]
    convert_element_type x4, other arithmetic: 15 us -> 22.9 us  [attend_backward(): grad_scores = (probs * (grad_probs - inner)).astype(jnp.bfloat16)]
    unnamed x262 -> x234, local copies, waits for them, and re-layouts: 19.4 us -> 15.6 us
  transfers between devices with their start and end apart: 36 -> 36, of which waited for: 18 -> 28; matrix products, arithmetic and copies ran while one was open for 41% -> 16% of each run, Pallas kernels for 0% -> 0%
where the time goes in v5:
time: 771 us; the launch traced here: 765 us
  waiting for transfers between devices  426 us (55%)
  matrix products  143 us (19%)
  other arithmetic  98.5 us (13%)
  local copies, waits for them, and re-layouts  52.9 us (7%)
  starting transfers between devices  28 us (4%)
  between operations  16.1 us (2%)
    reduce_scatter x1, waiting for transfers between devices, per_device(): mlp_shard = lax.psum_scatter(mlp_acc, 'dp', scatter_dimension=0, tiled=True)  144 us
    ppermute x7, waiting for transfers between devices, tensor_gather(): pair = jnp.concatenate([block, lax.ppermute(block, 'tx', SWAP)])  88.5 us
    ppermute x8, waiting for transfers between devices, tensor_scatter(): got2 = lax.ppermute(chip[rows:].astype(send_dtype), 'tx', SWAP)  80.2 us
    unnamed x5, waiting for transfers between devices  65.6 us
    all_gather x1, waiting for transfers between devices, per_device(): attn_full = lax.all_gather(attn_pack, 'dp', axis=0, tiled=True)  32.7 us
    convert_element_type x4, other arithmetic, attend_backward(): grad_scores = (probs * (grad_probs - inner)).astype(jnp.bfloat16)  22.9 us
    dot_general x4, matrix products, attend_backward(): jnp.einsum('qbhe,kbhe->bhqk', grad_block, values, preferred_element_type=...  20.7 us
    unnamed x234, local copies, waits for them, and re-layouts  15.6 us
  transfers between devices with their start and end apart: 36, of which 28 were waited for; matrix products, arithmetic and copies ran while one was open for 16% of the time, Pallas kernels for 0%

profile of v5, /device:TPU:0, one launch (start us, length us, event | category | flops | bytes accessed | tf_op | source)
XLA Modules:
  0.0 765.0 jit_solution(9238302915841662556)
XLA Ops:
  19.2 10.0 %collective-permute-done = bf16[256,1,1024]{2,0,1:T(8,128)(2,1)S(1)} collective-permute-done((bf16[256,1,1024]{2,0,1:T(8,128)(2,1)S(1)}, bf16[256,1,1024]{2,0,1:T(8,128)(2,1)S(1)}, u32[]{:S(2)}, u32[]{:S(2)}) %collective-permute-start) | collective-permute-done | bytes 524320 | tf_op jit(solution)/shard_map/ppermute | solution.py:107
  30.9 32.7 %all-gather.3.cloned.1.call-done = bf16[1024,1024]{0,1:T(8,128)(2,1)} async-done(((bf16[128,1024]{0,1:T(8,128)(2,1)}), bf16[1024,1024]{0,1:T(8,128)(2,1)}) %all-gather.3.cloned.1.call-update) | async-done | bytes 2097168 | tf_op jit(solution)/shard_map/all_gather | solution.py:249
  76.2 4.9 fusion.219
  81.2 4.5 fusion
  96.4 21.5 %collective-permute-done.16 = bf16[256,2,1,1024]{3,0,2,1:T(8,128)(2,1)S(1)} collective-permute-done((bf16[256,2,1,1024]{3,0,2,1:T(8,128)(2,1)S(1)}, bf16[256,2,1,1024]{3,0,2,1:T(8,128)(2,1)S(1)}, u32[]{:S(2)}, u32[]{:S(2)}) %collective-permute-start.16) | collective-permute-done | bytes 1048608 | tf_op jit(solution)/shard_map/ppermute | solution.py:107
  118.2 10.3 %collective-permute-done.3 = bf16[256,1,1024]{2,0,1:T(8,128)(2,1)S(1)} collective-permute-done((bf16[256,1,1024]{2,0,1:T(8,128)(2,1)S(1)}, bf16[256,1,1024]{2,0,1:T(8,128)(2,1)S(1)}, u32[]{:S(2)}, u32[]{:S(2)}) %collective-permute-start.3) | collective-permute-done | bytes 524320 | tf_op jit(solution)/shard_map/ppermute | solution.py:115
  131.0 12.0 %collective-permute-done.4 = bf16[256,1,1024]{2,0,1:T(8,128)(2,1)S(1)} collective-permute-done((bf16[256,1,1024]{2,0,1:T(8,128)(2,1)S(1)}, bf16[256,1,1024]{2,0,1:T(8,128)(2,1)S(1)}, u32[]{:S(2)}, u32[]{:S(2)}) %collective-permute-start.4) | collective-permute-done | bytes 524320 | tf_op jit(solution)/shard_map/ppermute | solution.py:107
  145.9 4.7 fusion.74
  150.6 6.7 convert_reduce_fusion.1
  167.9 11.0 %collective-permute-done.19 = bf16[256,1,1024]{2,0,1:T(8,128)(2,1)S(1)} collective-permute-done((bf16[256,1,1024]{2,0,1:T(8,128)(2,1)S(1)}, bf16[256,1,1024]{2,0,1:T(8,128)(2,1)S(1)}, u32[]{:S(2)}, u32[]{:S(2)}) %collective-permute-start.19) | collective-permute-done | bytes 524320 | tf_op jit(solution)/shard_map/ppermute | solution.py:115
  178.9 10.4 %collective-permute-done.7 = bf16[256,1,1024]{2,0,1:T(8,128)(2,1)S(1)} collective-permute-done((bf16[256,1,1024]{2,0,1:T(8,128)(2,1)S(1)}, bf16[256,1,1024]{2,0,1:T(8,128)(2,1)S(1)}, u32[]{:S(2)}, u32[]{:S(2)}) %collective-permute-start.7) | collective-permute-done | bytes 524320 | tf_op jit(solution)/shard_map/ppermute | solution.py:115
  193.9 11.6 %collective-permute-done.20 = bf16[256,1,1024]{2,0,1:T(8,128)(2,1)S(1)} collective-permute-done((bf16[256,1,1024]{2,0,1:T(8,128)(2,1)S(1)}, bf16[256,1,1024]{2,0,1:T(8,128)(2,1)S(1)}, u32[]{:S(2)}, u32[]{:S(2)}) %collective-permute-start.20) | collective-permute-done | bytes 524320 | tf_op jit(solution)/shard_map/ppermute | solution.py:107
  232.3 7.0 multiply_convert_fusion.2
  255.1 12.5 %collective-permute-done.23 = bf16[256,1,1024]{2,0,1:T(8,128)(2,1)S(1)} collective-permute-done((bf16[256,1,1024]{2,0,1:T(8,128)(2,1)S(1)}, bf16[256,1,1024]{2,0,1:T(8,128)(2,1)S(1)}, u32[]{:S(2)}, u32[]{:S(2)}) %collective-permute-start.23) | collective-permute-done | bytes 524320 | tf_op jit(solution)/shard_map/ppermute | solution.py:115
  271.3 11.6 %collective-permute-done.8 = bf16[256,1,1024]{2,0,1:T(8,128)(2,1)S(1)} collective-permute-done((bf16[256,1,1024]{2,0,1:T(8,128)(2,1)S(1)}, bf16[256,1,1024]{2,0,1:T(8,128)(2,1)S(1)}, u32[]{:S(2)}, u32[]{:S(2)}) %collective-permute-start.8) | collective-permute-done | bytes 524320 | tf_op jit(solution)/shard_map/ppermute | solution.py:107
  289.5 5.4 fusion.221
  315.0 12.5 %collective-permute-done.11 = bf16[256,1,1024]{2,0,1:T(8,128)(2,1)S(1)} collective-permute-done((bf16[256,1,1024]{2,0,1:T(8,128)(2,1)S(1)}, bf16[256,1,1024]{2,0,1:T(8,128)(2,1)S(1)}, u32[]{:S(2)}, u32[]{:S(2)}) %collective-permute-start.11) | collective-permute-done | bytes 524320 | tf_op jit(solution)/shard_map/ppermute | solution.py:115
  329.9 11.6 %collective-permute-done.12 = bf16[256,1,1024]{2,0,1:T(8,128)(2,1)S(1)} collective-permute-done((bf16[256,1,1024]{2,0,1:T(8,128)(2,1)S(1)}, bf16[256,1,1024]{2,0,1:T(8,128)(2,1)S(1)}, u32[]{:S(2)}, u32[]{:S(2)}) %collective-permute-start.12) | collective-permute-done | bytes 524320 | tf_op jit(solution)/shard_map/ppermute | solution.py:107
  356.5 4.7 fusion.72
  361.3 6.1 convert_reduce_fusion
  390.7 5.2 collective-permute-done.25
  397.5 9.0 %collective-permute-done.15 = bf16[256,1,1024]{2,0,1:T(8,128)(2,1)S(1)} collective-permute-done((bf16[256,1,1024]{2,0,1:T(8,128)(2,1)S(1)}, bf16[256,1,1024]{2,0,1:T(8,128)(2,1)S(1)}, u32[]{:S(2)}, u32[]{:S(2)}) %collective-permute-start.15) | collective-permute-done | bytes 524320 | tf_op jit(solution)/shard_map/ppermute | solution.py:115
  413.3 10.3 %collective-permute-done.26 = bf16[256,1,1024]{2,0,1:T(8,128)(2,1)S(1)} collective-permute-done((bf16[256,1,1024]{2,0,1:T(8,128)(2,1)S(1)}, bf16[256,1,1024]{2,0,1:T(8,128)(2,1)S(1)}, u32[]{:S(2)}, u32[]{:S(2)}) %collective-permute-start.26) | collective-permute-done | bytes 524320 | tf_op jit(solution)/shard_map/ppermute | solution.py:107
  430.3 7.7 %multiply_reduce_fusion.1 = (f32[4,512]{1,0:T(4,128)S(1)}, f32[4,512,1024]{2,1,0:T(8,128)}) fusion(f32[4,512,1024]{2,1,0:T(8,128)} %get-tuple-element.140, f32[4,512]{1,0:T(4,128)S(1)} %log_add_fusion.1, bf16[512,4,64]{0,2,1:T(8,128)(2,1)S(1)} %bitcast.479, bf16[1024,1,3,4,64]{0,4,3,2,1:T(8,128)(2,1)S(1)} %bitcast.453), kind=kOutput, calls=%fused_computation.5 | convolution fusion | flops 274724864 | bytes 17580032 | tf_op jit(solution)/shard_map/qbhe,kbhe->bhqk/dot_general | solution.py:75
  438.0 4.5 multiply_convert_fusion.1
  453.5 6.9 multiply_convert_fusion
  492.5 9.4 %collective-permute-done.29 = bf16[256,1,1024]{2,0,1:T(8,128)(2,1)S(1)} collective-permute-done((bf16[256,1,1024]{2,0,1:T(8,128)(2,1)S(1)}, bf16[256,1,1024]{2,0,1:T(8,128)(2,1)S(1)}, u32[]{:S(2)}, u32[]{:S(2)}) %collective-permute-start.29) | collective-permute-done | bytes 524320 | tf_op jit(solution)/shard_map/ppermute | solution.py:115
  508.5 5.0 pad_maximum_fusion
  513.6 4.9 fusion.160
  528.5 4.7 maximum_add_fusion
  538.5 65.5 %reduce-scatter.7.cloned.1.call-done = f32[136,1024]{1,0:T(8,128)} async-done(((f32[1088,1024]{1,0:T(8,128)}), f32[136,1024]{1,0:T(8,128)}) %reduce-scatter.7.cloned.1.call-update) | async-done | bytes 557072
  611.3 143.7 %reduce-scatter.5.cloned.1.call-done = f32[128,2048]{0,1:T(8,128)} async-done(((f32[1024,2048]{0,1:T(8,128)}), f32[128,2048]{0,1:T(8,128)}) %reduce-scatter.5.cloned.1.call-update) | async-done | bytes 1048592 | tf_op jit(solution)/shard_map/reduce_scatter | solution.py:279
  (471 shorter events, 260.6 us)
Async XLA Ops:
  7.2 56.4 %all-gather.3.cloned.1.call-start = ((), (), s32[]{:S(2)}) async-start(), calls=%async_computation.2 | async-start | bytes 2359296 | tf_op jit(solution)/shard_map/all_gather | solution.py:249
  10.0 135.8 %all-gather.5.cloned.1.call-start = ((), (), s32[]{:S(2)}) async-start(), calls=%async_computation.3 | async-start | bytes 4718592 | tf_op jit(solution)/shard_map/all_gather | solution.py:250
  14.2 15.0 %collective-permute-start = (bf16[256,1,1024]{2,0,1:T(8,128)(2,1)S(1)}, bf16[256,1,1024]{2,0,1:T(8,128)(2,1)S(1)}, u32[]{:S(2)}, u32[]{:S(2)}) collective-permute-start(bf16[256,1,1024]{2,0,1:T(8,128)(2,1)S(1)} %fusion.130), channel_id=1, source_target_pairs={{0,2},{2,0},{1,3},{3,1},{4,6},{6,4},{5,7},{7,5},{8,10},{10,8},{9,1... | collective-permute-start | bytes 1572872 | tf_op jit(solution)/shard_map/ppermute | solution.py:107
  19.1 584.8 %reduce-scatter.7.cloned.1.call-start = ((), (), s32[]{:S(2)}) async-start(), calls=%async_computation.5 | async-start | bytes 5013504
  29.3 35.9 %collective-permute-start.1 = (bf16[512,1,1024]{2,0,1:T(8,128)(2,1)S(1)}, bf16[512,1,1024]{2,0,1:T(8,128)(2,1)}, u32[]{:S(2)}, u32[]{:S(2)}) collective-permute-start(bf16[512,1,1024]{2,0,1:T(8,128)(2,1)S(1)} %pad_maximum_fusion.8), channel_id=1, source_target_pairs={{0,1},{1,0},{2,3},{3,2},{4,5},{5,4},{6,7},{7,6},{8,9},{9,8},{10,11... | collective-permute-start | bytes 3145736 | tf_op jit(solution)/shard_map/ppermute | solution.py:108
  91.7 2.7 collective-permute-start.2
  91.8 26.1 %collective-permute-start.16 = (bf16[256,2,1,1024]{3,0,2,1:T(8,128)(2,1)S(1)}, bf16[256,2,1,1024]{3,0,2,1:T(8,128)(2,1)S(1)}, u32[]{:S(2)}, u32[]{:S(2)}) collective-permute-start(bf16[256,2,1,1024]{3,0,2,1:T(8,128)(2,1)S(1)} %bitcast.442), channel_id=1, source_target_pairs={{0,2},{2,0},{1,3},{3,1},{4,6},{6,4},{5,7},{7,5},{8,10},{10,8},{9,1... | collective-permute-start | bytes 3145736 | tf_op jit(solution)/shard_map/ppermute | solution.py:107
  94.8 33.7 %collective-permute-start.3 = (bf16[256,1,1024]{2,0,1:T(8,128)(2,1)S(1)}, bf16[256,1,1024]{2,0,1:T(8,128)(2,1)S(1)}, u32[]{:S(2)}, u32[]{:S(2)}) collective-permute-start(bf16[256,1,1024]{2,0,1:T(8,128)(2,1)S(1)} %slice.676), channel_id=1, source_target_pairs={{0,2},{2,0},{1,3},{3,1},{4,6},{6,4},{5,7},{7,5},{8,10},{10,8},{9,1... | collective-permute-start | bytes 1572872 | tf_op jit(solution)/shard_map/ppermute | solution.py:115
  118.1 25.0 %collective-permute-start.17 = (bf16[512,2,1,1024]{3,0,2,1:T(8,128)(2,1)S(1)}, bf16[512,2,1,1024]{3,0,2,1:T(8,128)(2,1)S(1)}, u32[]{:S(2)}, u32[]{:S(2)}) collective-permute-start(bf16[512,2,1,1024]{3,0,2,1:T(8,128)(2,1)S(1)} %pad_maximum_fusion.3), channel_id=1, source_target_pairs={{0,1},{1,0},{2,3},{3,2},{4,5},{5,4},{6,7},{7,6},{8,9},{9,8},{10,11... | collective-permute-start | bytes 6291464 | tf_op jit(solution)/shard_map/ppermute | solution.py:108
  129.4 13.5 %collective-permute-start.4 = (bf16[256,1,1024]{2,0,1:T(8,128)(2,1)S(1)}, bf16[256,1,1024]{2,0,1:T(8,128)(2,1)S(1)}, u32[]{:S(2)}, u32[]{:S(2)}) collective-permute-start(bf16[256,1,1024]{2,0,1:T(8,128)(2,1)S(1)} %add_convert_fusion.3), channel_id=1, source_target_pairs={{0,2},{2,0},{1,3},{3,1},{4,6},{6,4},{5,7},{7,5},{8,10},{10,8},{9,1... | collective-permute-start | bytes 1572872 | tf_op jit(solution)/shard_map/ppermute | solution.py:107
  143.0 2.9 collective-permute-start.5
  159.9 3.6 collective-permute-start.18
  163.1 2.7 collective-permute-start.6
  164.0 14.9 %collective-permute-start.19 = (bf16[256,1,1024]{2,0,1:T(8,128)(2,1)S(1)}, bf16[256,1,1024]{2,0,1:T(8,128)(2,1)S(1)}, u32[]{:S(2)}, u32[]{:S(2)}) collective-permute-start(bf16[256,1,1024]{2,0,1:T(8,128)(2,1)S(1)} %slice.672), channel_id=1, source_target_pairs={{0,2},{2,0},{1,3},{3,1},{4,6},{6,4},{5,7},{7,5},{8,10},{10,8},{9,1... | collective-permute-start | bytes 1572872 | tf_op jit(solution)/shard_map/ppermute | solution.py:115
  166.3 23.0 %collective-permute-start.7 = (bf16[256,1,1024]{2,0,1:T(8,128)(2,1)S(1)}, bf16[256,1,1024]{2,0,1:T(8,128)(2,1)S(1)}, u32[]{:S(2)}, u32[]{:S(2)}) collective-permute-start(bf16[256,1,1024]{2,0,1:T(8,128)(2,1)S(1)} %slice.675), channel_id=1, source_target_pairs={{0,2},{2,0},{1,3},{3,1},{4,6},{6,4},{5,7},{7,5},{8,10},{10,8},{9,1... | collective-permute-start | bytes 1572872 | tf_op jit(solution)/shard_map/ppermute | solution.py:115
  192.3 13.2 %collective-permute-start.20 = (bf16[256,1,1024]{2,0,1:T(8,128)(2,1)S(1)}, bf16[256,1,1024]{2,0,1:T(8,128)(2,1)S(1)}, u32[]{:S(2)}, u32[]{:S(2)}) collective-permute-start(bf16[256,1,1024]{2,0,1:T(8,128)(2,1)S(1)} %convert_element_type.412), channel_id=1, source_target_pairs={{0,2},{2,0},{1,3},{3,1},{4,6},{6,4},{5,7},{7,5},{8,10},{10,8},{9,1... | collective-permute-start | bytes 1572872 | tf_op jit(solution)/shard_map/ppermute | solution.py:107
  205.6 2.7 collective-permute-start.21
  253.5 14.0 %collective-permute-start.23 = (bf16[256,1,1024]{2,0,1:T(8,128)(2,1)S(1)}, bf16[256,1,1024]{2,0,1:T(8,128)(2,1)S(1)}, u32[]{:S(2)}, u32[]{:S(2)}) collective-permute-start(bf16[256,1,1024]{2,0,1:T(8,128)(2,1)S(1)} %slice.671), channel_id=1, source_target_pairs={{0,2},{2,0},{1,3},{3,1},{4,6},{6,4},{5,7},{7,5},{8,10},{10,8},{9,1... | collective-permute-start | bytes 1572872 | tf_op jit(solution)/shard_map/ppermute | solution.py:115
  269.8 13.1 %collective-permute-start.8 = (bf16[256,1,1024]{2,0,1:T(8,128)(2,1)S(1)}, bf16[256,1,1024]{2,0,1:T(8,128)(2,1)S(1)}, u32[]{:S(2)}, u32[]{:S(2)}) collective-permute-start(bf16[256,1,1024]{2,0,1:T(8,128)(2,1)S(1)} %get-tuple-element.100), channel_id=1, source_target_pairs={{0,2},{2,0},{1,3},{3,1},{4,6},{6,4},{5,7},{7,5},{8,10},{10,8},{9,1... | collective-permute-start | bytes 1572872 | tf_op jit(solution)/shard_map/ppermute | solution.py:107
  313.4 14.0 %collective-permute-start.11 = (bf16[256,1,1024]{2,0,1:T(8,128)(2,1)S(1)}, bf16[256,1,1024]{2,0,1:T(8,128)(2,1)S(1)}, u32[]{:S(2)}, u32[]{:S(2)}) collective-permute-start(bf16[256,1,1024]{2,0,1:T(8,128)(2,1)S(1)} %slice.674), channel_id=1, source_target_pairs={{0,2},{2,0},{1,3},{3,1},{4,6},{6,4},{5,7},{7,5},{8,10},{10,8},{9,1... | collective-permute-start | bytes 1572872 | tf_op jit(solution)/shard_map/ppermute | solution.py:115
  328.3 13.2 %collective-permute-start.12 = (bf16[256,1,1024]{2,0,1:T(8,128)(2,1)S(1)}, bf16[256,1,1024]{2,0,1:T(8,128)(2,1)S(1)}, u32[]{:S(2)}, u32[]{:S(2)}) collective-permute-start(bf16[256,1,1024]{2,0,1:T(8,128)(2,1)S(1)} %add_convert_fusion.2), channel_id=1, source_target_pairs={{0,2},{2,0},{1,3},{3,1},{4,6},{6,4},{5,7},{7,5},{8,10},{10,8},{9,1... | collective-permute-start | bytes 1572872 | tf_op jit(solution)/shard_map/ppermute | solution.py:107
  342.7 13.9 %collective-permute-start.13 = (bf16[512,1,1024]{2,0,1:T(8,128)(2,1)}, bf16[512,1,1024]{2,0,1:T(8,128)(2,1)}, u32[]{:S(2)}, u32[]{:S(2)}) collective-permute-start(bf16[512,1,1024]{2,0,1:T(8,128)(2,1)} %pad_maximum_fusion.11), channel_id=1, source_target_pairs={{0,1},{1,0},{2,3},{3,2},{4,5},{5,4},{6,7},{7,6},{8,9},{9,8},{10,11... | collective-permute-start | bytes 3145736 | tf_op jit(solution)/shard_map/ppermute | solution.py:108
  370.0 8.1 %collective-permute-start.24 = (bf16[512,1,1024]{2,0,1:T(8,128)(2,1)S(1)}, bf16[512,1,1024]{2,0,1:T(8,128)(2,1)S(1)}, u32[]{:S(2)}, u32[]{:S(2)}) collective-permute-start(bf16[512,1,1024]{2,0,1:T(8,128)(2,1)S(1)} %fusion.148), channel_id=1, source_target_pairs={{0,1},{1,0},{2,3},{3,2},{4,5},{5,4},{6,7},{7,6},{8,9},{9,8},{10,11... | collective-permute-start | bytes 3145736 | tf_op jit(solution)/shard_map/ppermute | solution.py:113
  374.7 13.0 %collective-permute-start.14 = (bf16[512,1,1024]{2,0,1:T(8,128)(2,1)}, bf16[512,1,1024]{2,0,1:T(8,128)(2,1)}, u32[]{:S(2)}, u32[]{:S(2)}) collective-permute-start(bf16[512,1,1024]{2,0,1:T(8,128)(2,1)} %fusion.145), channel_id=1, source_target_pairs={{0,1},{1,0},{2,3},{3,2},{4,5},{5,4},{6,7},{7,6},{8,9},{9,8},{10,11... | collective-permute-start | bytes 3145736 | tf_op jit(solution)/shard_map/ppermute | solution.py:113
  380.7 15.1 %collective-permute-start.25 = (bf16[256,1,1024]{2,0,1:T(8,128)(2,1)}, bf16[256,1,1024]{2,0,1:T(8,128)(2,1)}, u32[]{:S(2)}, u32[]{:S(2)}) collective-permute-start(bf16[256,1,1024]{2,0,1:T(8,128)(2,1)} %slice.670), channel_id=1, source_target_pairs={{0,2},{2,0},{1,3},{3,1},{4,6},{6,4},{5,7},{7,5},{8,10},{10,8},{9,1... | collective-permute-start | bytes 1572872 | tf_op jit(solution)/shard_map/ppermute | solution.py:115
  390.1 16.4 %collective-permute-start.15 = (bf16[256,1,1024]{2,0,1:T(8,128)(2,1)S(1)}, bf16[256,1,1024]{2,0,1:T(8,128)(2,1)S(1)}, u32[]{:S(2)}, u32[]{:S(2)}) collective-permute-start(bf16[256,1,1024]{2,0,1:T(8,128)(2,1)S(1)} %slice.673), channel_id=1, source_target_pairs={{0,2},{2,0},{1,3},{3,1},{4,6},{6,4},{5,7},{7,5},{8,10},{10,8},{9,1... | collective-permute-start | bytes 1572872 | tf_op jit(solution)/shard_map/ppermute | solution.py:115
  410.0 13.5 %collective-permute-start.26 = (bf16[256,1,1024]{2,0,1:T(8,128)(2,1)S(1)}, bf16[256,1,1024]{2,0,1:T(8,128)(2,1)S(1)}, u32[]{:S(2)}, u32[]{:S(2)}) collective-permute-start(bf16[256,1,1024]{2,0,1:T(8,128)(2,1)S(1)} %convert_element_type.428), channel_id=1, source_target_pairs={{0,2},{2,0},{1,3},{3,1},{4,6},{6,4},{5,7},{7,5},{8,10},{10,8},{9,1... | collective-permute-start | bytes 1572872 | tf_op jit(solution)/shard_map/ppermute | solution.py:107
  424.7 3.0 collective-permute-start.27
  471.7 14.4 %collective-permute-start.28 = (bf16[512,1,1024]{2,0,1:T(8,128)(2,1)}, bf16[512,1,1024]{2,0,1:T(8,128)(2,1)}, u32[]{:S(2)}, u32[]{:S(2)}) collective-permute-start(bf16[512,1,1024]{2,0,1:T(8,128)(2,1)} %fusion.149), channel_id=1, source_target_pairs={{0,1},{1,0},{2,3},{3,2},{4,5},{5,4},{6,7},{7,6},{8,9},{9,8},{10,11... | collective-permute-start | bytes 3145736 | tf_op jit(solution)/shard_map/ppermute | solution.py:113
  487.9 14.0 %collective-permute-start.29 = (bf16[256,1,1024]{2,0,1:T(8,128)(2,1)S(1)}, bf16[256,1,1024]{2,0,1:T(8,128)(2,1)S(1)}, u32[]{:S(2)}, u32[]{:S(2)}) collective-permute-start(bf16[256,1,1024]{2,0,1:T(8,128)(2,1)S(1)} %slice.669), channel_id=1, source_target_pairs={{0,2},{2,0},{1,3},{3,1},{4,6},{6,4},{5,7},{7,5},{8,10},{10,8},{9,1... | collective-permute-start | bytes 1572872 | tf_op jit(solution)/shard_map/ppermute | solution.py:115
  504.7 3.8 collective-permute-start.31
  513.6 241.4 %reduce-scatter.5.cloned.1.call-start = ((), (), s32[]{:S(2)}) async-start(), calls=%async_computation.4 | async-start | bytes 9437184 | tf_op jit(solution)/shard_map/reduce_scatter | solution.py:279
  (109 other events, 1062.2 us)
Sparse Core Ops, SparseCore 0:
  10.6 52.9 all-gather.2
  66.3 70.9 all-gather.4
  513.7 90.2 reduce-scatter.6
  607.5 147.4 reduce-scatter.4

commit v6 on v5

--- a/solution.py
+++ b/solution.py
@@ -2,6 +2,7 @@
 import jax.numpy as jnp
 from jax import lax
 from jax.sharding import PartitionSpec as P
+
 
 HEAD_DIM = 64
 
@@ -276,32 +277,27 @@
             attn_acc = attn_acc + attn_grads
             head_acc = head_acc + head_sums
             feature_acc = feature_acc + feature_sums
-    mlp_shard = lax.psum_scatter(mlp_acc, "dp", scatter_dimension=0, tiled=True)
+    mlp_shard = lax.psum_scatter(
+        mlp_acc.astype(jnp.bfloat16), "dp", scatter_dimension=0, tiled=True
+    ).astype(jnp.float32)
+    attn_shard = lax.psum_scatter(
+        attn_acc.astype(jnp.bfloat16), "dp", scatter_dimension=0, tiled=True
+    ).astype(jnp.float32)
     small = jnp.concatenate([tensor_sum(feature_acc), head_acc])
-    width_attn = attn_acc.shape[1]
-    small_rows = -(-small.shape[0] // width_attn)
-    small = jnp.pad(small, (0, small_rows * width_attn - small.shape[0])).reshape(
-        small_rows, width_attn
-    )
-    blocks = depth // rows
-    attn_rows = jnp.concatenate(
-        [
-            attn_acc.reshape(blocks, rows, width_attn),
-            jnp.broadcast_to(small, (blocks, small_rows, width_attn)),
-        ],
-        axis=1,
-    ).reshape(blocks * (rows + small_rows), width_attn)
-    attn_shard = lax.psum_scatter(attn_rows, "dp", scatter_dimension=0, tiled=True)
-    small_total = attn_shard[rows:].reshape(-1)
-    features = small_total[: feature_acc.shape[0]].reshape(6, -1)
-    head_total = small_total[feature_acc.shape[0] : feature_acc.shape[0] + head_acc.shape[0]]
+    groups = lax.psum(1, "dp")
+    step = 1
+    while step < groups:
+        small = small + lax.ppermute(small, "dp", [(i, i ^ step) for i in range(groups)])
+        step *= 2
+    features = small[: feature_acc.shape[0]].reshape(6, -1)
+    head_total = small[feature_acc.shape[0] :]
     qv_size = qv_bias.size
     return (
         jnp.stack(outputs),
         jnp.stack(in_grads),
-        attn_shard[:rows, :width_qkv].reshape(qkv_weight.shape),
+        attn_shard[:, :width_qkv].reshape(qkv_weight.shape),
         head_total[:qv_size].reshape(qv_bias.shape),
-        attn_shard[:rows, width_qkv:],
+        attn_shard[:, width_qkv:],
         features[0],
         mlp_shard[:, :width_fc],
         head_total[qv_size:],
@@ -350,6 +346,7 @@
         P(),
         P(),
     )
+
     return jax.shard_map(
         per_device, mesh=mesh, in_specs=in_specs, out_specs=out_specs, check_vma=False
     )

time: 771 us -> 631 us (0.82)
  waiting for transfers between devices: 426 us -> 327 us
  other arithmetic: 98.5 us -> 72.2 us
  matrix products: 143 us -> 132 us
    reduce_scatter x1 -> x0, waiting for transfers between devices: 144 us -> none  [per_device(): mlp_shard = lax.psum_scatter(mlp_acc, 'dp', scatter_dimension=0, tiled=True)]
    unnamed x5 -> x6, waiting for transfers between devices: 65.6 us -> 87.1 us
    ppermute x0 -> x3, waiting for transfers between devices: none -> 11.5 us  [per_device(): lax.ppermute(small, 'dp', [(i, i ^ step) for i in range(groups)])]
    ppermute x8, waiting for transfers between devices: 80.2 us -> 89.7 us  [tensor_scatter(): got2 = lax.ppermute(chip[rows:].astype(send_dtype), 'tx', SWAP)]
    unnamed x234 -> x241, local copies, waits for them, and re-layouts: 15.6 us -> 24.3 us
  transfers between devices with their start and end apart: 36 -> 39, of which waited for: 28 -> 32; matrix products, arithmetic and copies ran while one was open for 16% -> 14% of each run, Pallas kernels for 0% -> 0%
where the time goes in v6:
time: 631 us; the launch traced here: 625 us
  waiting for transfers between devices  327 us (52%)
  matrix products  132 us (21%)
  other arithmetic  72.2 us (11%)
  local copies, waits for them, and re-layouts  46.5 us (7%)
  starting transfers between devices  31.3 us (5%)
  between operations  16.1 us (3%)
    ppermute x8, waiting for transfers between devices, tensor_scatter(): got2 = lax.ppermute(chip[rows:].astype(send_dtype), 'tx', SWAP)  89.7 us
    unnamed x6, waiting for transfers between devices  87.1 us
    ppermute x7, waiting for transfers between devices, tensor_gather(): pair = jnp.concatenate([block, lax.ppermute(block, 'tx', SWAP)])  86.3 us
    all_gather x1, waiting for transfers between devices, per_device(): attn_full = lax.all_gather(attn_pack, 'dp', axis=0, tiled=True)  33.4 us
    unnamed x241, local copies, waits for them, and re-layouts  24.3 us
    convert_element_type x4, other arithmetic, attend_backward(): grad_scores = (probs * (grad_probs - inner)).astype(jnp.bfloat16)  23 us
    dot_general x4, matrix products, attend_backward(): jnp.einsum('qbhe,kbhe->bhqk', grad_block, values, preferred_element_type=...  17.5 us
    dot_general x2, matrix products, one_micro(): jnp.einsum('lbo,of->lbf', grad_top_full, proj_full, preferred_element_typ...  12.8 us
  transfers between devices with their start and end apart: 39, of which 32 were waited for; matrix products, arithmetic and copies ran while one was open for 14% of the time, Pallas kernels for 0%

profile of v6, /device:TPU:0, one launch (start us, length us, event | category | flops | bytes accessed | tf_op | source)
XLA Modules:
  0.0 625.5 jit_solution(17373177000960456397)
XLA Ops:
  19.2 10.0 %collective-permute-done = bf16[256,1,1024]{2,0,1:T(8,128)(2,1)S(1)} collective-permute-done((bf16[256,1,1024]{2,0,1:T(8,128)(2,1)S(1)}, bf16[256,1,1024]{2,0,1:T(8,128)(2,1)S(1)}, u32[]{:S(2)}, u32[]{:S(2)}) %collective-permute-start) | collective-permute-done | bytes 524320 | tf_op jit(solution)/shard_map/ppermute | solution.py:108
  30.3 33.4 %all-gather.3.cloned.1.call-done = bf16[1024,1024]{0,1:T(8,128)(2,1)} async-done(((bf16[128,1024]{0,1:T(8,128)(2,1)}), bf16[1024,1024]{0,1:T(8,128)(2,1)}) %all-gather.3.cloned.1.call-update) | async-done | bytes 2097168 | tf_op jit(solution)/shard_map/all_gather | solution.py:250
  90.3 21.5 %collective-permute-done.16 = bf16[256,2,1,1024]{3,0,2,1:T(8,128)(2,1)S(1)} collective-permute-done((bf16[256,2,1,1024]{3,0,2,1:T(8,128)(2,1)S(1)}, bf16[256,2,1,1024]{3,0,2,1:T(8,128)(2,1)S(1)}, u32[]{:S(2)}, u32[]{:S(2)}) %collective-permute-start.16) | collective-permute-done | bytes 1048608 | tf_op jit(solution)/shard_map/ppermute | solution.py:108
  112.1 10.3 %collective-permute-done.3 = bf16[256,1,1024]{2,0,1:T(8,128)(2,1)S(1)} collective-permute-done((bf16[256,1,1024]{2,0,1:T(8,128)(2,1)S(1)}, bf16[256,1,1024]{2,0,1:T(8,128)(2,1)S(1)}, u32[]{:S(2)}, u32[]{:S(2)}) %collective-permute-start.3) | collective-permute-done | bytes 524320 | tf_op jit(solution)/shard_map/ppermute | solution.py:116
  124.9 12.0 %collective-permute-done.4 = bf16[256,1,1024]{2,0,1:T(8,128)(2,1)S(1)} collective-permute-done((bf16[256,1,1024]{2,0,1:T(8,128)(2,1)S(1)}, bf16[256,1,1024]{2,0,1:T(8,128)(2,1)S(1)}, u32[]{:S(2)}, u32[]{:S(2)}) %collective-permute-start.4) | collective-permute-done | bytes 524320 | tf_op jit(solution)/shard_map/ppermute | solution.py:108
  139.8 4.7 fusion.76
  144.6 6.7 %convert_reduce_fusion.1 = (f32[1024]{0:T(1024)}, bf16[1024,1024]{1,0:T(8,128)(2,1)S(1)}) fusion(bf16[1024,2048]{1,0:T(8,128)(2,1)S(1)} %copy-done.82, bf16[2,1024,1,1024]{3,1,2,0:T(8,128)(2,1)S(1)} %copy-done.22, f32[1024,1024]{1,0:T(8,128)S(1)} %fusion.76, f32[1024]{0:T(1024)S(1)} %copy-done.90), kind=kOutput, calls=%fused_computation.62 | convolution fusion | flops 2175794176 | bytes 10493952 | tf_op jit(solution)/shard_map/lbo,of->lbf/dot_general | solution.py:173
  163.0 11.0 %collective-permute-done.19 = bf16[256,1,1024]{2,0,1:T(8,128)(2,1)S(1)} collective-permute-done((bf16[256,1,1024]{2,0,1:T(8,128)(2,1)S(1)}, bf16[256,1,1024]{2,0,1:T(8,128)(2,1)S(1)}, u32[]{:S(2)}, u32[]{:S(2)}) %collective-permute-start.19) | collective-permute-done | bytes 524320 | tf_op jit(solution)/shard_map/ppermute | solution.py:116
  174.0 10.4 %collective-permute-done.7 = bf16[256,1,1024]{2,0,1:T(8,128)(2,1)S(1)} collective-permute-done((bf16[256,1,1024]{2,0,1:T(8,128)(2,1)S(1)}, bf16[256,1,1024]{2,0,1:T(8,128)(2,1)S(1)}, u32[]{:S(2)}, u32[]{:S(2)}) %collective-permute-start.7) | collective-permute-done | bytes 524320 | tf_op jit(solution)/shard_map/ppermute | solution.py:116
  189.1 11.6 %collective-permute-done.20 = bf16[256,1,1024]{2,0,1:T(8,128)(2,1)S(1)} collective-permute-done((bf16[256,1,1024]{2,0,1:T(8,128)(2,1)S(1)}, bf16[256,1,1024]{2,0,1:T(8,128)(2,1)S(1)}, u32[]{:S(2)}, u32[]{:S(2)}) %collective-permute-start.20) | collective-permute-done | bytes 524320 | tf_op jit(solution)/shard_map/ppermute | solution.py:108
  205.8 4.4 multiply_reduce_fusion.3
  210.2 4.5 multiply_convert_fusion.3
  218.6 4.4 multiply_reduce_fusion.2
  227.5 7.0 %multiply_convert_fusion.2 = bf16[4,512,1024]{2,1,0:T(8,128)(2,1)S(1)} fusion(f32[4,512,1024]{2,1,0:T(8,128)} %get-tuple-element.121, f32[4,512,1024]{2,1,0:T(8,128)} %copy-done, f32[4,512]{1,0:T(4,128)S(1)} %get-tuple-element.120, f32[4,512]{1,0:T(4,128)S(1)} %log_add_fusion.2), kind=kLoop, calls=%fused_computation.8 | loop fusion | flops 8388608 | bytes 20987904 | tf_op jit(solution)/shard_map/convert_element_type | solution.py:80
  250.3 12.5 %collective-permute-done.23 = bf16[256,1,1024]{2,0,1:T(8,128)(2,1)S(1)} collective-permute-done((bf16[256,1,1024]{2,0,1:T(8,128)(2,1)S(1)}, bf16[256,1,1024]{2,0,1:T(8,128)(2,1)S(1)}, u32[]{:S(2)}, u32[]{:S(2)}) %collective-permute-start.23) | collective-permute-done | bytes 524320 | tf_op jit(solution)/shard_map/ppermute | solution.py:116
  267.0 11.6 %collective-permute-done.8 = bf16[256,1,1024]{2,0,1:T(8,128)(2,1)S(1)} collective-permute-done((bf16[256,1,1024]{2,0,1:T(8,128)(2,1)S(1)}, bf16[256,1,1024]{2,0,1:T(8,128)(2,1)S(1)}, u32[]{:S(2)}, u32[]{:S(2)}) %collective-permute-start.8) | collective-permute-done | bytes 524320 | tf_op jit(solution)/shard_map/ppermute | solution.py:108
  302.2 12.5 %collective-permute-done.11 = bf16[256,1,1024]{2,0,1:T(8,128)(2,1)S(1)} collective-permute-done((bf16[256,1,1024]{2,0,1:T(8,128)(2,1)S(1)}, bf16[256,1,1024]{2,0,1:T(8,128)(2,1)S(1)}, u32[]{:S(2)}, u32[]{:S(2)}) %collective-permute-start.11) | collective-permute-done | bytes 524320 | tf_op jit(solution)/shard_map/ppermute | solution.py:116
  317.1 11.6 %collective-permute-done.12 = bf16[256,1,1024]{2,0,1:T(8,128)(2,1)S(1)} collective-permute-done((bf16[256,1,1024]{2,0,1:T(8,128)(2,1)S(1)}, bf16[256,1,1024]{2,0,1:T(8,128)(2,1)S(1)}, u32[]{:S(2)}, u32[]{:S(2)}) %collective-permute-start.12) | collective-permute-done | bytes 524320 | tf_op jit(solution)/shard_map/ppermute | solution.py:108
  334.9 6.1 convert_reduce_fusion
  351.5 10.9 %collective-permute-done.25 = bf16[256,1,1024]{2,0,1:T(8,128)(2,1)S(1)} collective-permute-done((bf16[256,1,1024]{2,0,1:T(8,128)(2,1)S(1)}, bf16[256,1,1024]{2,0,1:T(8,128)(2,1)S(1)}, u32[]{:S(2)}, u32[]{:S(2)}) %collective-permute-start.25) | collective-permute-done | bytes 524320 | tf_op jit(solution)/shard_map/ppermute | solution.py:116
  363.0 9.8 %collective-permute-done.15 = bf16[256,1,1024]{2,0,1:T(8,128)(2,1)S(1)} collective-permute-done((bf16[256,1,1024]{2,0,1:T(8,128)(2,1)S(1)}, bf16[256,1,1024]{2,0,1:T(8,128)(2,1)S(1)}, u32[]{:S(2)}, u32[]{:S(2)}) %collective-permute-start.15) | collective-permute-done | bytes 524320 | tf_op jit(solution)/shard_map/ppermute | solution.py:116
  380.6 8.0 %collective-permute-done.26 = bf16[256,1,1024]{2,0,1:T(8,128)(2,1)} collective-permute-done((bf16[256,1,1024]{2,0,1:T(8,128)(2,1)}, bf16[256,1,1024]{2,0,1:T(8,128)(2,1)}, u32[]{:S(2)}, u32[]{:S(2)}) %collective-permute-start.26) | collective-permute-done | bytes 524320 | tf_op jit(solution)/shard_map/ppermute | solution.py:108
  393.5 4.8 fusion.52
  400.9 4.4 multiply_reduce_fusion.1
  405.3 4.7 multiply_convert_fusion.1
  414.9 4.4 multiply_reduce_fusion
  423.8 6.8 %multiply_convert_fusion = bf16[4,512,1024]{2,1,0:T(8,128)(2,1)S(1)} fusion(f32[4,512,1024]{2,1,0:T(8,128)} %get-tuple-element.129, f32[4,512,1024]{2,1,0:T(8,128)} %copy-done.1, f32[4,512]{1,0:T(4,128)S(1)} %get-tuple-element.128, f32[4,512]{1,0:T(4,128)S(1)} %log_add_fusion), kind=kLoop, calls=%fused_computation.2 | loop fusion | flops 8388608 | bytes 20987904 | tf_op jit(solution)/shard_map/convert_element_type | solution.py:80
  456.8 4.9 fusion.153
  473.6 6.5 %copy.79 = bf16[1024,2048]{1,0:T(8,128)(2,1)} copy(bf16[1024,2048]{0,1:T(8,128)(2,1)} %fusion) | data formatting | bytes 8388608
  490.0 12.4 %collective-permute-done.29 = bf16[256,1,1024]{2,0,1:T(8,128)(2,1)S(1)} collective-permute-done((bf16[256,1,1024]{2,0,1:T(8,128)(2,1)S(1)}, bf16[256,1,1024]{2,0,1:T(8,128)(2,1)S(1)}, u32[]{:S(2)}, u32[]{:S(2)}) %collective-permute-start.29) | collective-permute-done | bytes 524320 | tf_op jit(solution)/shard_map/ppermute | solution.py:116
  513.4 5.1 collective-permute-done.33
  528.3 87.0 %reduce-scatter.9.cloned.1.call-done = bf16[128,2048]{1,0:T(8,128)(2,1)} async-done(((bf16[1024,2048]{1,0:T(8,128)(2,1)}), bf16[128,2048]{1,0:T(8,128)(2,1)}) %reduce-scatter.9.cloned.1.call-update) | async-done | bytes 524304
  (471 shorter events, 233.8 us)
Async XLA Ops:
  7.2 56.4 %all-gather.3.cloned.1.call-start = ((), (), s32[]{:S(2)}) async-start(), calls=%async_computation.2 | async-start | bytes 2359296 | tf_op jit(solution)/shard_map/all_gather | solution.py:250
  10.0 129.8 %all-gather.5.cloned.1.call-start = ((), (), s32[]{:S(2)}) async-start(), calls=%async_computation.3 | async-start | bytes 4718592 | tf_op jit(solution)/shard_map/all_gather | solution.py:251
  14.2 15.0 %collective-permute-start = (bf16[256,1,1024]{2,0,1:T(8,128)(2,1)S(1)}, bf16[256,1,1024]{2,0,1:T(8,128)(2,1)S(1)}, u32[]{:S(2)}, u32[]{:S(2)}) collective-permute-start(bf16[256,1,1024]{2,0,1:T(8,128)(2,1)S(1)} %fusion.126), channel_id=1, source_target_pairs={{0,2},{2,0},{1,3},{3,1},{4,6},{6,4},{5,7},{7,5},{8,10},{10,8},{9,1... | collective-permute-start | bytes 1572872 | tf_op jit(solution)/shard_map/ppermute | solution.py:108
  19.1 505.4 %reduce-scatter.7.cloned.1.call-start = ((), (), s32[]{:S(2)}) async-start(), calls=%async_computation.4 | async-start | bytes 2359296
  29.3 35.9 %collective-permute-start.1 = (bf16[512,1,1024]{2,0,1:T(8,128)(2,1)S(1)}, bf16[512,1,1024]{2,0,1:T(8,128)(2,1)}, u32[]{:S(2)}, u32[]{:S(2)}) collective-permute-start(bf16[512,1,1024]{2,0,1:T(8,128)(2,1)S(1)} %pad_maximum_fusion.5), channel_id=1, source_target_pairs={{0,1},{1,0},{2,3},{3,2},{4,5},{5,4},{6,7},{7,6},{8,9},{9,8},{10,11... | collective-permute-start | bytes 3145736 | tf_op jit(solution)/shard_map/ppermute | solution.py:109
  85.6 2.7 collective-permute-start.2
  85.7 26.1 %collective-permute-start.16 = (bf16[256,2,1,1024]{3,0,2,1:T(8,128)(2,1)S(1)}, bf16[256,2,1,1024]{3,0,2,1:T(8,128)(2,1)S(1)}, u32[]{:S(2)}, u32[]{:S(2)}) collective-permute-start(bf16[256,2,1,1024]{3,0,2,1:T(8,128)(2,1)S(1)} %bitcast.402), channel_id=1, source_target_pairs={{0,2},{2,0},{1,3},{3,1},{4,6},{6,4},{5,7},{7,5},{8,10},{10,8},{9,1... | collective-permute-start | bytes 3145736 | tf_op jit(solution)/shard_map/ppermute | solution.py:108
  88.7 33.7 %collective-permute-start.3 = (bf16[256,1,1024]{2,0,1:T(8,128)(2,1)S(1)}, bf16[256,1,1024]{2,0,1:T(8,128)(2,1)S(1)}, u32[]{:S(2)}, u32[]{:S(2)}) collective-permute-start(bf16[256,1,1024]{2,0,1:T(8,128)(2,1)S(1)} %slice.680), channel_id=1, source_target_pairs={{0,2},{2,0},{1,3},{3,1},{4,6},{6,4},{5,7},{7,5},{8,10},{10,8},{9,1... | collective-permute-start | bytes 1572872 | tf_op jit(solution)/shard_map/ppermute | solution.py:116
  112.0 25.0 %collective-permute-start.17 = (bf16[512,2,1,1024]{3,0,2,1:T(8,128)(2,1)S(1)}, bf16[512,2,1,1024]{3,0,2,1:T(8,128)(2,1)S(1)}, u32[]{:S(2)}, u32[]{:S(2)}) collective-permute-start(bf16[512,2,1,1024]{3,0,2,1:T(8,128)(2,1)S(1)} %pad_maximum_fusion.2), channel_id=1, source_target_pairs={{0,1},{1,0},{2,3},{3,2},{4,5},{5,4},{6,7},{7,6},{8,9},{9,8},{10,11... | collective-permute-start | bytes 6291464 | tf_op jit(solution)/shard_map/ppermute | solution.py:109
  123.3 13.5 %collective-permute-start.4 = (bf16[256,1,1024]{2,0,1:T(8,128)(2,1)S(1)}, bf16[256,1,1024]{2,0,1:T(8,128)(2,1)S(1)}, u32[]{:S(2)}, u32[]{:S(2)}) collective-permute-start(bf16[256,1,1024]{2,0,1:T(8,128)(2,1)S(1)} %add_convert_fusion.3), channel_id=1, source_target_pairs={{0,2},{2,0},{1,3},{3,1},{4,6},{6,4},{5,7},{7,5},{8,10},{10,8},{9,1... | collective-permute-start | bytes 1572872 | tf_op jit(solution)/shard_map/ppermute | solution.py:108
  136.9 2.9 collective-permute-start.5
  155.1 3.6 collective-permute-start.18
  158.3 2.7 collective-permute-start.6
  159.1 14.9 %collective-permute-start.19 = (bf16[256,1,1024]{2,0,1:T(8,128)(2,1)S(1)}, bf16[256,1,1024]{2,0,1:T(8,128)(2,1)S(1)}, u32[]{:S(2)}, u32[]{:S(2)}) collective-permute-start(bf16[256,1,1024]{2,0,1:T(8,128)(2,1)S(1)} %slice.676), channel_id=1, source_target_pairs={{0,2},{2,0},{1,3},{3,1},{4,6},{6,4},{5,7},{7,5},{8,10},{10,8},{9,1... | collective-permute-start | bytes 1572872 | tf_op jit(solution)/shard_map/ppermute | solution.py:116
  161.4 23.0 %collective-permute-start.7 = (bf16[256,1,1024]{2,0,1:T(8,128)(2,1)S(1)}, bf16[256,1,1024]{2,0,1:T(8,128)(2,1)S(1)}, u32[]{:S(2)}, u32[]{:S(2)}) collective-permute-start(bf16[256,1,1024]{2,0,1:T(8,128)(2,1)S(1)} %slice.679), channel_id=1, source_target_pairs={{0,2},{2,0},{1,3},{3,1},{4,6},{6,4},{5,7},{7,5},{8,10},{10,8},{9,1... | collective-permute-start | bytes 1572872 | tf_op jit(solution)/shard_map/ppermute | solution.py:116
  187.5 13.2 %collective-permute-start.20 = (bf16[256,1,1024]{2,0,1:T(8,128)(2,1)S(1)}, bf16[256,1,1024]{2,0,1:T(8,128)(2,1)S(1)}, u32[]{:S(2)}, u32[]{:S(2)}) collective-permute-start(bf16[256,1,1024]{2,0,1:T(8,128)(2,1)S(1)} %convert_element_type.422), channel_id=1, source_target_pairs={{0,2},{2,0},{1,3},{3,1},{4,6},{6,4},{5,7},{7,5},{8,10},{10,8},{9,1... | collective-permute-start | bytes 1572872 | tf_op jit(solution)/shard_map/ppermute | solution.py:108
  245.5 2.7 collective-permute-start.22
  248.8 14.0 %collective-permute-start.23 = (bf16[256,1,1024]{2,0,1:T(8,128)(2,1)S(1)}, bf16[256,1,1024]{2,0,1:T(8,128)(2,1)S(1)}, u32[]{:S(2)}, u32[]{:S(2)}) collective-permute-start(bf16[256,1,1024]{2,0,1:T(8,128)(2,1)S(1)} %slice.675), channel_id=1, source_target_pairs={{0,2},{2,0},{1,3},{3,1},{4,6},{6,4},{5,7},{7,5},{8,10},{10,8},{9,1... | collective-permute-start | bytes 1572872 | tf_op jit(solution)/shard_map/ppermute | solution.py:116
  265.5 13.1 %collective-permute-start.8 = (bf16[256,1,1024]{2,0,1:T(8,128)(2,1)S(1)}, bf16[256,1,1024]{2,0,1:T(8,128)(2,1)S(1)}, u32[]{:S(2)}, u32[]{:S(2)}) collective-permute-start(bf16[256,1,1024]{2,0,1:T(8,128)(2,1)S(1)} %get-tuple-element.86), channel_id=1, source_target_pairs={{0,2},{2,0},{1,3},{3,1},{4,6},{6,4},{5,7},{7,5},{8,10},{10,8},{9,1... | collective-permute-start | bytes 1572872 | tf_op jit(solution)/shard_map/ppermute | solution.py:108
  300.6 14.0 %collective-permute-start.11 = (bf16[256,1,1024]{2,0,1:T(8,128)(2,1)S(1)}, bf16[256,1,1024]{2,0,1:T(8,128)(2,1)S(1)}, u32[]{:S(2)}, u32[]{:S(2)}) collective-permute-start(bf16[256,1,1024]{2,0,1:T(8,128)(2,1)S(1)} %slice.678), channel_id=1, source_target_pairs={{0,2},{2,0},{1,3},{3,1},{4,6},{6,4},{5,7},{7,5},{8,10},{10,8},{9,1... | collective-permute-start | bytes 1572872 | tf_op jit(solution)/shard_map/ppermute | solution.py:116
  315.5 13.2 %collective-permute-start.12 = (bf16[256,1,1024]{2,0,1:T(8,128)(2,1)S(1)}, bf16[256,1,1024]{2,0,1:T(8,128)(2,1)S(1)}, u32[]{:S(2)}, u32[]{:S(2)}) collective-permute-start(bf16[256,1,1024]{2,0,1:T(8,128)(2,1)S(1)} %add_convert_fusion.2), channel_id=1, source_target_pairs={{0,2},{2,0},{1,3},{3,1},{4,6},{6,4},{5,7},{7,5},{8,10},{10,8},{9,1... | collective-permute-start | bytes 1572872 | tf_op jit(solution)/shard_map/ppermute | solution.py:108
  343.6 3.6 collective-permute-start.24
  347.6 14.9 %collective-permute-start.25 = (bf16[256,1,1024]{2,0,1:T(8,128)(2,1)S(1)}, bf16[256,1,1024]{2,0,1:T(8,128)(2,1)S(1)}, u32[]{:S(2)}, u32[]{:S(2)}) collective-permute-start(bf16[256,1,1024]{2,0,1:T(8,128)(2,1)S(1)} %slice.674), channel_id=1, source_target_pairs={{0,2},{2,0},{1,3},{3,1},{4,6},{6,4},{5,7},{7,5},{8,10},{10,8},{9,1... | collective-permute-start | bytes 1572872 | tf_op jit(solution)/shard_map/ppermute | solution.py:116
  349.9 22.9 %collective-permute-start.15 = (bf16[256,1,1024]{2,0,1:T(8,128)(2,1)S(1)}, bf16[256,1,1024]{2,0,1:T(8,128)(2,1)S(1)}, u32[]{:S(2)}, u32[]{:S(2)}) collective-permute-start(bf16[256,1,1024]{2,0,1:T(8,128)(2,1)S(1)} %slice.677), channel_id=1, source_target_pairs={{0,2},{2,0},{1,3},{3,1},{4,6},{6,4},{5,7},{7,5},{8,10},{10,8},{9,1... | collective-permute-start | bytes 1572872 | tf_op jit(solution)/shard_map/ppermute | solution.py:116
  375.1 13.4 %collective-permute-start.26 = (bf16[256,1,1024]{2,0,1:T(8,128)(2,1)}, bf16[256,1,1024]{2,0,1:T(8,128)(2,1)}, u32[]{:S(2)}, u32[]{:S(2)}) collective-permute-start(bf16[256,1,1024]{2,0,1:T(8,128)(2,1)} %convert_element_type.438), channel_id=1, source_target_pairs={{0,2},{2,0},{1,3},{3,1},{4,6},{6,4},{5,7},{7,5},{8,10},{10,8},{9,1... | collective-permute-start | bytes 1572872 | tf_op jit(solution)/shard_map/ppermute | solution.py:108
  389.9 8.4 %collective-permute-start.27 = (bf16[512,1,1024]{2,0,1:T(8,128)(2,1)S(1)}, bf16[512,1,1024]{2,0,1:T(8,128)(2,1)S(1)}, u32[]{:S(2)}, u32[]{:S(2)}) collective-permute-start(bf16[512,1,1024]{2,0,1:T(8,128)(2,1)S(1)} %pad_maximum_fusion.11), channel_id=1, source_target_pairs={{0,1},{1,0},{2,3},{3,2},{4,5},{5,4},{6,7},{7,6},{8,9},{9,8},{10,11... | collective-permute-start | bytes 3145736 | tf_op jit(solution)/shard_map/ppermute | solution.py:109
  456.5 158.8 %reduce-scatter.9.cloned.1.call-start = ((), (), s32[]{:S(2)}) async-start(), calls=%async_computation.5 | async-start | bytes 4718592
  488.2 14.3 %collective-permute-start.29 = (bf16[256,1,1024]{2,0,1:T(8,128)(2,1)S(1)}, bf16[256,1,1024]{2,0,1:T(8,128)(2,1)S(1)}, u32[]{:S(2)}, u32[]{:S(2)}) collective-permute-start(bf16[256,1,1024]{2,0,1:T(8,128)(2,1)S(1)} %slice.673), channel_id=1, source_target_pairs={{0,2},{2,0},{1,3},{3,1},{4,6},{6,4},{5,7},{7,5},{8,10},{10,8},{9,1... | collective-permute-start | bytes 1572872 | tf_op jit(solution)/shard_map/ppermute | solution.py:116
  504.4 3.8 collective-permute-start.31
  508.2 4.6 collective-permute-start.32
  512.9 5.6 collective-permute-start.33
  518.5 4.9 collective-permute-start.34
  (114 other events, 1150.6 us)
Sparse Core Ops, SparseCore 0:
  10.6 52.9 all-gather.2
  66.3 71.0 all-gather.4
  456.6 67.5 reduce-scatter.6
  527.7 87.5 reduce-scatter.8
